TPU v7x, 256 devices: a 4x2x16 block of a 4x16x16 slice. The times are simulated.
256 devices in a mesh: groups: 2 (over y), seq: 16 (over z), section: 4 (over x), mp: 2 (over core).
Axes of the slice: x: 4, y: 2, z: 16, core: 2. Of those that a mesh axis runs over, the one named last changes fastest.
The devices are a block of a 4x16x16 slice.
Arguments:
- light_queries: bfloat16 [8192, 8192], P(('groups', 'seq'), ('section', 'mp')), parts along dimension 0, may hold values from -6 to 6
- light_keys: bfloat16 [8192, 8192], P(('groups', 'seq'), ('section', 'mp')), parts along dimension 0, may hold values from -6 to 6
- light_values: bfloat16 [8192, 8192], P(('groups', 'seq'), ('section', 'mp')), parts along dimension 0, may hold values from -6 to 6
- decay_log: float32 [8192, 64], P(('groups', 'seq'), ('section', 'mp')), parts along dimension 0, may hold values from -1 to 0
- norm_gain: float32 [8192], P(('section', 'mp')), may hold values from 0.25 to 1.75
- soft_queries: bfloat16 [8192, 8192], P(('groups', 'seq'), ('section', 'mp')), parts along dimension 0, may hold values from -150 to 150
- soft_keys: bfloat16 [8192, 1024], P(('groups', 'seq'), ('section', 'mp')), parts along dimension 0, may hold values from -6 to 6
- soft_values: bfloat16 [8192, 1024], P(('groups', 'seq'), ('section', 'mp')), parts along dimension 0, may hold values from -6 to 6
- lengths: int32 [32], P('groups'), parts along dimension 0, may hold values from 1 to 256, 3072 in all
Outputs:
- light_out: bfloat16 [8192, 8192], P(('groups', 'seq'), ('section', 'mp')), parts along dimension 0
- soft_out: bfloat16 [8192, 8192], P(('groups', 'seq'), ('section', 'mp')), parts along dimension 0
There are 2 independent parts, one for each index of `groups`. A program takes and returns all parts, laid end to end along the dimension named above; an argument that names none is the same for every part. Nothing has to cross between parts.
Inputs may be any that keep to these rules, and one draw needn't show every extreme that they name: The live tokens of a block stand at its first slots; the lengths sum to 3072.
All inputs are finite; a program needn't handle non-finite values.
Results may differ from a plain program's by a relative error of at most 0.007.
Values may be sent and summed in bfloat16 or wider, within the bound.
No kernel may reach another device: no remote copies, remote signals or barrier semaphores. Data moves between devices by JAX's collectives and lax.ppermute only.
A program may use at most 64 MiB of HBM per device.

v0:
```python
from functools import partial

import jax
import jax.numpy as jnp
from jax import lax
from jax.experimental import pallas as pl
from jax.experimental.pallas import tpu as pltpu
from jax.sharding import PartitionSpec as P


F32 = jnp.float32
BF16 = jnp.bfloat16
NEG = -1e30
LOG2E = 1.4426950408889634
E_ROWS = 32
VMEM = pl.BlockSpec(memory_space=pltpu.VMEM)
SMEM = pl.BlockSpec(memory_space=pltpu.SMEM)


def call(kernel, out_shape, ins, aliases=None, flops=2_000_000, scratch=()):
    specs = [SMEM if s else VMEM for s, unused in ins]
    arrays = [a for unused, a in ins]
    outs = [jax.ShapeDtypeStruct(s, d) for s, d in out_shape]
    return pl.pallas_call(
        kernel,
        out_shape=outs,
        in_specs=specs,
        out_specs=[VMEM] * len(outs),
        scratch_shapes=list(scratch),
        input_output_aliases=aliases or {},
        compiler_params=pltpu.CompilerParams(vmem_limit_bytes=48 * 1024 * 1024),
        cost_estimate=pl.CostEstimate(flops=flops, bytes_accessed=1 << 20, transcendentals=0),
    )(*arrays)


def bit(i, level):
    return lax.shift_right_logical(i, level) & 1


def keep_bit(i, level):
    return bit(i, level) ^ (bit(i, 3) if level == 2 else 0)


def first_head(i, level):
    start = keep_bit(i, 0) * 4
    if level >= 1:
        start += keep_bit(i, 1) * 2
    if level >= 2:
        start += keep_bit(i, 2)
    return start


def put_logs(msg_ref, at, logs):
    hi = logs.astype(BF16)
    rest = logs - hi.astype(F32)
    mid = rest.astype(BF16)
    low = (rest - mid.astype(F32)).astype(BF16)
    both = jnp.concatenate([hi.astype(F32), mid.astype(F32), low.astype(F32), jnp.zeros_like(logs)], axis=0)
    msg_ref[pl.ds(at, E_ROWS), :] = both.astype(BF16)


def get_logs(msg_ref, at):
    rows = msg_ref[pl.ds(at, E_ROWS), :].astype(F32)
    return rows[0:8] + rows[8:16] + rows[16:24]


def prep_kernel(len_ref, k_ref, v_ref, dec_ref, msg_ref, kept_ref, logs_ref, c_ref, ct_ref, states):
    i = lax.axis_index("seq")
    rows = k_ref.shape[0]
    heads = dec_ref.shape[0]
    width = k_ref.shape[1] // heads
    half = heads // 2
    length = len_ref[i]
    lane = lax.broadcasted_iota(jnp.int32, (heads, rows), 1)
    live = lane < length
    masked = jnp.where(live, dec_ref[...], 0.0)
    tri = (
        lax.broadcasted_iota(jnp.int32, (rows, rows), 0)
        <= lax.broadcasted_iota(jnp.int32, (rows, rows), 1)
    ).astype(F32)
    running = jnp.dot(masked, tri, preferred_element_type=F32, precision=lax.Precision.HIGHEST)
    ending = running[:, rows - 1 : rows]
    c_ref[...] = running
    ct_ref[...] = running.T
    logs = jnp.broadcast_to(ending, (heads, 128))
    logs_ref[...] = logs
    fading = jnp.where(live, jnp.exp(ending - running), 0.0)
    for h in range(heads):
        kt = k_ref[:, h * width : (h + 1) * width].T.astype(F32)
        scaled = (kt * fading[h : h + 1, :]).astype(BF16)
        states[h] = jnp.dot(scaled, v_ref[:, h * width : (h + 1) * width], preferred_element_type=F32)
    keep = keep_bit(i, 0) * half
    send = half - keep
    for h in range(half):
        kept_ref[h] = states[keep + h]
        msg_ref[h * width : (h + 1) * width, :] = states[send + h].astype(BF16)
    put_logs(msg_ref, half * width, logs)


def up_kernel(level, recv_ref, kept_ref, logs_ref, msg_ref, next_ref, low_ref, lowlog_ref, sum_ref):
    i = lax.axis_index("seq")
    count, width = kept_ref.shape[0], kept_ref.shape[1]
    upper = bit(i, level) == 1
    own = logs_ref[...]
    other = get_logs(recv_ref, count * width)
    low_logs = jnp.where(upper, other, own)
    lowlog_ref[...] = low_logs
    sum_ref[...] = own + other
    grown = jnp.exp(jnp.where(upper, own, other))
    start = first_head(i, level)
    which = lax.broadcasted_iota(jnp.int32, grown.shape, 0)
    half = count // 2
    keep = keep_bit(i, level + 1) * half
    totals = []
    for h in range(count):
        factor = jnp.sum(jnp.where(which == start + h, grown, 0.0), axis=0, keepdims=True)
        mine = kept_ref[h]
        got = recv_ref[h * width : (h + 1) * width, :].astype(F32)
        low = jnp.where(upper, got, mine)
        high = jnp.where(upper, mine, got)
        low_ref[h] = low
        totals.append(factor * low + high)
    if count == 1:
        msg_ref[...] = totals[0].astype(BF16)
        next_ref[...] = jnp.zeros_like(next_ref)
        return
    first = keep == 0
    for h in range(half):
        next_ref[h] = jnp.where(first, totals[h], totals[half + h])
        msg_ref[h * width : (h + 1) * width, :] = jnp.where(first, totals[half + h], totals[h]).astype(BF16)
    put_logs(msg_ref, half * width, own + other)


def down_kernel(level, top, *refs):
    if top:
        recv_ref, low_ref, lowlog_ref, mine_ref, msg_ref = refs
    else:
        held_ref, recv_ref, low_ref, lowlog_ref, mine_ref, msg_ref = refs
    i = lax.axis_index("seq")
    count, width = low_ref.shape[0], low_ref.shape[1]
    half = count // 2
    upper = bit(i, level) == 1
    grown = jnp.exp(lowlog_ref[...])
    start = first_head(i, level)
    which = lax.broadcasted_iota(jnp.int32, grown.shape, 0)
    if top:
        entering = [recv_ref[...].astype(F32)]
    else:
        first = keep_bit(i, level + 1) == 0
        held = [held_ref[h] for h in range(half)]
        got = [recv_ref[h * width : (h + 1) * width, :].astype(F32) for h in range(half)]
        entering = [jnp.where(first, a, b) for a, b in zip(held, got)]
        entering += [jnp.where(first, b, a) for a, b in zip(held, got)]
    for h in range(count):
        factor = jnp.sum(jnp.where(which == start + h, grown, 0.0), axis=0, keepdims=True)
        low = entering[h]
        high = factor * low + low_ref[h]
        mine_ref[h] = jnp.where(upper, high, low)
        msg_ref[h * width : (h + 1) * width, :] = jnp.where(upper, low, high).astype(BF16)


def inside_kernel(len_ref, q_ref, k_ref, v_ref, c_ref, ct_ref, out_ref):
    i = lax.axis_index("seq")
    rows = q_ref.shape[0]
    heads = c_ref.shape[0]
    width = q_ref.shape[1] // heads
    scale = width ** (-0.5)
    length = len_ref[i]
    row = lax.broadcasted_iota(jnp.int32, (rows, rows), 0)
    col = lax.broadcasted_iota(jnp.int32, (rows, rows), 1)
    allowed = (col <= row) & (col < length)
    running = c_ref[...]
    running_t = ct_ref[...]
    for h in range(heads):
        at = slice(h * width, (h + 1) * width)
        scores = lax.dot_general(
            q_ref[:, at], k_ref[:, at], (((1,), (1,)), ((), ())), preferred_element_type=F32
        )
        gaps = running_t[:, h : h + 1] - running[h : h + 1, :]
        weights = jnp.exp(jnp.where(allowed, gaps, NEG))
        intra = (scores * scale * weights).astype(BF16)
        out_ref[:, at] = jnp.dot(intra, v_ref[:, at], preferred_element_type=F32)


def light_kernel(len_ref, q_ref, inside_ref, held_ref, recv_ref, ct_ref, gain_ref, out_ref):
    i = lax.axis_index("seq")
    rows = q_ref.shape[0]
    half, width = held_ref.shape[0], held_ref.shape[1]
    scale = width ** (-0.5)
    first = keep_bit(i, 0) == 0
    live = lax.broadcasted_iota(jnp.int32, (rows, 1), 0) < len_ref[i]
    grown = jnp.exp(ct_ref[...])
    for h in range(2 * half):
        at = slice(h * width, (h + 1) * width)
        mod = h % half
        held = held_ref[mod].astype(BF16)
        got = recv_ref[mod * width : (mod + 1) * width, :]
        pick_held = first if h < half else jnp.logical_not(first)
        entering = jnp.where(pick_held, held.astype(F32), got.astype(F32)).astype(BF16)
        across = jnp.dot(q_ref[:, at], entering, preferred_element_type=F32) * scale
        combined = inside_ref[:, at] + across * grown[:, h : h + 1]
        mean = jnp.mean(combined * combined, axis=-1, keepdims=True)
        normed = combined * lax.rsqrt(mean + 1e-06) * gain_ref[:, at]
        out_ref[:, at] = jnp.where(live, normed, 0.0).astype(BF16)


def unit_columns(rows):
    return jnp.where(lax.broadcasted_iota(jnp.int32, (rows, 128), 1) == 0, 1.0, 0.0).astype(BF16)


def own_kernel(len_ref, q_ref, k_ref, v_ref, q2_ref, m_ref, l_ref, acc_ref):
    i = lax.axis_index("seq")
    rows, width = k_ref.shape
    heads = q_ref.shape[1] // width
    factor = width ** (-0.5) * LOG2E
    q2_ref[:, width:] = unit_columns(heads * rows)
    for h in range(heads):
        q2_ref[h * rows : (h + 1) * rows, :width] = q_ref[:, h * width : (h + 1) * width]
    row = lax.broadcasted_iota(jnp.int32, (rows, rows), 0)
    col = lax.broadcasted_iota(jnp.int32, (rows, rows), 1)
    allowed = (col <= row) & (col < len_ref[i])
    scores = jnp.dot(q2_ref[:, :width], k_ref[...].T, preferred_element_type=F32)
    scores = jnp.where(allowed[None], scores.reshape(heads, rows, rows), NEG).reshape(heads * rows, rows)
    peak = jnp.broadcast_to(jnp.max(scores, axis=-1, keepdims=True), (heads * rows, 128))
    probs = [jnp.exp2((scores[:, t : t + 128] - peak) * factor) for t in range(0, rows, 128)]
    m_ref[...] = peak
    l_ref[...] = sum(probs[1:], probs[0])
    acc_ref[...] = jnp.dot(
        jnp.concatenate([p.astype(BF16) for p in probs], axis=1), v_ref[...], preferred_element_type=F32
    )


def attend(q2_ref, blocks, lengths, old_ref):
    rows, width = blocks[0].shape[0] // 2, blocks[0].shape[1]
    factor = width ** (-0.5) * LOG2E
    row = lax.broadcasted_iota(jnp.int32, (128, rows), 0)
    col = lax.broadcasted_iota(jnp.int32, (128, rows), 1)
    biases = [jnp.where((row == 0) & (col >= n), NEG, 0.0).astype(BF16) for n in lengths]
    keys_t = jnp.concatenate([ref[0:rows, :].T for ref in blocks], axis=1)
    keys_t = jnp.concatenate([keys_t, jnp.concatenate(biases, axis=1)], axis=0)
    values = jnp.concatenate([ref[rows : 2 * rows, :] for ref in blocks], axis=0)
    scores = jnp.dot(q2_ref[...], keys_t, preferred_element_type=F32)
    old = old_ref[...]
    new = jnp.maximum(old, jnp.max(scores, axis=-1, keepdims=True))
    probs = [jnp.exp2((scores[:, t : t + 128] - new) * factor) for t in range(0, scores.shape[1], 128)]
    summed = jnp.dot(
        jnp.concatenate([p.astype(BF16) for p in probs], axis=1), values, preferred_element_type=F32
    )
    return new, jnp.exp2((old - new) * factor), sum(probs[1:], probs[0]), summed


def step_kernel(step, count, len_ref, q2_ref, f_ref, b_ref, unused_m, unused_l, unused_acc, m_ref, l_ref, acc_ref):
    i = lax.axis_index("seq")

    @pl.when(i >= step)
    def run():
        wrapped = i + step - count
        lengths = [
            len_ref[jnp.maximum(i - step, 0)],
            jnp.where(wrapped >= 0, len_ref[jnp.maximum(wrapped, 0)], 0),
        ]
        new, shrink, total, summed = attend(q2_ref, [f_ref, b_ref], lengths, m_ref)
        m_ref[...] = new
        l_ref[...] = shrink * l_ref[...] + total
        acc_ref[...] = shrink * acc_ref[...] + summed


def last_kernel(step, len_ref, q2_ref, f_ref, m_ref, l_ref, acc_ref, out_ref):
    i = lax.axis_index("seq")
    rows, width = f_ref.shape[0] // 2, f_ref.shape[1]
    heads = q2_ref.shape[0] // rows
    live = lax.broadcasted_iota(jnp.int32, (rows, 1), 0) < len_ref[i]

    def finish(total, summed):
        result = summed / jnp.sum(total, axis=-1, keepdims=True)
        for h in range(heads):
            picked = jnp.where(live, result[h * rows : (h + 1) * rows, :], 0.0)
            out_ref[:, h * width : (h + 1) * width] = picked.astype(BF16)

    @pl.when(i >= step)
    def run():
        _, shrink, total, summed = attend(q2_ref, [f_ref], [len_ref[jnp.maximum(i - step, 0)]], m_ref)
        finish(shrink * l_ref[...] + total, shrink * acc_ref[...] + summed)

    @pl.when(i < step)
    def skip():
        finish(l_ref[...], acc_ref[...])


def body(
    light_queries,
    light_keys,
    light_values,
    decay_log,
    norm_gain,
    soft_queries,
    soft_keys,
    soft_values,
    lengths,
):
    rows = light_queries.shape[0]
    heads = decay_log.shape[1]
    width = light_queries.shape[1] // heads
    count = lax.axis_size("seq")
    half = heads // 2
    forward = [(i, (i + 1) % count) for i in range(count)]
    backward = [(i, (i - 1) % count) for i in range(count)]

    def send(x, pairs):
        return lax.ppermute(x, "seq", pairs)

    def exchange(x, distance):
        return send(x, [(i, i ^ distance) for i in range(count)])

    lens = (True, lengths)
    own_kv = jnp.concatenate([soft_keys, soft_values], axis=0)
    f = send(own_kv, forward)
    b = send(own_kv, backward)

    msg, kept, logs, running, running_t = call(
        prep_kernel,
        [
            ((half * width + E_ROWS, width), BF16),
            ((half, width, width), F32),
            ((heads, 128), F32),
            ((heads, rows), F32),
            ((rows, heads), F32),
        ],
        [lens, (False, light_keys), (False, light_values), (False, decay_log.T)],
        scratch=[pltpu.VMEM((heads, width, width), F32)],
    )
    saved = []
    n = half
    for level in range(3):
        recv = exchange(msg, 1 << level)
        m = max(n // 2, 1)
        tail = E_ROWS if n > 1 else 0
        msg, nxt, low, low_logs, new_logs = call(
            partial(up_kernel, level),
            [
                ((m * width + tail, width), BF16),
                ((m, width, width), F32),
                ((n, width, width), F32),
                ((heads, 128), F32),
                ((heads, 128), F32),
            ],
            [(False, recv), (False, kept), (False, logs)],
        )
        saved.append((low, low_logs))
        kept, logs, n = (nxt, new_logs, n // 2)
    recv = send(msg, [(i, (i + 4 if i >= 4 else i - 4) % count) for i in range(count // 2)])
    held = None
    for level in (2, 1, 0):
        low, low_logs = saved[level]
        n = low.shape[0]
        ins = [(False, recv), (False, low), (False, low_logs)]
        if held is not None:
            ins = [(False, held)] + ins
        held, msg = call(
            partial(down_kernel, level, held is None),
            [((n, width, width), F32), ((n * width, width), BF16)],
            ins,
        )
        recv = exchange(msg, 1 << level)
    (inside,) = call(
        inside_kernel,
        [((rows, heads * width), F32)],
        [
            lens,
            (False, light_queries),
            (False, light_keys),
            (False, light_values),
            (False, running),
            (False, running_t),
        ],
    )
    (light_out,) = call(
        light_kernel,
        [((rows, heads * width), BF16)],
        [
            lens,
            (False, light_queries),
            (False, inside),
            (False, held),
            (False, recv),
            (False, running_t),
            (False, norm_gain.reshape(1, heads * width)),
        ],
    )

    soft_rows = soft_queries.shape[1] // width * rows
    stat = ((soft_rows, 128), F32)
    q2, *state = call(
        own_kernel,
        [((soft_rows, width + 128), BF16), stat, stat, stat],
        [lens, (False, soft_queries), (False, soft_keys), (False, soft_values)],
    )
    for step in range(1, count // 2):
        nf = send(f, forward)
        nb = send(b, backward) if step + 1 < count // 2 else None
        state = call(
            partial(step_kernel, step, count),
            [stat, stat, stat],
            [lens, (False, q2), (False, f), (False, b)] + [(False, s) for s in state],
            aliases={4: 0, 5: 1, 6: 2},
        )
        f, b = nf, nb
    (soft_out,) = call(
        partial(last_kernel, count // 2),
        [((rows, soft_queries.shape[1]), BF16)],
        [lens, (False, q2), (False, f)] + [(False, s) for s in state],
    )
    return (light_out, soft_out)


def solution(mesh):
    return jax.shard_map(
        body,
        mesh=mesh,
        in_specs=(
            P(("groups", "seq"), ("section", "mp")),
            P(("groups", "seq"), ("section", "mp")),
            P(("groups", "seq"), ("section", "mp")),
            P(("groups", "seq"), ("section", "mp")),
            P(("section", "mp")),
            P(("groups", "seq"), ("section", "mp")),
            P(("groups", "seq"), ("section", "mp")),
            P(("groups", "seq"), ("section", "mp")),
            P("groups"),
        ),
        out_specs=(
            P(("groups", "seq"), ("section", "mp")),
            P(("groups", "seq"), ("section", "mp")),
        ),
        check_vma=False,
    )
```

profile of v0, /device:TPU:36, one launch (start us, length us, event | category | flops | bytes accessed | tf_op | source)
XLA Modules:
  0.0 110.1 jit_solution(9681657926538297256)
XLA Ops:
  0.6 0.9 constant_dynamic-update-slice_fusion.1
  1.6 2.9 %collective-permute-start.7 = (bf16[512,128]{1,0:T(8,128)(2,1)S(1)}, bf16[512,128]{1,0:T(8,128)(2,1)S(1)}, u32[]{:S(2)}, u32[]{:S(2)}) collective-permute-start(bf16[512,128]{1,0:T(8,128)(2,1)S(1)} %constant_dynamic-update-slice_fusion), channel_id=1, source_target_pairs={{0,8},{8,16},{16,24},{24,32},{32,40},{40,48},{48,56},{56,64},{64,7... | collective-permute-start | bytes 393224 | tf_op jit(solution)/shard_map/ppermute | solution.py:310
  4.4 19.7 %collective-permute-start.15 = (bf16[512,128]{1,0:T(8,128)(2,1)S(1)}, bf16[512,128]{1,0:T(8,128)(2,1)S(1)}, u32[]{:S(2)}, u32[]{:S(2)}) collective-permute-start(bf16[512,128]{1,0:T(8,128)(2,1)S(1)} %constant_dynamic-update-slice_fusion), channel_id=1, source_target_pairs={{0,120},{8,0},{16,8},{24,16},{32,24},{40,32},{48,40},{56,48},{64,5... | collective-permute-start | bytes 393224 | tf_op jit(solution)/shard_map/ppermute | solution.py:310
  24.2 3.4 %collective-permute-done.7.f_ref = bf16[512,128]{1,0:T(8,128)(2,1)S(1)} collective-permute-done((bf16[512,128]{1,0:T(8,128)(2,1)S(1)}, bf16[512,128]{1,0:T(8,128)(2,1)S(1)}, u32[]{:S(2)}, u32[]{:S(2)}) %collective-permute-start.7) | collective-permute-done | bytes 131104 | tf_op jit(solution)/shard_map/ppermute | solution.py:310
  27.6 3.2 %collective-permute-start.16 = (bf16[512,128]{1,0:T(8,128)(2,1)S(1)}, bf16[512,128]{1,0:T(8,128)(2,1)S(1)}, u32[]{:S(2)}, u32[]{:S(2)}) collective-permute-start(bf16[512,128]{1,0:T(8,128)(2,1)S(1)} %collective-permute-done.15.b_ref), channel_id=1, source_target_pairs={{0,120},{8,0},{16,8},{24,16},{32,24},{40,32},{48,40},{56,48},{64,5... | collective-permute-start | bytes 393224 | tf_op jit(solution)/shard_map/ppermute | solution.py:310
  30.9 2.9 %collective-permute-done.8.f_ref = bf16[512,128]{1,0:T(8,128)(2,1)S(1)} collective-permute-done((bf16[512,128]{1,0:T(8,128)(2,1)S(1)}, bf16[512,128]{1,0:T(8,128)(2,1)S(1)}, u32[]{:S(2)}, u32[]{:S(2)}) %collective-permute-start.8) | collective-permute-done | bytes 131104 | tf_op jit(solution)/shard_map/ppermute | solution.py:310
  33.8 3.2 %collective-permute-start.17 = (bf16[512,128]{1,0:T(8,128)(2,1)S(1)}, bf16[512,128]{1,0:T(8,128)(2,1)S(1)}, u32[]{:S(2)}, u32[]{:S(2)}) collective-permute-start(bf16[512,128]{1,0:T(8,128)(2,1)S(1)} %collective-permute-done.16.b_ref), channel_id=1, source_target_pairs={{0,120},{8,0},{16,8},{24,16},{32,24},{40,32},{48,40},{56,48},{64,5... | collective-permute-start | bytes 393224 | tf_op jit(solution)/shard_map/ppermute | solution.py:310
  37.0 2.9 %collective-permute-done.9.f_ref = bf16[512,128]{1,0:T(8,128)(2,1)S(1)} collective-permute-done((bf16[512,128]{1,0:T(8,128)(2,1)S(1)}, bf16[512,128]{1,0:T(8,128)(2,1)S(1)}, u32[]{:S(2)}, u32[]{:S(2)}) %collective-permute-start.9) | collective-permute-done | bytes 131104 | tf_op jit(solution)/shard_map/ppermute | solution.py:310
  40.0 3.2 %collective-permute-start.18 = (bf16[512,128]{1,0:T(8,128)(2,1)S(1)}, bf16[512,128]{1,0:T(8,128)(2,1)S(1)}, u32[]{:S(2)}, u32[]{:S(2)}) collective-permute-start(bf16[512,128]{1,0:T(8,128)(2,1)S(1)} %collective-permute-done.17.b_ref), channel_id=1, source_target_pairs={{0,120},{8,0},{16,8},{24,16},{32,24},{40,32},{48,40},{56,48},{64,5... | collective-permute-start | bytes 393224 | tf_op jit(solution)/shard_map/ppermute | solution.py:310
  43.2 3.3 %collective-permute-done.10.f_ref = bf16[512,128]{1,0:T(8,128)(2,1)S(1)} collective-permute-done((bf16[512,128]{1,0:T(8,128)(2,1)S(1)}, bf16[512,128]{1,0:T(8,128)(2,1)S(1)}, u32[]{:S(2)}, u32[]{:S(2)}) %collective-permute-start.10) | collective-permute-done | bytes 131104 | tf_op jit(solution)/shard_map/ppermute | solution.py:310
  46.5 1.0 copy-done
  47.5 1.0 copy-done.2
  48.6 1.4 %shard_map.104 = (bf16[544,128]{1,0:T(8,128)(2,1)S(1)}, f32[4,128,128]{2,1,0:T(8,128)S(1)}, f32[8,128]{1,0:T(8,128)S(1)}, f32[8,256]{1,0:T(8,128)S(1)}, f32[256,8]{1,0:T(8,128)S(1)}) custom-call(s32[16]{0:T(128)S(1)} %copy-done.8, bf16[256,1024]{1,0:T(8,128)(2,1)S(1)} %copy-done, bf16[256,1024]{1,0:T(8,128)(2,1)S(1)} %copy-done.2, f32[8,256]{1,0:T(8,128)S(1)} %bitcast.2), custom_call_target="tpu_custom_call" | custom-call | flops 2000000 | bytes 1048576 | tf_op jit(solution)/shard_map/pallas_call | solution.py:24
  50.1 3.3 %collective-permute-start.19 = (bf16[512,128]{1,0:T(8,128)(2,1)S(1)}, bf16[512,128]{1,0:T(8,128)(2,1)S(1)}, u32[]{:S(2)}, u32[]{:S(2)}) collective-permute-start(bf16[512,128]{1,0:T(8,128)(2,1)S(1)} %collective-permute-done.18.b_ref), channel_id=1, source_target_pairs={{0,120},{8,0},{16,8},{24,16},{32,24},{40,32},{48,40},{56,48},{64,5... | collective-permute-start | bytes 393224 | tf_op jit(solution)/shard_map/ppermute | solution.py:310
  53.5 2.4 %collective-permute-done.recv_ref = bf16[544,128]{1,0:T(8,128)(2,1)S(1)} collective-permute-done((bf16[544,128]{1,0:T(8,128)(2,1)S(1)}, bf16[544,128]{1,0:T(8,128)(2,1)S(1)}, u32[]{:S(2)}, u32[]{:S(2)}) %collective-permute-start) | collective-permute-done | bytes 139296 | tf_op jit(solution)/shard_map/ppermute | solution.py:310
  56.1 5.3 %collective-permute-done.1.recv_ref = bf16[288,128]{1,0:T(8,128)(2,1)S(1)} collective-permute-done((bf16[288,128]{1,0:T(8,128)(2,1)S(1)}, bf16[288,128]{1,0:T(8,128)(2,1)S(1)}, u32[]{:S(2)}, u32[]{:S(2)}) %collective-permute-start.1) | collective-permute-done | bytes 73760 | tf_op jit(solution)/shard_map/ppermute | solution.py:310
  61.6 8.0 %collective-permute-done.2.recv_ref = bf16[160,128]{1,0:T(8,128)(2,1)S(1)} collective-permute-done((bf16[160,128]{1,0:T(8,128)(2,1)S(1)}, bf16[160,128]{1,0:T(8,128)(2,1)S(1)}, u32[]{:S(2)}, u32[]{:S(2)}) %collective-permute-start.2) | collective-permute-done | bytes 40992 | tf_op jit(solution)/shard_map/ppermute | solution.py:310
  69.6 0.6 shard_map.108
  70.2 4.4 %collective-permute-start.3 = (bf16[128,128]{1,0:T(8,128)(2,1)S(1)}, bf16[128,128]{1,0:T(8,128)(2,1)S(1)}, u32[]{:S(2)}, u32[]{:S(2)}) collective-permute-start(bf16[128,128]{1,0:T(8,128)(2,1)S(1)} %get-tuple-element.62), channel_id=1, source_target_pairs={{0,96},{8,104},{16,112},{24,120},{32,64},{40,72},{48,80},{56,88},{... | collective-permute-start | bytes 98312 | tf_op jit(solution)/shard_map/ppermute | solution.py:310
  74.6 1.5 %collective-permute-start.20 = (bf16[512,128]{1,0:T(8,128)(2,1)S(1)}, bf16[512,128]{1,0:T(8,128)(2,1)S(1)}, u32[]{:S(2)}, u32[]{:S(2)}) collective-permute-start(bf16[512,128]{1,0:T(8,128)(2,1)S(1)} %collective-permute-done.19.b_ref), channel_id=1, source_target_pairs={{0,120},{8,0},{16,8},{24,16},{32,24},{40,32},{48,40},{56,48},{64,5... | collective-permute-start | bytes 393224 | tf_op jit(solution)/shard_map/ppermute | solution.py:310
  76.1 0.9 collective-permute-start.13
  77.0 5.8 %collective-permute-start.4 = (bf16[128,128]{1,0:T(8,128)(2,1)S(1)}, bf16[128,128]{1,0:T(8,128)(2,1)S(1)}, u32[]{:S(2)}, u32[]{:S(2)}) collective-permute-start(bf16[128,128]{1,0:T(8,128)(2,1)S(1)} %get-tuple-element.66), channel_id=1, source_target_pairs={{0,32},{8,40},{16,48},{24,56},{32,0},{40,8},{48,16},{56,24},{64,96... | collective-permute-start | bytes 98312 | tf_op jit(solution)/shard_map/ppermute | solution.py:310
  82.8 3.2 %collective-permute-done.4.refs_1_ = bf16[128,128]{1,0:T(8,128)(2,1)S(1)} collective-permute-done((bf16[128,128]{1,0:T(8,128)(2,1)S(1)}, bf16[128,128]{1,0:T(8,128)(2,1)S(1)}, u32[]{:S(2)}, u32[]{:S(2)}) %collective-permute-start.4) | collective-permute-done | bytes 32800 | tf_op jit(solution)/shard_map/ppermute | solution.py:310
  86.1 2.9 %collective-permute-start.5 = (bf16[256,128]{1,0:T(8,128)(2,1)S(1)}, bf16[256,128]{1,0:T(8,128)(2,1)S(1)}, u32[]{:S(2)}, u32[]{:S(2)}) collective-permute-start(bf16[256,128]{1,0:T(8,128)(2,1)S(1)} %get-tuple-element.70), channel_id=1, source_target_pairs={{0,16},{8,24},{16,0},{24,8},{32,48},{40,56},{48,32},{56,40},{64,80... | collective-permute-start | bytes 196616 | tf_op jit(solution)/shard_map/ppermute | solution.py:310
  89.0 2.4 %collective-permute-done.5.refs_1_ = bf16[256,128]{1,0:T(8,128)(2,1)S(1)} collective-permute-done((bf16[256,128]{1,0:T(8,128)(2,1)S(1)}, bf16[256,128]{1,0:T(8,128)(2,1)S(1)}, u32[]{:S(2)}, u32[]{:S(2)}) %collective-permute-start.5) | collective-permute-done | bytes 65568 | tf_op jit(solution)/shard_map/ppermute | solution.py:310
  91.5 3.2 %collective-permute-start.6 = (bf16[512,128]{1,0:T(8,128)(2,1)S(1)}, bf16[512,128]{1,0:T(8,128)(2,1)S(1)}, u32[]{:S(2)}, u32[]{:S(2)}) collective-permute-start(bf16[512,128]{1,0:T(8,128)(2,1)S(1)} %get-tuple-element.74), channel_id=1, source_target_pairs={{0,8},{8,0},{16,24},{24,16},{32,40},{40,32},{48,56},{56,48},{64,72... | collective-permute-start | bytes 393224 | tf_op jit(solution)/shard_map/ppermute | solution.py:310
  94.7 4.0 %collective-permute-start.21 = (bf16[512,128]{1,0:T(8,128)(2,1)S(1)}, bf16[512,128]{1,0:T(8,128)(2,1)S(1)}, u32[]{:S(2)}, u32[]{:S(2)}) collective-permute-start(bf16[512,128]{1,0:T(8,128)(2,1)S(1)} %collective-permute-done.20.b_ref), channel_id=1, source_target_pairs={{0,120},{8,0},{16,8},{24,16},{32,24},{40,32},{48,40},{56,48},{64,5... | collective-permute-start | bytes 393224 | tf_op jit(solution)/shard_map/ppermute | solution.py:310
  98.7 1.4 %shard_map.113 = (bf16[2048,256]{1,0:T(8,128)(2,1)S(1)}, f32[2048,128]{1,0:T(8,128)S(1)}, f32[2048,128]{1,0:T(8,128)S(1)}, f32[2048,128]{1,0:T(8,128)S(1)}) custom-call(s32[16]{0:T(128)S(1)} %copy-done.8, bf16[256,1024]{1,0:T(8,128)(2,1)S(1)} %copy-done.5, bf16[256,128]{1,0:T(8,128)(2,1)S(1)} %copy-done.6, bf16[256,128]{1,0:T(8,128)(2,1)S(1)} %copy-done.7), custom_call_target="tpu_custom_call" | custom-call | flops 2000000 | bytes 1048576 | tf_op jit(solution)/shard_map/pallas_call | solution.py:24
  100.2 1.5 %shard_map.105.inside_ref = f32[256,1024]{1,0:T(8,128)S(1)} custom-call(s32[16]{0:T(128)S(1)} %copy-done.8, bf16[256,1024]{1,0:T(8,128)(2,1)S(1)} %copy-done.4, bf16[256,1024]{1,0:T(8,128)(2,1)S(1)} %copy-done.1, bf16[256,1024]{1,0:T(8,128)(2,1)S(1)} %copy-done.3, f32[8,256]{1,0:T(8,128)S(1)} %get-tuple-element.51.c_ref, f32[256,8]{1,0:T(8,128)S(1)} %get-tuple-element.52.ct_ref), custom_call_target="tpu_custom_call" | custom-call | flops 2000000 | bytes 1048576 | tf_op jit(solution)/shard_map/pallas_call | solution.py:24
  103.5 2.4 %shard_map.112 = bf16[256,1024]{1,0:T(8,128)(2,1)} custom-call(s32[16]{0:T(128)S(1)} %copy-done.8, bf16[256,1024]{1,0:T(8,128)(2,1)S(1)} %copy-done.4, f32[256,1024]{1,0:T(8,128)S(1)} %shard_map.105.inside_ref, f32[4,128,128]{2,1,0:T(8,128)S(1)} %get-tuple-element.73.held_ref, bf16[512,128]{1,0:T(8,128)(2,1)S(1)} %collective-permute-done.6.recv_ref, ...), custom_call_target="tpu_custom_call" | custom-call | flops 2000000 | bytes 1048576 | tf_op jit(solution)/shard_map/pallas_call | solution.py:24
  105.9 0.8 shard_map.117
  108.4 1.7 %shard_map.121 = bf16[256,1024]{1,0:T(8,128)(2,1)} custom-call(s32[16]{0:T(128)S(1)} %copy-done.8, bf16[2048,256]{1,0:T(8,128)(2,1)S(1)} %get-tuple-element.75.q2_ref, bf16[512,128]{1,0:T(8,128)(2,1)S(1)} %collective-permute-done.14.f_ref, f32[2048,128]{1,0:T(8,128)S(1)} %get-tuple-element.97.m_ref, f32[2048,128]{1,0:T(8,128)S(1)} %get-tuple-element.98.l_ref, ...), custom_call_target="tpu_custom_call" | custom-call | flops 2000000 | bytes 1048576 | tf_op jit(solution)/shard_map/pallas_call | solution.py:24
  (54 shorter events, 4.3 us)
Async XLA Ops:
  0.6 0.9 copy-start.7
  1.5 45.0 %copy-start.9 = (f32[256,8]{0,1:T(8,128)S(1)}, f32[256,8]{0,1:T(8,128)}, u32[]{:S(2)}) copy-start(f32[256,8]{0,1:T(8,128)} %param.12) | copy-start | bytes 24580
  1.5 44.9 %copy-start.8 = (s32[16]{0:T(128)S(1)}, s32[16]{0:T(128)}, u32[]{:S(2)}) copy-start(s32[16]{0:T(128)} %len_ref.23) | copy-start | bytes 196
  1.6 26.1 %collective-permute-start.7 = (bf16[512,128]{1,0:T(8,128)(2,1)S(1)}, bf16[512,128]{1,0:T(8,128)(2,1)S(1)}, u32[]{:S(2)}, u32[]{:S(2)}) collective-permute-start(bf16[512,128]{1,0:T(8,128)(2,1)S(1)} %constant_dynamic-update-slice_fusion), channel_id=1, source_target_pairs={{0,8},{8,16},{16,24},{24,32},{32,40},{40,48},{48,56},{56,64},{64,7... | collective-permute-start | bytes 393224 | tf_op jit(solution)/shard_map/ppermute | solution.py:310
  4.4 23.2 %collective-permute-start.15 = (bf16[512,128]{1,0:T(8,128)(2,1)S(1)}, bf16[512,128]{1,0:T(8,128)(2,1)S(1)}, u32[]{:S(2)}, u32[]{:S(2)}) collective-permute-start(bf16[512,128]{1,0:T(8,128)(2,1)S(1)} %constant_dynamic-update-slice_fusion), channel_id=1, source_target_pairs={{0,120},{8,0},{16,8},{24,16},{32,24},{40,32},{48,40},{56,48},{64,5... | collective-permute-start | bytes 393224 | tf_op jit(solution)/shard_map/ppermute | solution.py:310
  27.6 6.2 %collective-permute-start.8 = (bf16[512,128]{1,0:T(8,128)(2,1)S(1)}, bf16[512,128]{1,0:T(8,128)(2,1)S(1)}, u32[]{:S(2)}, u32[]{:S(2)}) collective-permute-start(bf16[512,128]{1,0:T(8,128)(2,1)S(1)} %collective-permute-done.7.f_ref), channel_id=1, source_target_pairs={{0,8},{8,16},{16,24},{24,32},{32,40},{40,48},{48,56},{56,64},{64,7... | collective-permute-start | bytes 393224 | tf_op jit(solution)/shard_map/ppermute | solution.py:310
  27.6 6.2 %collective-permute-start.16 = (bf16[512,128]{1,0:T(8,128)(2,1)S(1)}, bf16[512,128]{1,0:T(8,128)(2,1)S(1)}, u32[]{:S(2)}, u32[]{:S(2)}) collective-permute-start(bf16[512,128]{1,0:T(8,128)(2,1)S(1)} %collective-permute-done.15.b_ref), channel_id=1, source_target_pairs={{0,120},{8,0},{16,8},{24,16},{32,24},{40,32},{48,40},{56,48},{64,5... | collective-permute-start | bytes 393224 | tf_op jit(solution)/shard_map/ppermute | solution.py:310
  33.8 6.2 %collective-permute-start.9 = (bf16[512,128]{1,0:T(8,128)(2,1)S(1)}, bf16[512,128]{1,0:T(8,128)(2,1)S(1)}, u32[]{:S(2)}, u32[]{:S(2)}) collective-permute-start(bf16[512,128]{1,0:T(8,128)(2,1)S(1)} %collective-permute-done.8.f_ref), channel_id=1, source_target_pairs={{0,8},{8,16},{16,24},{24,32},{32,40},{40,48},{48,56},{56,64},{64,7... | collective-permute-start | bytes 393224 | tf_op jit(solution)/shard_map/ppermute | solution.py:310
  33.8 6.2 %collective-permute-start.17 = (bf16[512,128]{1,0:T(8,128)(2,1)S(1)}, bf16[512,128]{1,0:T(8,128)(2,1)S(1)}, u32[]{:S(2)}, u32[]{:S(2)}) collective-permute-start(bf16[512,128]{1,0:T(8,128)(2,1)S(1)} %collective-permute-done.16.b_ref), channel_id=1, source_target_pairs={{0,120},{8,0},{16,8},{24,16},{32,24},{40,32},{48,40},{56,48},{64,5... | collective-permute-start | bytes 393224 | tf_op jit(solution)/shard_map/ppermute | solution.py:310
  40.0 6.5 %collective-permute-start.10 = (bf16[512,128]{1,0:T(8,128)(2,1)S(1)}, bf16[512,128]{1,0:T(8,128)(2,1)S(1)}, u32[]{:S(2)}, u32[]{:S(2)}) collective-permute-start(bf16[512,128]{1,0:T(8,128)(2,1)S(1)} %collective-permute-done.9.f_ref), channel_id=1, source_target_pairs={{0,8},{8,16},{16,24},{24,32},{32,40},{40,48},{48,56},{56,64},{64,7... | collective-permute-start | bytes 393224 | tf_op jit(solution)/shard_map/ppermute | solution.py:310
  40.0 10.1 %collective-permute-start.18 = (bf16[512,128]{1,0:T(8,128)(2,1)S(1)}, bf16[512,128]{1,0:T(8,128)(2,1)S(1)}, u32[]{:S(2)}, u32[]{:S(2)}) collective-permute-start(bf16[512,128]{1,0:T(8,128)(2,1)S(1)} %collective-permute-done.17.b_ref), channel_id=1, source_target_pairs={{0,120},{8,0},{16,8},{24,16},{32,24},{40,32},{48,40},{56,48},{64,5... | collective-permute-start | bytes 393224 | tf_op jit(solution)/shard_map/ppermute | solution.py:310
  46.5 7.0 %collective-permute-start.11 = (bf16[512,128]{1,0:T(8,128)(2,1)S(1)}, bf16[512,128]{1,0:T(8,128)(2,1)S(1)}, u32[]{:S(2)}, u32[]{:S(2)}) collective-permute-start(bf16[512,128]{1,0:T(8,128)(2,1)S(1)} %collective-permute-done.10.f_ref), channel_id=1, source_target_pairs={{0,8},{8,16},{16,24},{24,32},{32,40},{40,48},{48,56},{56,64},{64,7... | collective-permute-start | bytes 393224 | tf_op jit(solution)/shard_map/ppermute | solution.py:310
  46.5 1.0 copy-start
  47.5 1.0 copy-start.2
  50.0 5.9 %collective-permute-start = (bf16[544,128]{1,0:T(8,128)(2,1)S(1)}, bf16[544,128]{1,0:T(8,128)(2,1)S(1)}, u32[]{:S(2)}, u32[]{:S(2)}) collective-permute-start(bf16[544,128]{1,0:T(8,128)(2,1)S(1)} %get-tuple-element.53), channel_id=1, source_target_pairs={{0,8},{8,0},{16,24},{24,16},{32,40},{40,32},{48,56},{56,48},{64,72... | collective-permute-start | bytes 417800 | tf_op jit(solution)/shard_map/ppermute | solution.py:310
  50.1 24.5 %collective-permute-start.19 = (bf16[512,128]{1,0:T(8,128)(2,1)S(1)}, bf16[512,128]{1,0:T(8,128)(2,1)S(1)}, u32[]{:S(2)}, u32[]{:S(2)}) collective-permute-start(bf16[512,128]{1,0:T(8,128)(2,1)S(1)} %collective-permute-done.18.b_ref), channel_id=1, source_target_pairs={{0,120},{8,0},{16,8},{24,16},{32,24},{40,32},{48,40},{56,48},{64,5... | collective-permute-start | bytes 393224 | tf_op jit(solution)/shard_map/ppermute | solution.py:310
  53.5 22.6 %collective-permute-start.12 = (bf16[512,128]{1,0:T(8,128)(2,1)S(1)}, bf16[512,128]{1,0:T(8,128)(2,1)S(1)}, u32[]{:S(2)}, u32[]{:S(2)}) collective-permute-start(bf16[512,128]{1,0:T(8,128)(2,1)S(1)} %collective-permute-done.11.f_ref), channel_id=1, source_target_pairs={{0,8},{8,16},{16,24},{24,32},{32,40},{40,48},{48,56},{56,64},{64,7... | collective-permute-start | bytes 393224 | tf_op jit(solution)/shard_map/ppermute | solution.py:310
  55.9 42.8 %copy-start.5 = (bf16[256,1024]{1,0:T(8,128)(2,1)S(1)}, bf16[256,1024]{1,0:T(8,128)(2,1)}, u32[]{:S(2)}) copy-start(bf16[256,1024]{1,0:T(8,128)(2,1)} %q_ref.5) | copy-start | bytes 1572868
  56.0 5.4 %collective-permute-start.1 = (bf16[288,128]{1,0:T(8,128)(2,1)S(1)}, bf16[288,128]{1,0:T(8,128)(2,1)S(1)}, u32[]{:S(2)}, u32[]{:S(2)}) collective-permute-start(bf16[288,128]{1,0:T(8,128)(2,1)S(1)} %get-tuple-element.56), channel_id=1, source_target_pairs={{0,16},{8,24},{16,0},{24,8},{32,48},{40,56},{48,32},{56,40},{64,80... | collective-permute-start | bytes 221192 | tf_op jit(solution)/shard_map/ppermute | solution.py:310
  61.4 37.3 %copy-start.6 = (bf16[256,128]{1,0:T(8,128)(2,1)S(1)}, bf16[256,128]{1,0:T(8,128)(2,1)}, u32[]{:S(2)}) copy-start(bf16[256,128]{1,0:T(8,128)(2,1)} %k_ref.5) | copy-start | bytes 196612
  61.5 8.1 %collective-permute-start.2 = (bf16[160,128]{1,0:T(8,128)(2,1)S(1)}, bf16[160,128]{1,0:T(8,128)(2,1)S(1)}, u32[]{:S(2)}, u32[]{:S(2)}) collective-permute-start(bf16[160,128]{1,0:T(8,128)(2,1)S(1)} %get-tuple-element.59), channel_id=1, source_target_pairs={{0,32},{8,40},{16,48},{24,56},{32,0},{40,8},{48,16},{56,24},{64,96... | collective-permute-start | bytes 122888 | tf_op jit(solution)/shard_map/ppermute | solution.py:310
  69.6 30.6 %copy-start.4 = (bf16[256,1024]{1,0:T(8,128)(2,1)S(1)}, bf16[256,1024]{1,0:T(8,128)(2,1)}, u32[]{:S(2)}) copy-start(bf16[256,1024]{1,0:T(8,128)(2,1)} %q_ref.4) | copy-start | bytes 1572868
  70.2 6.8 %collective-permute-start.3 = (bf16[128,128]{1,0:T(8,128)(2,1)S(1)}, bf16[128,128]{1,0:T(8,128)(2,1)S(1)}, u32[]{:S(2)}, u32[]{:S(2)}) collective-permute-start(bf16[128,128]{1,0:T(8,128)(2,1)S(1)} %get-tuple-element.62), channel_id=1, source_target_pairs={{0,96},{8,104},{16,112},{24,120},{32,64},{40,72},{48,80},{56,88},{... | collective-permute-start | bytes 98312 | tf_op jit(solution)/shard_map/ppermute | solution.py:310
  74.6 20.1 %collective-permute-start.20 = (bf16[512,128]{1,0:T(8,128)(2,1)S(1)}, bf16[512,128]{1,0:T(8,128)(2,1)S(1)}, u32[]{:S(2)}, u32[]{:S(2)}) collective-permute-start(bf16[512,128]{1,0:T(8,128)(2,1)S(1)} %collective-permute-done.19.b_ref), channel_id=1, source_target_pairs={{0,120},{8,0},{16,8},{24,16},{32,24},{40,32},{48,40},{56,48},{64,5... | collective-permute-start | bytes 393224 | tf_op jit(solution)/shard_map/ppermute | solution.py:310
  76.1 22.6 %collective-permute-start.13 = (bf16[512,128]{1,0:T(8,128)(2,1)S(1)}, bf16[512,128]{1,0:T(8,128)(2,1)S(1)}, u32[]{:S(2)}, u32[]{:S(2)}) collective-permute-start(bf16[512,128]{1,0:T(8,128)(2,1)S(1)} %collective-permute-done.12.f_ref), channel_id=1, source_target_pairs={{0,8},{8,16},{16,24},{24,32},{32,40},{40,48},{48,56},{56,64},{64,7... | collective-permute-start | bytes 393224 | tf_op jit(solution)/shard_map/ppermute | solution.py:310
  77.0 9.0 %collective-permute-start.4 = (bf16[128,128]{1,0:T(8,128)(2,1)S(1)}, bf16[128,128]{1,0:T(8,128)(2,1)S(1)}, u32[]{:S(2)}, u32[]{:S(2)}) collective-permute-start(bf16[128,128]{1,0:T(8,128)(2,1)S(1)} %get-tuple-element.66), channel_id=1, source_target_pairs={{0,32},{8,40},{16,48},{24,56},{32,0},{40,8},{48,16},{56,24},{64,96... | collective-permute-start | bytes 98312 | tf_op jit(solution)/shard_map/ppermute | solution.py:310
  86.1 5.3 %collective-permute-start.5 = (bf16[256,128]{1,0:T(8,128)(2,1)S(1)}, bf16[256,128]{1,0:T(8,128)(2,1)S(1)}, u32[]{:S(2)}, u32[]{:S(2)}) collective-permute-start(bf16[256,128]{1,0:T(8,128)(2,1)S(1)} %get-tuple-element.70), channel_id=1, source_target_pairs={{0,16},{8,24},{16,0},{24,8},{32,48},{40,56},{48,32},{56,40},{64,80... | collective-permute-start | bytes 196616 | tf_op jit(solution)/shard_map/ppermute | solution.py:310
  91.4 8.8 %copy-start.1 = (bf16[256,1024]{1,0:T(8,128)(2,1)S(1)}, bf16[256,1024]{1,0:T(8,128)(2,1)}, u32[]{:S(2)}) copy-start(bf16[256,1024]{1,0:T(8,128)(2,1)} %k_ref.4) | copy-start | bytes 1572868
  91.4 8.8 %copy-start.3 = (bf16[256,1024]{1,0:T(8,128)(2,1)S(1)}, bf16[256,1024]{1,0:T(8,128)(2,1)}, u32[]{:S(2)}) copy-start(bf16[256,1024]{1,0:T(8,128)(2,1)} %v_ref.4) | copy-start | bytes 1572868
  91.5 11.9 %collective-permute-start.6 = (bf16[512,128]{1,0:T(8,128)(2,1)S(1)}, bf16[512,128]{1,0:T(8,128)(2,1)S(1)}, u32[]{:S(2)}, u32[]{:S(2)}) collective-permute-start(bf16[512,128]{1,0:T(8,128)(2,1)S(1)} %get-tuple-element.74), channel_id=1, source_target_pairs={{0,8},{8,0},{16,24},{24,16},{32,40},{40,32},{48,56},{56,48},{64,72... | collective-permute-start | bytes 393224 | tf_op jit(solution)/shard_map/ppermute | solution.py:310
  94.7 13.2 %collective-permute-start.21 = (bf16[512,128]{1,0:T(8,128)(2,1)S(1)}, bf16[512,128]{1,0:T(8,128)(2,1)S(1)}, u32[]{:S(2)}, u32[]{:S(2)}) collective-permute-start(bf16[512,128]{1,0:T(8,128)(2,1)S(1)} %collective-permute-done.20.b_ref), channel_id=1, source_target_pairs={{0,120},{8,0},{16,8},{24,16},{32,24},{40,32},{48,40},{56,48},{64,5... | collective-permute-start | bytes 393224 | tf_op jit(solution)/shard_map/ppermute | solution.py:310
  98.7 9.7 %collective-permute-start.14 = (bf16[512,128]{1,0:T(8,128)(2,1)S(1)}, bf16[512,128]{1,0:T(8,128)(2,1)S(1)}, u32[]{:S(2)}, u32[]{:S(2)}) collective-permute-start(bf16[512,128]{1,0:T(8,128)(2,1)S(1)} %collective-permute-done.13.f_ref), channel_id=1, source_target_pairs={{0,8},{8,16},{16,24},{24,32},{32,40},{40,48},{48,56},{56,64},{64,7... | collective-permute-start | bytes 393224 | tf_op jit(solution)/shard_map/ppermute | solution.py:310
  (1 other events, 0.7 us)
where the time goes:
time: 110 us
  starting transfers between devices  58.8 us (53%)
  waiting for transfers between devices  33.9 us (31%)
  Pallas kernels  13.5 us (12%)
  local copies, waits for them, and re-layouts  3.11 us (3%)
    ppermute x22, starting transfers between devices, send(): return lax.ppermute(x, 'seq', pairs)  58.8 us
    ppermute x22, waiting for transfers between devices, send(): return lax.ppermute(x, 'seq', pairs)  33.9 us
    pallas_call x18, Pallas kernels, call(): pl.pallas_call(kernel, out_shape=outs, in_specs=specs, out_specs=[VMEM] *...  13.5 us
    unnamed x23, local copies, waits for them, and re-layouts  3.09 us
  transfers between devices with their start and end apart: 22, of which 9 were waited for; matrix products, arithmetic and copies ran while one was open for 0% of the time, Pallas kernels for 11%

commit v1 on v0

--- a/solution.py
+++ b/solution.py
@@ -14,11 +14,12 @@
 LOG2E = 1.4426950408889634
 E_ROWS = 32
 VMEM = pl.BlockSpec(memory_space=pltpu.VMEM)
+ANY = pl.BlockSpec(memory_space=pltpu.HBM)
 SMEM = pl.BlockSpec(memory_space=pltpu.SMEM)
 
 
 def call(kernel, out_shape, ins, aliases=None, flops=2_000_000, scratch=()):
-    specs = [SMEM if s else VMEM for s, unused in ins]
+    specs = [ANY if s is None else SMEM if s else VMEM for s, unused in ins]
     arrays = [a for unused, a in ins]
     outs = [jax.ShapeDtypeStruct(s, d) for s, d in out_shape]
     return pl.pallas_call(
@@ -64,7 +65,11 @@
     return rows[0:8] + rows[8:16] + rows[16:24]
 
 
-def prep_kernel(len_ref, k_ref, v_ref, dec_ref, msg_ref, kept_ref, logs_ref, c_ref, ct_ref, states):
+def prep_kernel(len_ref, k_hbm, v_hbm, dec_ref, msg_ref, kept_ref, logs_ref, c_ref, ct_ref, states, k_ref, v_ref, sems):
+    k_copy = pltpu.make_async_copy(k_hbm, k_ref, sems.at[0])
+    v_copy = pltpu.make_async_copy(v_hbm, v_ref, sems.at[1])
+    k_copy.start()
+    v_copy.start()
     i = lax.axis_index("seq")
     rows = k_ref.shape[0]
     heads = dec_ref.shape[0]
@@ -85,6 +90,8 @@
     logs = jnp.broadcast_to(ending, (heads, 128))
     logs_ref[...] = logs
     fading = jnp.where(live, jnp.exp(ending - running), 0.0)
+    k_copy.wait()
+    v_copy.wait()
     for h in range(heads):
         kt = k_ref[:, h * width : (h + 1) * width].T.astype(F32)
         scaled = (kt * fading[h : h + 1, :]).astype(BF16)
@@ -303,8 +310,13 @@
     width = light_queries.shape[1] // heads
     count = lax.axis_size("seq")
     half = heads // 2
-    forward = [(i, (i + 1) % count) for i in range(count)]
-    backward = [(i, (i - 1) % count) for i in range(count)]
+    back = count // 2 - 1
+
+    def forward(step):
+        return [(i, i + 1) for i in range(step - 1, count - 1)]
+
+    def backward(step):
+        return [((j + 1) % count, j) for j in range(count) if j + step < back or j + step >= count]
 
     def send(x, pairs):
         return lax.ppermute(x, "seq", pairs)
@@ -314,8 +326,8 @@
 
     lens = (True, lengths)
     own_kv = jnp.concatenate([soft_keys, soft_values], axis=0)
-    f = send(own_kv, forward)
-    b = send(own_kv, backward)
+    f = send(own_kv, forward(1))
+    b = send(own_kv, backward(1))
 
     msg, kept, logs, running, running_t = call(
         prep_kernel,
@@ -326,8 +338,13 @@
             ((heads, rows), F32),
             ((rows, heads), F32),
         ],
-        [lens, (False, light_keys), (False, light_values), (False, decay_log.T)],
-        scratch=[pltpu.VMEM((heads, width, width), F32)],
+        [lens, (None, light_keys), (None, light_values), (False, decay_log.T)],
+        scratch=[
+            pltpu.VMEM((heads, width, width), F32),
+            pltpu.VMEM((rows, heads * width), BF16),
+            pltpu.VMEM((rows, heads * width), BF16),
+            pltpu.SemaphoreType.DMA((2,)),
+        ],
     )
     saved = []
     n = half
@@ -357,9 +374,7 @@
         if held is not None:
             ins = [(False, held)] + ins
         held, msg = call(
-            partial(down_kernel, level, held is None),
-            [((n, width, width), F32), ((n * width, width), BF16)],
-            ins,
+            partial(down_kernel, level, held is None), [((n, width, width), F32), ((n * width, width), BF16)], ins
         )
         recv = exchange(msg, 1 << level)
     (inside,) = call(
@@ -396,8 +411,8 @@
         [lens, (False, soft_queries), (False, soft_keys), (False, soft_values)],
     )
     for step in range(1, count // 2):
-        nf = send(f, forward)
-        nb = send(b, backward) if step + 1 < count // 2 else None
+        nf = send(f, forward(step + 1))
+        nb = send(b, backward(step + 1)) if step + 1 < count // 2 else None
         state = call(
             partial(step_kernel, step, count),
             [stat, stat, stat],

time: 110 us -> 122 us (1.11)
  starting transfers between devices: 58.8 us -> 72.2 us
  waiting for transfers between devices: 33.9 us -> 30.9 us
    ppermute x22, starting transfers between devices: 58.8 us -> 72.2 us  [send(): return lax.ppermute(x, 'seq', pairs)]
    ppermute x22, waiting for transfers between devices: 33.9 us -> 30.9 us  [send(): return lax.ppermute(x, 'seq', pairs)]
  transfers between devices with their start and end apart: 22 -> 22, of which waited for: 9 -> 7; matrix products, arithmetic and copies ran while one was open for 0% -> 0% of each run, Pallas kernels for 11% -> 10%
where the time goes in v1:
time: 122 us; the launch traced here: 121 us
  starting transfers between devices  72.2 us (59%)
  waiting for transfers between devices  30.9 us (25%)
  Pallas kernels  13.7 us (11%)
  local copies, waits for them, and re-layouts  3.01 us (2%)
    ppermute x22, starting transfers between devices, send(): return lax.ppermute(x, 'seq', pairs)  72.2 us
    ppermute x22, waiting for transfers between devices, send(): return lax.ppermute(x, 'seq', pairs)  30.9 us
    pallas_call x18, Pallas kernels, call(): pl.pallas_call(kernel, out_shape=outs, in_specs=specs, out_specs=[VMEM] *...  13.7 us
    unnamed x23, local copies, waits for them, and re-layouts  3 us
  transfers between devices with their start and end apart: 22, of which 7 were waited for; matrix products, arithmetic and copies ran while one was open for 0% of the time, Pallas kernels for 10%

profile of v1, /device:TPU:36, one launch (start us, length us, event | category | flops | bytes accessed | tf_op | source)
XLA Modules:
  0.0 120.9 jit_solution(6493665523465591436)
XLA Ops:
  0.6 0.9 constant_dynamic-update-slice_fusion.1
  1.6 4.7 %collective-permute-start.7 = (bf16[512,128]{1,0:T(8,128)(2,1)S(1)}, bf16[512,128]{1,0:T(8,128)(2,1)S(1)}, u32[]{:S(2)}, u32[]{:S(2)}) collective-permute-start(bf16[512,128]{1,0:T(8,128)(2,1)S(1)} %constant_dynamic-update-slice_fusion), channel_id=1, source_target_pairs={{0,8},{8,16},{16,24},{24,32},{32,40},{40,48},{48,56},{56,64},{64,7... | collective-permute-start | bytes 393224 | tf_op jit(solution)/shard_map/ppermute | solution.py:322
  6.3 20.9 %collective-permute-start.15 = (bf16[512,128]{1,0:T(8,128)(2,1)S(1)}, bf16[512,128]{1,0:T(8,128)(2,1)S(1)}, u32[]{:S(2)}, u32[]{:S(2)}) collective-permute-start(bf16[512,128]{1,0:T(8,128)(2,1)S(1)} %constant_dynamic-update-slice_fusion), channel_id=1, source_target_pairs={{8,0},{16,8},{24,16},{32,24},{40,32},{48,40},{0,120},{9,1},{17,9},... | collective-permute-start | bytes 393224 | tf_op jit(solution)/shard_map/ppermute | solution.py:322
  27.2 0.7 collective-permute-start.8
  27.9 2.1 %collective-permute-done.15.b_ref = bf16[512,128]{1,0:T(8,128)(2,1)S(1)} collective-permute-done((bf16[512,128]{1,0:T(8,128)(2,1)S(1)}, bf16[512,128]{1,0:T(8,128)(2,1)S(1)}, u32[]{:S(2)}, u32[]{:S(2)}) %collective-permute-start.15) | collective-permute-done | bytes 131104 | tf_op jit(solution)/shard_map/ppermute | solution.py:322
  30.0 5.6 %collective-permute-start.16 = (bf16[512,128]{1,0:T(8,128)(2,1)S(1)}, bf16[512,128]{1,0:T(8,128)(2,1)S(1)}, u32[]{:S(2)}, u32[]{:S(2)}) collective-permute-start(bf16[512,128]{1,0:T(8,128)(2,1)S(1)} %collective-permute-done.15.b_ref), channel_id=1, source_target_pairs={{8,0},{16,8},{24,16},{32,24},{40,32},{120,112},{0,120},{9,1},{17,9... | collective-permute-start | bytes 393224 | tf_op jit(solution)/shard_map/ppermute | solution.py:322
  35.6 0.7 collective-permute-start.9
  36.3 1.8 %collective-permute-done.16.b_ref = bf16[512,128]{1,0:T(8,128)(2,1)S(1)} collective-permute-done((bf16[512,128]{1,0:T(8,128)(2,1)S(1)}, bf16[512,128]{1,0:T(8,128)(2,1)S(1)}, u32[]{:S(2)}, u32[]{:S(2)}) %collective-permute-start.16) | collective-permute-done | bytes 131104 | tf_op jit(solution)/shard_map/ppermute | solution.py:322
  38.1 5.6 %collective-permute-start.17 = (bf16[512,128]{1,0:T(8,128)(2,1)S(1)}, bf16[512,128]{1,0:T(8,128)(2,1)S(1)}, u32[]{:S(2)}, u32[]{:S(2)}) collective-permute-start(bf16[512,128]{1,0:T(8,128)(2,1)S(1)} %collective-permute-done.16.b_ref), channel_id=1, source_target_pairs={{8,0},{16,8},{24,16},{32,24},{112,104},{120,112},{0,120},{9,1},{17... | collective-permute-start | bytes 393224 | tf_op jit(solution)/shard_map/ppermute | solution.py:322
  43.7 0.7 collective-permute-start.10
  44.4 1.8 %collective-permute-done.17.b_ref = bf16[512,128]{1,0:T(8,128)(2,1)S(1)} collective-permute-done((bf16[512,128]{1,0:T(8,128)(2,1)S(1)}, bf16[512,128]{1,0:T(8,128)(2,1)S(1)}, u32[]{:S(2)}, u32[]{:S(2)}) %collective-permute-start.17) | collective-permute-done | bytes 131104 | tf_op jit(solution)/shard_map/ppermute | solution.py:322
  46.2 5.6 %collective-permute-start.18 = (bf16[512,128]{1,0:T(8,128)(2,1)S(1)}, bf16[512,128]{1,0:T(8,128)(2,1)S(1)}, u32[]{:S(2)}, u32[]{:S(2)}) collective-permute-start(bf16[512,128]{1,0:T(8,128)(2,1)S(1)} %collective-permute-done.17.b_ref), channel_id=1, source_target_pairs={{8,0},{16,8},{24,16},{104,96},{112,104},{120,112},{0,120},{9,1},{1... | collective-permute-start | bytes 393224 | tf_op jit(solution)/shard_map/ppermute | solution.py:322
  51.8 0.7 collective-permute-start.11
  52.5 1.0 copy-done
  53.6 1.0 copy-done.2
  54.6 1.6 %shard_map.104 = (bf16[544,128]{1,0:T(8,128)(2,1)S(1)}, f32[4,128,128]{2,1,0:T(8,128)S(1)}, f32[8,128]{1,0:T(8,128)S(1)}, f32[8,256]{1,0:T(8,128)S(1)}, f32[256,8]{1,0:T(8,128)S(1)}) custom-call(s32[16]{0:T(128)S(1)} %copy-done.8, bf16[256,1024]{1,0:T(8,128)(2,1)S(1)} %copy-done, bf16[256,1024]{1,0:T(8,128)(2,1)S(1)} %copy-done.2, f32[8,256]{1,0:T(8,128)S(1)} %bitcast.2), custom_call_target="tpu_custom_call" | custom-call | flops 2000000 | bytes 1048576 | tf_op jit(solution)/shard_map/pallas_call | solution.py:25
  56.4 5.2 %collective-permute-start.19 = (bf16[512,128]{1,0:T(8,128)(2,1)S(1)}, bf16[512,128]{1,0:T(8,128)(2,1)S(1)}, u32[]{:S(2)}, u32[]{:S(2)}) collective-permute-start(bf16[512,128]{1,0:T(8,128)(2,1)S(1)} %collective-permute-done.18.b_ref), channel_id=1, source_target_pairs={{8,0},{16,8},{96,88},{104,96},{112,104},{120,112},{0,120},{9,1},{1... | collective-permute-start | bytes 393224 | tf_op jit(solution)/shard_map/ppermute | solution.py:322
  62.7 5.1 %collective-permute-done.1.recv_ref = bf16[288,128]{1,0:T(8,128)(2,1)S(1)} collective-permute-done((bf16[288,128]{1,0:T(8,128)(2,1)S(1)}, bf16[288,128]{1,0:T(8,128)(2,1)S(1)}, u32[]{:S(2)}, u32[]{:S(2)}) %collective-permute-start.1) | collective-permute-done | bytes 73760 | tf_op jit(solution)/shard_map/ppermute | solution.py:322
  67.8 1.7 %collective-permute-start.2 = (bf16[160,128]{1,0:T(8,128)(2,1)S(1)}, bf16[160,128]{1,0:T(8,128)(2,1)S(1)}, u32[]{:S(2)}, u32[]{:S(2)}) collective-permute-start(bf16[160,128]{1,0:T(8,128)(2,1)S(1)} %get-tuple-element.59), channel_id=1, source_target_pairs={{0,32},{8,40},{16,48},{24,56},{32,0},{40,8},{48,16},{56,24},{64,96... | collective-permute-start | bytes 122888 | tf_op jit(solution)/shard_map/ppermute | solution.py:322
  69.5 6.9 %collective-permute-done.2.recv_ref = bf16[160,128]{1,0:T(8,128)(2,1)S(1)} collective-permute-done((bf16[160,128]{1,0:T(8,128)(2,1)S(1)}, bf16[160,128]{1,0:T(8,128)(2,1)S(1)}, u32[]{:S(2)}, u32[]{:S(2)}) %collective-permute-start.2) | collective-permute-done | bytes 40992 | tf_op jit(solution)/shard_map/ppermute | solution.py:322
  77.0 8.3 %collective-permute-start.3 = (bf16[128,128]{1,0:T(8,128)(2,1)S(1)}, bf16[128,128]{1,0:T(8,128)(2,1)S(1)}, u32[]{:S(2)}, u32[]{:S(2)}) collective-permute-start(bf16[128,128]{1,0:T(8,128)(2,1)S(1)} %get-tuple-element.62), channel_id=1, source_target_pairs={{0,96},{8,104},{16,112},{24,120},{32,64},{40,72},{48,80},{56,88},{... | collective-permute-start | bytes 98312 | tf_op jit(solution)/shard_map/ppermute | solution.py:322
  85.3 2.0 %collective-permute-start.20 = (bf16[512,128]{1,0:T(8,128)(2,1)S(1)}, bf16[512,128]{1,0:T(8,128)(2,1)S(1)}, u32[]{:S(2)}, u32[]{:S(2)}) collective-permute-start(bf16[512,128]{1,0:T(8,128)(2,1)S(1)} %collective-permute-done.19.b_ref), channel_id=1, source_target_pairs={{8,0},{88,80},{96,88},{104,96},{112,104},{120,112},{0,120},{9,1},{... | collective-permute-start | bytes 393224 | tf_op jit(solution)/shard_map/ppermute | solution.py:322
  87.3 0.7 collective-permute-start.13
  88.2 8.4 %collective-permute-done.4.refs_1_ = bf16[128,128]{1,0:T(8,128)(2,1)S(1)} collective-permute-done((bf16[128,128]{1,0:T(8,128)(2,1)S(1)}, bf16[128,128]{1,0:T(8,128)(2,1)S(1)}, u32[]{:S(2)}, u32[]{:S(2)}) %collective-permute-start.4) | collective-permute-done | bytes 32800 | tf_op jit(solution)/shard_map/ppermute | solution.py:322
  97.2 4.7 %collective-permute-done.5.refs_1_ = bf16[256,128]{1,0:T(8,128)(2,1)S(1)} collective-permute-done((bf16[256,128]{1,0:T(8,128)(2,1)S(1)}, bf16[256,128]{1,0:T(8,128)(2,1)S(1)}, u32[]{:S(2)}, u32[]{:S(2)}) %collective-permute-start.5) | collective-permute-done | bytes 65568 | tf_op jit(solution)/shard_map/ppermute | solution.py:322
  102.0 1.6 %collective-permute-start.6 = (bf16[512,128]{1,0:T(8,128)(2,1)S(1)}, bf16[512,128]{1,0:T(8,128)(2,1)S(1)}, u32[]{:S(2)}, u32[]{:S(2)}) collective-permute-start(bf16[512,128]{1,0:T(8,128)(2,1)S(1)} %get-tuple-element.74), channel_id=1, source_target_pairs={{0,8},{8,0},{16,24},{24,16},{32,40},{40,32},{48,56},{56,48},{64,72... | collective-permute-start | bytes 393224 | tf_op jit(solution)/shard_map/ppermute | solution.py:322
  103.6 5.3 %collective-permute-start.21 = (bf16[512,128]{1,0:T(8,128)(2,1)S(1)}, bf16[512,128]{1,0:T(8,128)(2,1)S(1)}, u32[]{:S(2)}, u32[]{:S(2)}) collective-permute-start(bf16[512,128]{1,0:T(8,128)(2,1)S(1)} %collective-permute-done.20.b_ref), channel_id=1, source_target_pairs={{80,72},{88,80},{96,88},{104,96},{112,104},{120,112},{0,120},{81,7... | collective-permute-start | bytes 393224 | tf_op jit(solution)/shard_map/ppermute | solution.py:322
  109.6 1.4 %shard_map.113 = (bf16[2048,256]{1,0:T(8,128)(2,1)S(1)}, f32[2048,128]{1,0:T(8,128)S(1)}, f32[2048,128]{1,0:T(8,128)S(1)}, f32[2048,128]{1,0:T(8,128)S(1)}) custom-call(s32[16]{0:T(128)S(1)} %copy-done.8, bf16[256,1024]{1,0:T(8,128)(2,1)S(1)} %copy-done.5, bf16[256,128]{1,0:T(8,128)(2,1)S(1)} %copy-done.6, bf16[256,128]{1,0:T(8,128)(2,1)S(1)} %copy-done.7), custom_call_target="tpu_custom_call" | custom-call | flops 2000000 | bytes 1048576 | tf_op jit(solution)/shard_map/pallas_call | solution.py:25
  111.1 1.5 %shard_map.105.inside_ref = f32[256,1024]{1,0:T(8,128)S(1)} custom-call(s32[16]{0:T(128)S(1)} %copy-done.8, bf16[256,1024]{1,0:T(8,128)(2,1)S(1)} %copy-done.4, bf16[256,1024]{1,0:T(8,128)(2,1)S(1)} %copy-done.1, bf16[256,1024]{1,0:T(8,128)(2,1)S(1)} %copy-done.3, f32[8,256]{1,0:T(8,128)S(1)} %get-tuple-element.51.c_ref, f32[256,8]{1,0:T(8,128)S(1)} %get-tuple-element.52.ct_ref), custom_call_target="tpu_custom_call" | custom-call | flops 2000000 | bytes 1048576 | tf_op jit(solution)/shard_map/pallas_call | solution.py:25
  113.7 0.7 shard_map.116
  114.5 2.4 %shard_map.112 = bf16[256,1024]{1,0:T(8,128)(2,1)} custom-call(s32[16]{0:T(128)S(1)} %copy-done.8, bf16[256,1024]{1,0:T(8,128)(2,1)S(1)} %copy-done.4, f32[256,1024]{1,0:T(8,128)S(1)} %shard_map.105.inside_ref, f32[4,128,128]{2,1,0:T(8,128)S(1)} %get-tuple-element.73.held_ref, bf16[512,128]{1,0:T(8,128)(2,1)S(1)} %collective-permute-done.6.recv_ref, ...), custom_call_target="tpu_custom_call" | custom-call | flops 2000000 | bytes 1048576 | tf_op jit(solution)/shard_map/pallas_call | solution.py:25
  119.2 1.7 %shard_map.121 = bf16[256,1024]{1,0:T(8,128)(2,1)} custom-call(s32[16]{0:T(128)S(1)} %copy-done.8, bf16[2048,256]{1,0:T(8,128)(2,1)S(1)} %get-tuple-element.75.q2_ref, bf16[512,128]{1,0:T(8,128)(2,1)S(1)} %collective-permute-done.14.f_ref, f32[2048,128]{1,0:T(8,128)S(1)} %get-tuple-element.97.m_ref, f32[2048,128]{1,0:T(8,128)S(1)} %get-tuple-element.98.l_ref, ...), custom_call_target="tpu_custom_call" | custom-call | flops 2000000 | bytes 1048576 | tf_op jit(solution)/shard_map/pallas_call | solution.py:25
  (54 shorter events, 6.8 us)
Async XLA Ops:
  0.6 0.9 copy-start.7
  1.5 51.0 %copy-start.9 = (f32[256,8]{0,1:T(8,128)S(1)}, f32[256,8]{0,1:T(8,128)}, u32[]{:S(2)}) copy-start(f32[256,8]{0,1:T(8,128)} %param.12) | copy-start | bytes 24580
  1.5 51.0 %copy-start.8 = (s32[16]{0:T(128)S(1)}, s32[16]{0:T(128)}, u32[]{:S(2)}) copy-start(s32[16]{0:T(128)} %len_ref.23) | copy-start | bytes 196
  1.6 25.6 %collective-permute-start.7 = (bf16[512,128]{1,0:T(8,128)(2,1)S(1)}, bf16[512,128]{1,0:T(8,128)(2,1)S(1)}, u32[]{:S(2)}, u32[]{:S(2)}) collective-permute-start(bf16[512,128]{1,0:T(8,128)(2,1)S(1)} %constant_dynamic-update-slice_fusion), channel_id=1, source_target_pairs={{0,8},{8,16},{16,24},{24,32},{32,40},{40,48},{48,56},{56,64},{64,7... | collective-permute-start | bytes 393224 | tf_op jit(solution)/shard_map/ppermute | solution.py:322
  6.3 23.7 %collective-permute-start.15 = (bf16[512,128]{1,0:T(8,128)(2,1)S(1)}, bf16[512,128]{1,0:T(8,128)(2,1)S(1)}, u32[]{:S(2)}, u32[]{:S(2)}) collective-permute-start(bf16[512,128]{1,0:T(8,128)(2,1)S(1)} %constant_dynamic-update-slice_fusion), channel_id=1, source_target_pairs={{8,0},{16,8},{24,16},{32,24},{40,32},{48,40},{0,120},{9,1},{17,9},... | collective-permute-start | bytes 393224 | tf_op jit(solution)/shard_map/ppermute | solution.py:322
  27.2 8.4 %collective-permute-start.8 = (bf16[512,128]{1,0:T(8,128)(2,1)S(1)}, bf16[512,128]{1,0:T(8,128)(2,1)S(1)}, u32[]{:S(2)}, u32[]{:S(2)}) collective-permute-start(bf16[512,128]{1,0:T(8,128)(2,1)S(1)} %collective-permute-done.7.f_ref), channel_id=1, source_target_pairs={{8,16},{16,24},{24,32},{32,40},{40,48},{48,56},{56,64},{64,72},{72... | collective-permute-start | bytes 393224 | tf_op jit(solution)/shard_map/ppermute | solution.py:322
  30.0 8.1 %collective-permute-start.16 = (bf16[512,128]{1,0:T(8,128)(2,1)S(1)}, bf16[512,128]{1,0:T(8,128)(2,1)S(1)}, u32[]{:S(2)}, u32[]{:S(2)}) collective-permute-start(bf16[512,128]{1,0:T(8,128)(2,1)S(1)} %collective-permute-done.15.b_ref), channel_id=1, source_target_pairs={{8,0},{16,8},{24,16},{32,24},{40,32},{120,112},{0,120},{9,1},{17,9... | collective-permute-start | bytes 393224 | tf_op jit(solution)/shard_map/ppermute | solution.py:322
  35.6 8.1 %collective-permute-start.9 = (bf16[512,128]{1,0:T(8,128)(2,1)S(1)}, bf16[512,128]{1,0:T(8,128)(2,1)S(1)}, u32[]{:S(2)}, u32[]{:S(2)}) collective-permute-start(bf16[512,128]{1,0:T(8,128)(2,1)S(1)} %collective-permute-done.8.f_ref), channel_id=1, source_target_pairs={{16,24},{24,32},{32,40},{40,48},{48,56},{56,64},{64,72},{72,80},{8... | collective-permute-start | bytes 393224 | tf_op jit(solution)/shard_map/ppermute | solution.py:322
  38.1 8.1 %collective-permute-start.17 = (bf16[512,128]{1,0:T(8,128)(2,1)S(1)}, bf16[512,128]{1,0:T(8,128)(2,1)S(1)}, u32[]{:S(2)}, u32[]{:S(2)}) collective-permute-start(bf16[512,128]{1,0:T(8,128)(2,1)S(1)} %collective-permute-done.16.b_ref), channel_id=1, source_target_pairs={{8,0},{16,8},{24,16},{32,24},{112,104},{120,112},{0,120},{9,1},{17... | collective-permute-start | bytes 393224 | tf_op jit(solution)/shard_map/ppermute | solution.py:322
  43.7 8.1 %collective-permute-start.10 = (bf16[512,128]{1,0:T(8,128)(2,1)S(1)}, bf16[512,128]{1,0:T(8,128)(2,1)S(1)}, u32[]{:S(2)}, u32[]{:S(2)}) collective-permute-start(bf16[512,128]{1,0:T(8,128)(2,1)S(1)} %collective-permute-done.9.f_ref), channel_id=1, source_target_pairs={{24,32},{32,40},{40,48},{48,56},{56,64},{64,72},{72,80},{80,88},{8... | collective-permute-start | bytes 393224 | tf_op jit(solution)/shard_map/ppermute | solution.py:322
  46.2 10.1 %collective-permute-start.18 = (bf16[512,128]{1,0:T(8,128)(2,1)S(1)}, bf16[512,128]{1,0:T(8,128)(2,1)S(1)}, u32[]{:S(2)}, u32[]{:S(2)}) collective-permute-start(bf16[512,128]{1,0:T(8,128)(2,1)S(1)} %collective-permute-done.17.b_ref), channel_id=1, source_target_pairs={{8,0},{16,8},{24,16},{104,96},{112,104},{120,112},{0,120},{9,1},{1... | collective-permute-start | bytes 393224 | tf_op jit(solution)/shard_map/ppermute | solution.py:322
  51.8 9.8 %collective-permute-start.11 = (bf16[512,128]{1,0:T(8,128)(2,1)S(1)}, bf16[512,128]{1,0:T(8,128)(2,1)S(1)}, u32[]{:S(2)}, u32[]{:S(2)}) collective-permute-start(bf16[512,128]{1,0:T(8,128)(2,1)S(1)} %collective-permute-done.10.f_ref), channel_id=1, source_target_pairs={{32,40},{40,48},{48,56},{56,64},{64,72},{72,80},{80,88},{88,96},{9... | collective-permute-start | bytes 393224 | tf_op jit(solution)/shard_map/ppermute | solution.py:322
  52.5 1.0 copy-start
  53.6 1.0 copy-start.2
  56.2 6.1 %collective-permute-start = (bf16[544,128]{1,0:T(8,128)(2,1)S(1)}, bf16[544,128]{1,0:T(8,128)(2,1)S(1)}, u32[]{:S(2)}, u32[]{:S(2)}) collective-permute-start(bf16[544,128]{1,0:T(8,128)(2,1)S(1)} %get-tuple-element.53), channel_id=1, source_target_pairs={{0,8},{8,0},{16,24},{24,16},{32,40},{40,32},{48,56},{56,48},{64,72... | collective-permute-start | bytes 417800 | tf_op jit(solution)/shard_map/ppermute | solution.py:322
  56.4 29.0 %collective-permute-start.19 = (bf16[512,128]{1,0:T(8,128)(2,1)S(1)}, bf16[512,128]{1,0:T(8,128)(2,1)S(1)}, u32[]{:S(2)}, u32[]{:S(2)}) collective-permute-start(bf16[512,128]{1,0:T(8,128)(2,1)S(1)} %collective-permute-done.18.b_ref), channel_id=1, source_target_pairs={{8,0},{16,8},{96,88},{104,96},{112,104},{120,112},{0,120},{9,1},{1... | collective-permute-start | bytes 393224 | tf_op jit(solution)/shard_map/ppermute | solution.py:322
  61.6 25.7 %collective-permute-start.12 = (bf16[512,128]{1,0:T(8,128)(2,1)S(1)}, bf16[512,128]{1,0:T(8,128)(2,1)S(1)}, u32[]{:S(2)}, u32[]{:S(2)}) collective-permute-start(bf16[512,128]{1,0:T(8,128)(2,1)S(1)} %collective-permute-done.11.f_ref), channel_id=1, source_target_pairs={{40,48},{48,56},{56,64},{64,72},{72,80},{80,88},{88,96},{96,104},{... | collective-permute-start | bytes 393224 | tf_op jit(solution)/shard_map/ppermute | solution.py:322
  62.3 47.3 %copy-start.5 = (bf16[256,1024]{1,0:T(8,128)(2,1)S(1)}, bf16[256,1024]{1,0:T(8,128)(2,1)}, u32[]{:S(2)}) copy-start(bf16[256,1024]{1,0:T(8,128)(2,1)} %q_ref.5) | copy-start | bytes 1572868
  62.4 5.4 %collective-permute-start.1 = (bf16[288,128]{1,0:T(8,128)(2,1)S(1)}, bf16[288,128]{1,0:T(8,128)(2,1)S(1)}, u32[]{:S(2)}, u32[]{:S(2)}) collective-permute-start(bf16[288,128]{1,0:T(8,128)(2,1)S(1)} %get-tuple-element.56), channel_id=1, source_target_pairs={{0,16},{8,24},{16,0},{24,8},{32,48},{40,56},{48,32},{56,40},{64,80... | collective-permute-start | bytes 221192 | tf_op jit(solution)/shard_map/ppermute | solution.py:322
  67.8 41.8 %copy-start.6 = (bf16[256,128]{1,0:T(8,128)(2,1)S(1)}, bf16[256,128]{1,0:T(8,128)(2,1)}, u32[]{:S(2)}) copy-start(bf16[256,128]{1,0:T(8,128)(2,1)} %k_ref.3) | copy-start | bytes 196612
  67.8 8.5 %collective-permute-start.2 = (bf16[160,128]{1,0:T(8,128)(2,1)S(1)}, bf16[160,128]{1,0:T(8,128)(2,1)S(1)}, u32[]{:S(2)}, u32[]{:S(2)}) collective-permute-start(bf16[160,128]{1,0:T(8,128)(2,1)S(1)} %get-tuple-element.59), channel_id=1, source_target_pairs={{0,32},{8,40},{16,48},{24,56},{32,0},{40,8},{48,16},{56,24},{64,96... | collective-permute-start | bytes 122888 | tf_op jit(solution)/shard_map/ppermute | solution.py:322
  76.4 34.7 %copy-start.4 = (bf16[256,1024]{1,0:T(8,128)(2,1)S(1)}, bf16[256,1024]{1,0:T(8,128)(2,1)}, u32[]{:S(2)}) copy-start(bf16[256,1024]{1,0:T(8,128)(2,1)} %q_ref.4) | copy-start | bytes 1572868
  77.0 11.0 %collective-permute-start.3 = (bf16[128,128]{1,0:T(8,128)(2,1)S(1)}, bf16[128,128]{1,0:T(8,128)(2,1)S(1)}, u32[]{:S(2)}, u32[]{:S(2)}) collective-permute-start(bf16[128,128]{1,0:T(8,128)(2,1)S(1)} %get-tuple-element.62), channel_id=1, source_target_pairs={{0,96},{8,104},{16,112},{24,120},{32,64},{40,72},{48,80},{56,88},{... | collective-permute-start | bytes 98312 | tf_op jit(solution)/shard_map/ppermute | solution.py:322
  85.3 18.3 %collective-permute-start.20 = (bf16[512,128]{1,0:T(8,128)(2,1)S(1)}, bf16[512,128]{1,0:T(8,128)(2,1)S(1)}, u32[]{:S(2)}, u32[]{:S(2)}) collective-permute-start(bf16[512,128]{1,0:T(8,128)(2,1)S(1)} %collective-permute-done.19.b_ref), channel_id=1, source_target_pairs={{8,0},{88,80},{96,88},{104,96},{112,104},{120,112},{0,120},{9,1},{... | collective-permute-start | bytes 393224 | tf_op jit(solution)/shard_map/ppermute | solution.py:322
  87.3 21.6 %collective-permute-start.13 = (bf16[512,128]{1,0:T(8,128)(2,1)S(1)}, bf16[512,128]{1,0:T(8,128)(2,1)S(1)}, u32[]{:S(2)}, u32[]{:S(2)}) collective-permute-start(bf16[512,128]{1,0:T(8,128)(2,1)S(1)} %collective-permute-done.12.f_ref), channel_id=1, source_target_pairs={{48,56},{56,64},{64,72},{72,80},{80,88},{88,96},{96,104},{104,112}... | collective-permute-start | bytes 393224 | tf_op jit(solution)/shard_map/ppermute | solution.py:322
  88.0 8.6 %collective-permute-start.4 = (bf16[128,128]{1,0:T(8,128)(2,1)S(1)}, bf16[128,128]{1,0:T(8,128)(2,1)S(1)}, u32[]{:S(2)}, u32[]{:S(2)}) collective-permute-start(bf16[128,128]{1,0:T(8,128)(2,1)S(1)} %get-tuple-element.66), channel_id=1, source_target_pairs={{0,32},{8,40},{16,48},{24,56},{32,0},{40,8},{48,16},{56,24},{64,96... | collective-permute-start | bytes 98312 | tf_op jit(solution)/shard_map/ppermute | solution.py:322
  96.7 5.3 %collective-permute-start.5 = (bf16[256,128]{1,0:T(8,128)(2,1)S(1)}, bf16[256,128]{1,0:T(8,128)(2,1)S(1)}, u32[]{:S(2)}, u32[]{:S(2)}) collective-permute-start(bf16[256,128]{1,0:T(8,128)(2,1)S(1)} %get-tuple-element.70), channel_id=1, source_target_pairs={{0,16},{8,24},{16,0},{24,8},{32,48},{40,56},{48,32},{56,40},{64,80... | collective-permute-start | bytes 196616 | tf_op jit(solution)/shard_map/ppermute | solution.py:322
  102.0 9.1 %copy-start.1 = (bf16[256,1024]{1,0:T(8,128)(2,1)S(1)}, bf16[256,1024]{1,0:T(8,128)(2,1)}, u32[]{:S(2)}) copy-start(bf16[256,1024]{1,0:T(8,128)(2,1)} %k_ref.2) | copy-start | bytes 1572868
  102.0 9.1 %copy-start.3 = (bf16[256,1024]{1,0:T(8,128)(2,1)S(1)}, bf16[256,1024]{1,0:T(8,128)(2,1)}, u32[]{:S(2)}) copy-start(bf16[256,1024]{1,0:T(8,128)(2,1)} %v_ref.2) | copy-start | bytes 1572868
  102.0 12.5 %collective-permute-start.6 = (bf16[512,128]{1,0:T(8,128)(2,1)S(1)}, bf16[512,128]{1,0:T(8,128)(2,1)S(1)}, u32[]{:S(2)}, u32[]{:S(2)}) collective-permute-start(bf16[512,128]{1,0:T(8,128)(2,1)S(1)} %get-tuple-element.74), channel_id=1, source_target_pairs={{0,8},{8,0},{16,24},{24,16},{32,40},{40,32},{48,56},{56,48},{64,72... | collective-permute-start | bytes 393224 | tf_op jit(solution)/shard_map/ppermute | solution.py:322
  103.6 15.0 %collective-permute-start.21 = (bf16[512,128]{1,0:T(8,128)(2,1)S(1)}, bf16[512,128]{1,0:T(8,128)(2,1)S(1)}, u32[]{:S(2)}, u32[]{:S(2)}) collective-permute-start(bf16[512,128]{1,0:T(8,128)(2,1)S(1)} %collective-permute-done.20.b_ref), channel_id=1, source_target_pairs={{80,72},{88,80},{96,88},{104,96},{112,104},{120,112},{0,120},{81,7... | collective-permute-start | bytes 393224 | tf_op jit(solution)/shard_map/ppermute | solution.py:322
  108.9 10.3 %collective-permute-start.14 = (bf16[512,128]{1,0:T(8,128)(2,1)S(1)}, bf16[512,128]{1,0:T(8,128)(2,1)S(1)}, u32[]{:S(2)}, u32[]{:S(2)}) collective-permute-start(bf16[512,128]{1,0:T(8,128)(2,1)S(1)} %collective-permute-done.13.f_ref), channel_id=1, source_target_pairs={{56,64},{64,72},{72,80},{80,88},{88,96},{96,104},{104,112},{112,12... | collective-permute-start | bytes 393224 | tf_op jit(solution)/shard_map/ppermute | solution.py:322
  (1 other events, 0.8 us)

commit v2 on v1

--- a/solution.py
+++ b/solution.py
@@ -15,11 +15,10 @@
 E_ROWS = 32
 VMEM = pl.BlockSpec(memory_space=pltpu.VMEM)
 ANY = pl.BlockSpec(memory_space=pltpu.HBM)
-SMEM = pl.BlockSpec(memory_space=pltpu.SMEM)
-
-
-def call(kernel, out_shape, ins, aliases=None, flops=2_000_000, scratch=()):
-    specs = [ANY if s is None else SMEM if s else VMEM for s, unused in ins]
+
+
+def call(kernel, out_shape, ins, aliases=None, flops=2_000_000, scratch=(), limit=48 * 1024 * 1024):
+    specs = [ANY if s is None else VMEM for s, unused in ins]
     arrays = [a for unused, a in ins]
     outs = [jax.ShapeDtypeStruct(s, d) for s, d in out_shape]
     return pl.pallas_call(
@@ -29,7 +28,7 @@
         out_specs=[VMEM] * len(outs),
         scratch_shapes=list(scratch),
         input_output_aliases=aliases or {},
-        compiler_params=pltpu.CompilerParams(vmem_limit_bytes=48 * 1024 * 1024),
+        compiler_params=pltpu.CompilerParams(vmem_limit_bytes=limit),
         cost_estimate=pl.CostEstimate(flops=flops, bytes_accessed=1 << 20, transcendentals=0),
     )(*arrays)
 
@@ -65,7 +64,9 @@
     return rows[0:8] + rows[8:16] + rows[16:24]
 
 
-def prep_kernel(len_ref, k_hbm, v_hbm, dec_ref, msg_ref, kept_ref, logs_ref, c_ref, ct_ref, states, k_ref, v_ref, sems):
+def prep_kernel(
+    len_ref, k_hbm, v_hbm, dec_ref, msg_ref, kept_ref, logs_ref, c_ref, ct_ref, bias_ref, live_ref, states, k_ref, v_ref, sems
+):
     k_copy = pltpu.make_async_copy(k_hbm, k_ref, sems.at[0])
     v_copy = pltpu.make_async_copy(v_hbm, v_ref, sems.at[1])
     k_copy.start()
@@ -75,7 +76,17 @@
     heads = dec_ref.shape[0]
     width = k_ref.shape[1] // heads
     half = heads // 2
-    length = len_ref[i]
+    blocks = len_ref.shape[1]
+    lengths = len_ref[...]
+    at = lax.broadcasted_iota(jnp.int32, (1, blocks), 1)
+    length = jnp.sum(jnp.where(at == i, lengths, 0), axis=1, keepdims=True)
+    live_ref[...] = (lax.broadcasted_iota(jnp.int32, (rows, 128), 0) < length).astype(F32)
+    square = (blocks, blocks)
+    diagonal = lax.broadcasted_iota(jnp.int32, square, 0) == lax.broadcasted_iota(jnp.int32, square, 1)
+    column = jnp.sum(jnp.where(diagonal, lengths, 0), axis=1, keepdims=True)
+    dead = lax.broadcasted_iota(jnp.int32, (blocks, rows), 1) >= column
+    bias_ref[0:blocks, :] = jnp.where(dead, NEG, 0.0)
+    bias_ref[blocks:, :] = jnp.full((8, rows), NEG, F32)
     lane = lax.broadcasted_iota(jnp.int32, (heads, rows), 1)
     live = lane < length
     masked = jnp.where(live, dec_ref[...], 0.0)
@@ -104,7 +115,7 @@
     put_logs(msg_ref, half * width, logs)
 
 
-def up_kernel(level, recv_ref, kept_ref, logs_ref, msg_ref, next_ref, low_ref, lowlog_ref, sum_ref):
+def up_kernel(level, recv_ref, kept_ref, logs_ref, msg_ref, low_ref, lowlog_ref, next_ref=None, sum_ref=None):
     i = lax.axis_index("seq")
     count, width = kept_ref.shape[0], kept_ref.shape[1]
     upper = bit(i, level) == 1
@@ -112,7 +123,6 @@
     other = get_logs(recv_ref, count * width)
     low_logs = jnp.where(upper, other, own)
     lowlog_ref[...] = low_logs
-    sum_ref[...] = own + other
     grown = jnp.exp(jnp.where(upper, own, other))
     start = first_head(i, level)
     which = lax.broadcasted_iota(jnp.int32, grown.shape, 0)
@@ -129,8 +139,8 @@
         totals.append(factor * low + high)
     if count == 1:
         msg_ref[...] = totals[0].astype(BF16)
-        next_ref[...] = jnp.zeros_like(next_ref)
         return
+    sum_ref[...] = own + other
     first = keep == 0
     for h in range(half):
         next_ref[h] = jnp.where(first, totals[h], totals[half + h])
@@ -166,16 +176,15 @@
         msg_ref[h * width : (h + 1) * width, :] = jnp.where(upper, low, high).astype(BF16)
 
 
-def inside_kernel(len_ref, q_ref, k_ref, v_ref, c_ref, ct_ref, out_ref):
+def inside_kernel(bias_ref, q_ref, k_ref, v_ref, c_ref, ct_ref, out_ref):
     i = lax.axis_index("seq")
     rows = q_ref.shape[0]
     heads = c_ref.shape[0]
     width = q_ref.shape[1] // heads
     scale = width ** (-0.5)
-    length = len_ref[i]
     row = lax.broadcasted_iota(jnp.int32, (rows, rows), 0)
     col = lax.broadcasted_iota(jnp.int32, (rows, rows), 1)
-    allowed = (col <= row) & (col < length)
+    allowed = (col <= row) & (bias_ref[pl.ds(i, 1), :] == 0.0)
     running = c_ref[...]
     running_t = ct_ref[...]
     for h in range(heads):
@@ -189,14 +198,13 @@
         out_ref[:, at] = jnp.dot(intra, v_ref[:, at], preferred_element_type=F32)
 
 
-def light_kernel(len_ref, q_ref, inside_ref, held_ref, recv_ref, ct_ref, gain_ref, out_ref):
-    i = lax.axis_index("seq")
-    rows = q_ref.shape[0]
+def light_kernel(live_ref, q_ref, inside_ref, held_ref, recv_ref, ct_ref, gain_ref, out_ref):
+    i = lax.axis_index("seq")
     half, width = held_ref.shape[0], held_ref.shape[1]
     scale = width ** (-0.5)
     first = keep_bit(i, 0) == 0
-    live = lax.broadcasted_iota(jnp.int32, (rows, 1), 0) < len_ref[i]
-    grown = jnp.exp(ct_ref[...])
+    live = live_ref[...] > 0.0
+    grown = jnp.exp(ct_ref[...]) * scale
     for h in range(2 * half):
         at = slice(h * width, (h + 1) * width)
         mod = h % half
@@ -204,7 +212,7 @@
         got = recv_ref[mod * width : (mod + 1) * width, :]
         pick_held = first if h < half else jnp.logical_not(first)
         entering = jnp.where(pick_held, held.astype(F32), got.astype(F32)).astype(BF16)
-        across = jnp.dot(q_ref[:, at], entering, preferred_element_type=F32) * scale
+        across = jnp.dot(q_ref[:, at], entering, preferred_element_type=F32)
         combined = inside_ref[:, at] + across * grown[:, h : h + 1]
         mean = jnp.mean(combined * combined, axis=-1, keepdims=True)
         normed = combined * lax.rsqrt(mean + 1e-06) * gain_ref[:, at]
@@ -215,7 +223,7 @@
     return jnp.where(lax.broadcasted_iota(jnp.int32, (rows, 128), 1) == 0, 1.0, 0.0).astype(BF16)
 
 
-def own_kernel(len_ref, q_ref, k_ref, v_ref, q2_ref, m_ref, l_ref, acc_ref):
+def own_kernel(bias_ref, q_ref, k_ref, v_ref, q2_ref, m_ref, l_ref, acc_ref):
     i = lax.axis_index("seq")
     rows, width = k_ref.shape
     heads = q_ref.shape[1] // width
@@ -225,7 +233,7 @@
         q2_ref[h * rows : (h + 1) * rows, :width] = q_ref[:, h * width : (h + 1) * width]
     row = lax.broadcasted_iota(jnp.int32, (rows, rows), 0)
     col = lax.broadcasted_iota(jnp.int32, (rows, rows), 1)
-    allowed = (col <= row) & (col < len_ref[i])
+    allowed = (col <= row) & (bias_ref[pl.ds(i, 1), :] == 0.0)
     scores = jnp.dot(q2_ref[:, :width], k_ref[...].T, preferred_element_type=F32)
     scores = jnp.where(allowed[None], scores.reshape(heads, rows, rows), NEG).reshape(heads * rows, rows)
     peak = jnp.broadcast_to(jnp.max(scores, axis=-1, keepdims=True), (heads * rows, 128))
@@ -237,12 +245,11 @@
     )
 
 
-def attend(q2_ref, blocks, lengths, old_ref):
+def attend(q2_ref, blocks, biases, old_ref):
     rows, width = blocks[0].shape[0] // 2, blocks[0].shape[1]
     factor = width ** (-0.5) * LOG2E
     row = lax.broadcasted_iota(jnp.int32, (128, rows), 0)
-    col = lax.broadcasted_iota(jnp.int32, (128, rows), 1)
-    biases = [jnp.where((row == 0) & (col >= n), NEG, 0.0).astype(BF16) for n in lengths]
+    biases = [jnp.where(row == 0, bias, 0.0).astype(BF16) for bias in biases]
     keys_t = jnp.concatenate([ref[0:rows, :].T for ref in blocks], axis=1)
     keys_t = jnp.concatenate([keys_t, jnp.concatenate(biases, axis=1)], axis=0)
     values = jnp.concatenate([ref[rows : 2 * rows, :] for ref in blocks], axis=0)
@@ -256,27 +263,27 @@
     return new, jnp.exp2((old - new) * factor), sum(probs[1:], probs[0]), summed
 
 
-def step_kernel(step, count, len_ref, q2_ref, f_ref, b_ref, unused_m, unused_l, unused_acc, m_ref, l_ref, acc_ref):
+def step_kernel(step, count, bias_ref, q2_ref, f_ref, b_ref, unused_m, unused_l, unused_acc, m_ref, l_ref, acc_ref):
     i = lax.axis_index("seq")
 
     @pl.when(i >= step)
     def run():
         wrapped = i + step - count
-        lengths = [
-            len_ref[jnp.maximum(i - step, 0)],
-            jnp.where(wrapped >= 0, len_ref[jnp.maximum(wrapped, 0)], 0),
+        biases = [
+            bias_ref[pl.ds(i - step, 1), :],
+            bias_ref[pl.ds(jnp.where(wrapped >= 0, wrapped, count), 1), :],
         ]
-        new, shrink, total, summed = attend(q2_ref, [f_ref, b_ref], lengths, m_ref)
+        new, shrink, total, summed = attend(q2_ref, [f_ref, b_ref], biases, m_ref)
         m_ref[...] = new
         l_ref[...] = shrink * l_ref[...] + total
         acc_ref[...] = shrink * acc_ref[...] + summed
 
 
-def last_kernel(step, len_ref, q2_ref, f_ref, m_ref, l_ref, acc_ref, out_ref):
+def last_kernel(step, bias_ref, live_ref, q2_ref, f_ref, m_ref, l_ref, acc_ref, out_ref):
     i = lax.axis_index("seq")
     rows, width = f_ref.shape[0] // 2, f_ref.shape[1]
     heads = q2_ref.shape[0] // rows
-    live = lax.broadcasted_iota(jnp.int32, (rows, 1), 0) < len_ref[i]
+    live = live_ref[...] > 0.0
 
     def finish(total, summed):
         result = summed / jnp.sum(total, axis=-1, keepdims=True)
@@ -286,7 +293,7 @@
 
     @pl.when(i >= step)
     def run():
-        _, shrink, total, summed = attend(q2_ref, [f_ref], [len_ref[jnp.maximum(i - step, 0)]], m_ref)
+        _, shrink, total, summed = attend(q2_ref, [f_ref], [bias_ref[pl.ds(i - step, 1), :]], m_ref)
         finish(shrink * l_ref[...] + total, shrink * acc_ref[...] + summed)
 
     @pl.when(i < step)
@@ -310,13 +317,12 @@
     width = light_queries.shape[1] // heads
     count = lax.axis_size("seq")
     half = heads // 2
-    back = count // 2 - 1
-
-    def forward(step):
-        return [(i, i + 1) for i in range(step - 1, count - 1)]
-
-    def backward(step):
-        return [((j + 1) % count, j) for j in range(count) if j + step < back or j + step >= count]
+
+    def forward():
+        return [(i, (i + 1) % count) for i in range(count)]
+
+    def backward():
+        return [((j + 1) % count, j) for j in range(count)]
 
     def send(x, pairs):
         return lax.ppermute(x, "seq", pairs)
@@ -324,12 +330,11 @@
     def exchange(x, distance):
         return send(x, [(i, i ^ distance) for i in range(count)])
 
-    lens = (True, lengths)
     own_kv = jnp.concatenate([soft_keys, soft_values], axis=0)
-    f = send(own_kv, forward(1))
-    b = send(own_kv, backward(1))
-
-    msg, kept, logs, running, running_t = call(
+    f = send(own_kv, forward())
+    b = send(own_kv, backward())
+
+    msg, kept, logs, running, running_t, bias, live = call(
         prep_kernel,
         [
             ((half * width + E_ROWS, width), BF16),
@@ -337,14 +342,17 @@
             ((heads, 128), F32),
             ((heads, rows), F32),
             ((rows, heads), F32),
+            ((count + 8, rows), F32),
+            ((rows, 128), F32),
         ],
-        [lens, (None, light_keys), (None, light_values), (False, decay_log.T)],
+        [(False, lengths.reshape(1, count)), (None, pltpu.with_memory_space_constraint(light_keys, pltpu.HBM)), (None, pltpu.with_memory_space_constraint(light_values, pltpu.HBM)), (False, decay_log.T)],
         scratch=[
             pltpu.VMEM((heads, width, width), F32),
             pltpu.VMEM((rows, heads * width), BF16),
             pltpu.VMEM((rows, heads * width), BF16),
             pltpu.SemaphoreType.DMA((2,)),
         ],
+        limit=48 * 1024 * 1024,
     )
     saved = []
     n = half
@@ -352,19 +360,16 @@
         recv = exchange(msg, 1 << level)
         m = max(n // 2, 1)
         tail = E_ROWS if n > 1 else 0
-        msg, nxt, low, low_logs, new_logs = call(
+        onward = [((m, width, width), F32), ((heads, 128), F32)] if n > 1 else []
+        msg, low, low_logs, *rest = call(
             partial(up_kernel, level),
-            [
-                ((m * width + tail, width), BF16),
-                ((m, width, width), F32),
-                ((n, width, width), F32),
-                ((heads, 128), F32),
-                ((heads, 128), F32),
-            ],
+            [((m * width + tail, width), BF16), ((n, width, width), F32), ((heads, 128), F32)] + onward,
             [(False, recv), (False, kept), (False, logs)],
         )
         saved.append((low, low_logs))
-        kept, logs, n = (nxt, new_logs, n // 2)
+        n //= 2
+        if n:
+            kept, logs = rest
     recv = send(msg, [(i, (i + 4 if i >= 4 else i - 4) % count) for i in range(count // 2)])
     held = None
     for level in (2, 1, 0):
@@ -381,7 +386,7 @@
         inside_kernel,
         [((rows, heads * width), F32)],
         [
-            lens,
+            (False, bias),
             (False, light_queries),
             (False, light_keys),
             (False, light_values),
@@ -393,7 +398,7 @@
         light_kernel,
         [((rows, heads * width), BF16)],
         [
-            lens,
+            (False, live),
             (False, light_queries),
             (False, inside),
             (False, held),
@@ -408,22 +413,22 @@
     q2, *state = call(
         own_kernel,
         [((soft_rows, width + 128), BF16), stat, stat, stat],
-        [lens, (False, soft_queries), (False, soft_keys), (False, soft_values)],
+        [(False, bias), (False, soft_queries), (False, soft_keys), (False, soft_values)],
     )
     for step in range(1, count // 2):
-        nf = send(f, forward(step + 1))
-        nb = send(b, backward(step + 1)) if step + 1 < count // 2 else None
+        nf = send(f, forward())
+        nb = send(b, backward()) if step + 1 < count // 2 else None
         state = call(
             partial(step_kernel, step, count),
             [stat, stat, stat],
-            [lens, (False, q2), (False, f), (False, b)] + [(False, s) for s in state],
+            [(False, bias), (False, q2), (False, f), (False, b)] + [(False, s) for s in state],
             aliases={4: 0, 5: 1, 6: 2},
         )
         f, b = nf, nb
     (soft_out,) = call(
         partial(last_kernel, count // 2),
         [((rows, soft_queries.shape[1]), BF16)],
-        [lens, (False, q2), (False, f)] + [(False, s) for s in state],
+        [(False, bias), (False, live), (False, q2), (False, f)] + [(False, s) for s in state],
     )
     return (light_out, soft_out)
 

time: 122 us -> 105 us (0.86)
  starting transfers between devices: 72.2 us -> 58 us
  Pallas kernels: 13.7 us -> 7.29 us
  waiting for transfers between devices: 30.9 us -> 36.5 us
    ppermute x22, starting transfers between devices: 72.2 us -> 58 us  [send(): return lax.ppermute(x, 'seq', pairs)]
    pallas_call x18, Pallas kernels: 13.7 us -> 7.29 us  [call(): pl.pallas_call(kernel, out_shape=outs, in_specs=specs, out_specs=[VMEM] *...]
    ppermute x22, waiting for transfers between devices: 30.9 us -> 36.5 us  [send(): return lax.ppermute(x, 'seq', pairs)]
    unnamed x23 -> x19, local copies, waits for them, and re-layouts: 3 us -> 2.23 us
  transfers between devices with their start and end apart: 22 -> 22, of which waited for: 7 -> 11; matrix products, arithmetic and copies ran while one was open for 0% -> 0% of each run, Pallas kernels for 10% -> 6%
where the time goes in v2:
time: 105 us
  starting transfers between devices  58 us (55%)
  waiting for transfers between devices  36.5 us (35%)
  Pallas kernels  7.29 us (7%)
  local copies, waits for them, and re-layouts  2.24 us (2%)
    ppermute x22, starting transfers between devices, send(): return lax.ppermute(x, 'seq', pairs)  58 us
    ppermute x22, waiting for transfers between devices, send(): return lax.ppermute(x, 'seq', pairs)  36.5 us
    pallas_call x18, Pallas kernels, call(): pl.pallas_call(kernel, out_shape=outs, in_specs=specs, out_specs=[VMEM] *...  7.29 us
    unnamed x19, local copies, waits for them, and re-layouts  2.23 us
  transfers between devices with their start and end apart: 22, of which 11 were waited for; matrix products, arithmetic and copies ran while one was open for 0% of the time, Pallas kernels for 6%

profile of v2, /device:TPU:36, one launch (start us, length us, event | category | flops | bytes accessed | tf_op | source)
XLA Modules:
  0.0 104.9 jit_solution(17202787375765481130)
XLA Ops:
  0.6 0.9 constant_dynamic-update-slice_fusion.1
  1.5 2.9 %collective-permute-start.7 = (bf16[512,128]{1,0:T(8,128)(2,1)S(1)}, bf16[512,128]{1,0:T(8,128)(2,1)S(1)}, u32[]{:S(2)}, u32[]{:S(2)}) collective-permute-start(bf16[512,128]{1,0:T(8,128)(2,1)S(1)} %constant_dynamic-update-slice_fusion), channel_id=1, source_target_pairs={{0,8},{8,16},{16,24},{24,32},{32,40},{40,48},{48,56},{56,64},{64,7... | collective-permute-start | bytes 393224 | tf_op jit(solution)/shard_map/ppermute | solution.py:328
  4.4 19.7 %collective-permute-start.15 = (bf16[512,128]{1,0:T(8,128)(2,1)S(1)}, bf16[512,128]{1,0:T(8,128)(2,1)S(1)}, u32[]{:S(2)}, u32[]{:S(2)}) collective-permute-start(bf16[512,128]{1,0:T(8,128)(2,1)S(1)} %constant_dynamic-update-slice_fusion), channel_id=1, source_target_pairs={{8,0},{16,8},{24,16},{32,24},{40,32},{48,40},{56,48},{64,56},{72,6... | collective-permute-start | bytes 393224 | tf_op jit(solution)/shard_map/ppermute | solution.py:328
  24.2 3.4 %collective-permute-done.7.f_ref = bf16[512,128]{1,0:T(8,128)(2,1)S(1)} collective-permute-done((bf16[512,128]{1,0:T(8,128)(2,1)S(1)}, bf16[512,128]{1,0:T(8,128)(2,1)S(1)}, u32[]{:S(2)}, u32[]{:S(2)}) %collective-permute-start.7) | collective-permute-done | bytes 131104 | tf_op jit(solution)/shard_map/ppermute | solution.py:328
  27.6 3.2 %collective-permute-start.16 = (bf16[512,128]{1,0:T(8,128)(2,1)S(1)}, bf16[512,128]{1,0:T(8,128)(2,1)S(1)}, u32[]{:S(2)}, u32[]{:S(2)}) collective-permute-start(bf16[512,128]{1,0:T(8,128)(2,1)S(1)} %collective-permute-done.15.b_ref), channel_id=1, source_target_pairs={{8,0},{16,8},{24,16},{32,24},{40,32},{48,40},{56,48},{64,56},{72,6... | collective-permute-start | bytes 393224 | tf_op jit(solution)/shard_map/ppermute | solution.py:328
  30.9 2.9 %collective-permute-done.8.f_ref = bf16[512,128]{1,0:T(8,128)(2,1)S(1)} collective-permute-done((bf16[512,128]{1,0:T(8,128)(2,1)S(1)}, bf16[512,128]{1,0:T(8,128)(2,1)S(1)}, u32[]{:S(2)}, u32[]{:S(2)}) %collective-permute-start.8) | collective-permute-done | bytes 131104 | tf_op jit(solution)/shard_map/ppermute | solution.py:328
  33.8 3.2 %collective-permute-start.17 = (bf16[512,128]{1,0:T(8,128)(2,1)S(1)}, bf16[512,128]{1,0:T(8,128)(2,1)S(1)}, u32[]{:S(2)}, u32[]{:S(2)}) collective-permute-start(bf16[512,128]{1,0:T(8,128)(2,1)S(1)} %collective-permute-done.16.b_ref), channel_id=1, source_target_pairs={{8,0},{16,8},{24,16},{32,24},{40,32},{48,40},{56,48},{64,56},{72,6... | collective-permute-start | bytes 393224 | tf_op jit(solution)/shard_map/ppermute | solution.py:328
  37.0 2.9 %collective-permute-done.9.f_ref = bf16[512,128]{1,0:T(8,128)(2,1)S(1)} collective-permute-done((bf16[512,128]{1,0:T(8,128)(2,1)S(1)}, bf16[512,128]{1,0:T(8,128)(2,1)S(1)}, u32[]{:S(2)}, u32[]{:S(2)}) %collective-permute-start.9) | collective-permute-done | bytes 131104 | tf_op jit(solution)/shard_map/ppermute | solution.py:328
  40.0 3.2 %collective-permute-start.18 = (bf16[512,128]{1,0:T(8,128)(2,1)S(1)}, bf16[512,128]{1,0:T(8,128)(2,1)S(1)}, u32[]{:S(2)}, u32[]{:S(2)}) collective-permute-start(bf16[512,128]{1,0:T(8,128)(2,1)S(1)} %collective-permute-done.17.b_ref), channel_id=1, source_target_pairs={{8,0},{16,8},{24,16},{32,24},{40,32},{48,40},{56,48},{64,56},{72,6... | collective-permute-start | bytes 393224 | tf_op jit(solution)/shard_map/ppermute | solution.py:328
  43.2 3.3 %collective-permute-done.10.f_ref = bf16[512,128]{1,0:T(8,128)(2,1)S(1)} collective-permute-done((bf16[512,128]{1,0:T(8,128)(2,1)S(1)}, bf16[512,128]{1,0:T(8,128)(2,1)S(1)}, u32[]{:S(2)}, u32[]{:S(2)}) %collective-permute-start.10) | collective-permute-done | bytes 131104 | tf_op jit(solution)/shard_map/ppermute | solution.py:328
  46.5 0.6 copy-done.8
  47.1 2.0 %shard_map.104 = (bf16[544,128]{1,0:T(8,128)(2,1)S(1)}, f32[4,128,128]{2,1,0:T(8,128)S(1)}, f32[8,128]{1,0:T(8,128)S(1)}, f32[8,256]{1,0:T(8,128)S(1)}, f32[256,...) custom-call(s32[1,16]{1,0:T(1,128)S(1)} %bitcast.5, bf16[256,1024]{1,0:T(8,128)(2,1)} %k_ref.2, ...), custom_call_target="tpu_custom_call" | custom-call | flops 2000000 | bytes 1048576 | tf_op jit(solution)/shard_map/pallas_call | solution.py:24
  49.3 3.4 %collective-permute-start.19 = (bf16[512,128]{1,0:T(8,128)(2,1)S(1)}, bf16[512,128]{1,0:T(8,128)(2,1)S(1)}, u32[]{:S(2)}, u32[]{:S(2)}) collective-permute-start(bf16[512,128]{1,0:T(8,128)(2,1)S(1)} %collective-permute-done.18.b_ref), channel_id=1, source_target_pairs={{8,0},{16,8},{24,16},{32,24},{40,32},{48,40},{56,48},{64,56},{72,6... | collective-permute-start | bytes 393224 | tf_op jit(solution)/shard_map/ppermute | solution.py:328
  52.7 1.2 %collective-permute-done.11.f_ref = bf16[512,128]{1,0:T(8,128)(2,1)S(1)} collective-permute-done((bf16[512,128]{1,0:T(8,128)(2,1)S(1)}, bf16[512,128]{1,0:T(8,128)(2,1)S(1)}, u32[]{:S(2)}, u32[]{:S(2)}) %collective-permute-start.11) | collective-permute-done | bytes 131104 | tf_op jit(solution)/shard_map/ppermute | solution.py:328
  53.8 1.3 %collective-permute-done.recv_ref = bf16[544,128]{1,0:T(8,128)(2,1)S(1)} collective-permute-done((bf16[544,128]{1,0:T(8,128)(2,1)S(1)}, bf16[544,128]{1,0:T(8,128)(2,1)S(1)}, u32[]{:S(2)}, u32[]{:S(2)}) %collective-permute-start) | collective-permute-done | bytes 139296 | tf_op jit(solution)/shard_map/ppermute | solution.py:328
  55.3 6.4 %collective-permute-done.1.recv_ref = bf16[288,128]{1,0:T(8,128)(2,1)S(1)} collective-permute-done((bf16[288,128]{1,0:T(8,128)(2,1)S(1)}, bf16[288,128]{1,0:T(8,128)(2,1)S(1)}, u32[]{:S(2)}, u32[]{:S(2)}) %collective-permute-start.1) | collective-permute-done | bytes 73760 | tf_op jit(solution)/shard_map/ppermute | solution.py:328
  61.9 7.9 %collective-permute-done.2.recv_ref = bf16[160,128]{1,0:T(8,128)(2,1)S(1)} collective-permute-done((bf16[160,128]{1,0:T(8,128)(2,1)S(1)}, bf16[160,128]{1,0:T(8,128)(2,1)S(1)}, u32[]{:S(2)}, u32[]{:S(2)}) %collective-permute-start.2) | collective-permute-done | bytes 40992 | tf_op jit(solution)/shard_map/ppermute | solution.py:328
  69.8 3.0 %collective-permute-start.3 = (bf16[128,128]{1,0:T(8,128)(2,1)S(1)}, bf16[128,128]{1,0:T(8,128)(2,1)S(1)}, u32[]{:S(2)}, u32[]{:S(2)}) collective-permute-start(bf16[128,128]{1,0:T(8,128)(2,1)S(1)} %get-tuple-element.66), channel_id=1, source_target_pairs={{0,96},{8,104},{16,112},{24,120},{32,64},{40,72},{48,80},{56,88},{... | collective-permute-start | bytes 98312 | tf_op jit(solution)/shard_map/ppermute | solution.py:328
  72.9 2.0 %collective-permute-start.20 = (bf16[512,128]{1,0:T(8,128)(2,1)S(1)}, bf16[512,128]{1,0:T(8,128)(2,1)S(1)}, u32[]{:S(2)}, u32[]{:S(2)}) collective-permute-start(bf16[512,128]{1,0:T(8,128)(2,1)S(1)} %collective-permute-done.19.b_ref), channel_id=1, source_target_pairs={{8,0},{16,8},{24,16},{32,24},{40,32},{48,40},{56,48},{64,56},{72,6... | collective-permute-start | bytes 393224 | tf_op jit(solution)/shard_map/ppermute | solution.py:328
  74.9 1.0 %collective-permute-start.13 = (bf16[512,128]{1,0:T(8,128)(2,1)S(1)}, bf16[512,128]{1,0:T(8,128)(2,1)S(1)}, u32[]{:S(2)}, u32[]{:S(2)}) collective-permute-start(bf16[512,128]{1,0:T(8,128)(2,1)S(1)} %collective-permute-done.12.f_ref), channel_id=1, source_target_pairs={{0,8},{8,16},{16,24},{24,32},{32,40},{40,48},{48,56},{56,64},{64,7... | collective-permute-start | bytes 393224 | tf_op jit(solution)/shard_map/ppermute | solution.py:328
  76.0 5.6 %collective-permute-start.4 = (bf16[128,128]{1,0:T(8,128)(2,1)S(1)}, bf16[128,128]{1,0:T(8,128)(2,1)S(1)}, u32[]{:S(2)}, u32[]{:S(2)}) collective-permute-start(bf16[128,128]{1,0:T(8,128)(2,1)S(1)} %get-tuple-element.70), channel_id=1, source_target_pairs={{0,32},{8,40},{16,48},{24,56},{32,0},{40,8},{48,16},{56,24},{64,96... | collective-permute-start | bytes 98312 | tf_op jit(solution)/shard_map/ppermute | solution.py:328
  81.7 3.2 %collective-permute-done.4.refs_1_ = bf16[128,128]{1,0:T(8,128)(2,1)S(1)} collective-permute-done((bf16[128,128]{1,0:T(8,128)(2,1)S(1)}, bf16[128,128]{1,0:T(8,128)(2,1)S(1)}, u32[]{:S(2)}, u32[]{:S(2)}) %collective-permute-start.4) | collective-permute-done | bytes 32800 | tf_op jit(solution)/shard_map/ppermute | solution.py:328
  84.9 2.9 %collective-permute-start.5 = (bf16[256,128]{1,0:T(8,128)(2,1)S(1)}, bf16[256,128]{1,0:T(8,128)(2,1)S(1)}, u32[]{:S(2)}, u32[]{:S(2)}) collective-permute-start(bf16[256,128]{1,0:T(8,128)(2,1)S(1)} %get-tuple-element.74), channel_id=1, source_target_pairs={{0,16},{8,24},{16,0},{24,8},{32,48},{40,56},{48,32},{56,40},{64,80... | collective-permute-start | bytes 196616 | tf_op jit(solution)/shard_map/ppermute | solution.py:328
  87.8 2.4 %collective-permute-done.5.refs_1_ = bf16[256,128]{1,0:T(8,128)(2,1)S(1)} collective-permute-done((bf16[256,128]{1,0:T(8,128)(2,1)S(1)}, bf16[256,128]{1,0:T(8,128)(2,1)S(1)}, u32[]{:S(2)}, u32[]{:S(2)}) %collective-permute-start.5) | collective-permute-done | bytes 65568 | tf_op jit(solution)/shard_map/ppermute | solution.py:328
  90.3 3.3 %collective-permute-start.6 = (bf16[512,128]{1,0:T(8,128)(2,1)S(1)}, bf16[512,128]{1,0:T(8,128)(2,1)S(1)}, u32[]{:S(2)}, u32[]{:S(2)}) collective-permute-start(bf16[512,128]{1,0:T(8,128)(2,1)S(1)} %get-tuple-element.78), channel_id=1, source_target_pairs={{0,8},{8,0},{16,24},{24,16},{32,40},{40,32},{48,56},{56,48},{64,72... | collective-permute-start | bytes 393224 | tf_op jit(solution)/shard_map/ppermute | solution.py:328
  93.6 3.9 %collective-permute-start.21 = (bf16[512,128]{1,0:T(8,128)(2,1)S(1)}, bf16[512,128]{1,0:T(8,128)(2,1)S(1)}, u32[]{:S(2)}, u32[]{:S(2)}) collective-permute-start(bf16[512,128]{1,0:T(8,128)(2,1)S(1)} %collective-permute-done.20.b_ref), channel_id=1, source_target_pairs={{8,0},{16,8},{24,16},{32,24},{40,32},{48,40},{56,48},{64,56},{72,6... | collective-permute-start | bytes 393224 | tf_op jit(solution)/shard_map/ppermute | solution.py:328
  97.5 0.9 shard_map.113
  98.5 1.0 shard_map.105.inside_ref
  99.5 0.7 copy-done.7
  100.2 1.9 %shard_map.112 = bf16[256,1024]{1,0:T(8,128)(2,1)} custom-call(f32[256,128]{1,0:T(8,128)S(1)} %get-tuple-element.53.live_ref, bf16[256,1024]{1,0:T(8,128)(2,1)S(1)} %copy-done.2, f32[256,1024]{1,0:T(8,128)S(1)} %shard_map.105.inside_ref, f32[4,128,128]{2,1,0:T(8,128)S(1)} %get-tuple-element.77.held_ref, ...), custom_call_target="tpu_custom_call" | custom-call | flops 2000000 | bytes 1048576 | tf_op jit(solution)/shard_map/pallas_call | solution.py:24
  102.1 1.6 %collective-permute-done.14.f_ref = bf16[512,128]{1,0:T(8,128)(2,1)S(1)} collective-permute-done((bf16[512,128]{1,0:T(8,128)(2,1)S(1)}, bf16[512,128]{1,0:T(8,128)(2,1)S(1)}, u32[]{:S(2)}, u32[]{:S(2)}) %collective-permute-start.14) | collective-permute-done | bytes 131104 | tf_op jit(solution)/shard_map/ppermute | solution.py:328
  103.7 1.2 %shard_map.121 = bf16[256,1024]{1,0:T(8,128)(2,1)} custom-call(f32[24,256]{1,0:T(8,128)S(1)} %get-tuple-element.54.bias_ref, f32[256,128]{1,0:T(8,128)S(1)} %get-tuple-element.53.live_ref, bf16[2048,256]{1,0:T(8,128)(2,1)S(1)} %get-tuple-element.79.q2_ref, bf16[512,128]{1,0:T(8,128)(2,1)S(1)} %collective-permute-done.14.f_ref, ...), custom_call_target="tpu_custom_call" | custom-call | flops 2000000 | bytes 1048576 | tf_op jit(solution)/shard_map/pallas_call | solution.py:24
  (50 shorter events, 0.9 us)
Async XLA Ops:
  0.6 0.9 copy-start.5
  1.5 45.0 %copy-start.6 = (f32[256,8]{0,1:T(8,128)S(1)}, f32[256,8]{0,1:T(8,128)}, u32[]{:S(2)}) copy-start(f32[256,8]{0,1:T(8,128)} %param.12) | copy-start | bytes 24580
  1.5 26.1 %collective-permute-start.7 = (bf16[512,128]{1,0:T(8,128)(2,1)S(1)}, bf16[512,128]{1,0:T(8,128)(2,1)S(1)}, u32[]{:S(2)}, u32[]{:S(2)}) collective-permute-start(bf16[512,128]{1,0:T(8,128)(2,1)S(1)} %constant_dynamic-update-slice_fusion), channel_id=1, source_target_pairs={{0,8},{8,16},{16,24},{24,32},{32,40},{40,48},{48,56},{56,64},{64,7... | collective-permute-start | bytes 393224 | tf_op jit(solution)/shard_map/ppermute | solution.py:328
  4.4 23.2 %collective-permute-start.15 = (bf16[512,128]{1,0:T(8,128)(2,1)S(1)}, bf16[512,128]{1,0:T(8,128)(2,1)S(1)}, u32[]{:S(2)}, u32[]{:S(2)}) collective-permute-start(bf16[512,128]{1,0:T(8,128)(2,1)S(1)} %constant_dynamic-update-slice_fusion), channel_id=1, source_target_pairs={{8,0},{16,8},{24,16},{32,24},{40,32},{48,40},{56,48},{64,56},{72,6... | collective-permute-start | bytes 393224 | tf_op jit(solution)/shard_map/ppermute | solution.py:328
  27.6 6.2 %collective-permute-start.8 = (bf16[512,128]{1,0:T(8,128)(2,1)S(1)}, bf16[512,128]{1,0:T(8,128)(2,1)S(1)}, u32[]{:S(2)}, u32[]{:S(2)}) collective-permute-start(bf16[512,128]{1,0:T(8,128)(2,1)S(1)} %collective-permute-done.7.f_ref), channel_id=1, source_target_pairs={{0,8},{8,16},{16,24},{24,32},{32,40},{40,48},{48,56},{56,64},{64,7... | collective-permute-start | bytes 393224 | tf_op jit(solution)/shard_map/ppermute | solution.py:328
  27.6 6.2 %collective-permute-start.16 = (bf16[512,128]{1,0:T(8,128)(2,1)S(1)}, bf16[512,128]{1,0:T(8,128)(2,1)S(1)}, u32[]{:S(2)}, u32[]{:S(2)}) collective-permute-start(bf16[512,128]{1,0:T(8,128)(2,1)S(1)} %collective-permute-done.15.b_ref), channel_id=1, source_target_pairs={{8,0},{16,8},{24,16},{32,24},{40,32},{48,40},{56,48},{64,56},{72,6... | collective-permute-start | bytes 393224 | tf_op jit(solution)/shard_map/ppermute | solution.py:328
  33.8 6.2 %collective-permute-start.9 = (bf16[512,128]{1,0:T(8,128)(2,1)S(1)}, bf16[512,128]{1,0:T(8,128)(2,1)S(1)}, u32[]{:S(2)}, u32[]{:S(2)}) collective-permute-start(bf16[512,128]{1,0:T(8,128)(2,1)S(1)} %collective-permute-done.8.f_ref), channel_id=1, source_target_pairs={{0,8},{8,16},{16,24},{24,32},{32,40},{40,48},{48,56},{56,64},{64,7... | collective-permute-start | bytes 393224 | tf_op jit(solution)/shard_map/ppermute | solution.py:328
  33.8 6.2 %collective-permute-start.17 = (bf16[512,128]{1,0:T(8,128)(2,1)S(1)}, bf16[512,128]{1,0:T(8,128)(2,1)S(1)}, u32[]{:S(2)}, u32[]{:S(2)}) collective-permute-start(bf16[512,128]{1,0:T(8,128)(2,1)S(1)} %collective-permute-done.16.b_ref), channel_id=1, source_target_pairs={{8,0},{16,8},{24,16},{32,24},{40,32},{48,40},{56,48},{64,56},{72,6... | collective-permute-start | bytes 393224 | tf_op jit(solution)/shard_map/ppermute | solution.py:328
  40.0 6.5 %collective-permute-start.10 = (bf16[512,128]{1,0:T(8,128)(2,1)S(1)}, bf16[512,128]{1,0:T(8,128)(2,1)S(1)}, u32[]{:S(2)}, u32[]{:S(2)}) collective-permute-start(bf16[512,128]{1,0:T(8,128)(2,1)S(1)} %collective-permute-done.9.f_ref), channel_id=1, source_target_pairs={{0,8},{8,16},{16,24},{24,32},{32,40},{40,48},{48,56},{56,64},{64,7... | collective-permute-start | bytes 393224 | tf_op jit(solution)/shard_map/ppermute | solution.py:328
  40.0 9.3 %collective-permute-start.18 = (bf16[512,128]{1,0:T(8,128)(2,1)S(1)}, bf16[512,128]{1,0:T(8,128)(2,1)S(1)}, u32[]{:S(2)}, u32[]{:S(2)}) collective-permute-start(bf16[512,128]{1,0:T(8,128)(2,1)S(1)} %collective-permute-done.17.b_ref), channel_id=1, source_target_pairs={{8,0},{16,8},{24,16},{32,24},{40,32},{48,40},{56,48},{64,56},{72,6... | collective-permute-start | bytes 393224 | tf_op jit(solution)/shard_map/ppermute | solution.py:328
  46.5 7.4 %collective-permute-start.11 = (bf16[512,128]{1,0:T(8,128)(2,1)S(1)}, bf16[512,128]{1,0:T(8,128)(2,1)S(1)}, u32[]{:S(2)}, u32[]{:S(2)}) collective-permute-start(bf16[512,128]{1,0:T(8,128)(2,1)S(1)} %collective-permute-done.10.f_ref), channel_id=1, source_target_pairs={{0,8},{8,16},{16,24},{24,32},{32,40},{40,48},{48,56},{56,64},{64,7... | collective-permute-start | bytes 393224 | tf_op jit(solution)/shard_map/ppermute | solution.py:328
  46.5 0.7 copy-start.8
  49.2 5.9 %collective-permute-start = (bf16[544,128]{1,0:T(8,128)(2,1)S(1)}, bf16[544,128]{1,0:T(8,128)(2,1)S(1)}, u32[]{:S(2)}, u32[]{:S(2)}) collective-permute-start(bf16[544,128]{1,0:T(8,128)(2,1)S(1)} %get-tuple-element.57), channel_id=1, source_target_pairs={{0,8},{8,0},{16,24},{24,16},{32,40},{40,32},{48,56},{56,48},{64,72... | collective-permute-start | bytes 417800 | tf_op jit(solution)/shard_map/ppermute | solution.py:328
  49.3 23.6 %collective-permute-start.19 = (bf16[512,128]{1,0:T(8,128)(2,1)S(1)}, bf16[512,128]{1,0:T(8,128)(2,1)S(1)}, u32[]{:S(2)}, u32[]{:S(2)}) collective-permute-start(bf16[512,128]{1,0:T(8,128)(2,1)S(1)} %collective-permute-done.18.b_ref), channel_id=1, source_target_pairs={{8,0},{16,8},{24,16},{32,24},{40,32},{48,40},{56,48},{64,56},{72,6... | collective-permute-start | bytes 393224 | tf_op jit(solution)/shard_map/ppermute | solution.py:328
  53.8 21.1 %collective-permute-start.12 = (bf16[512,128]{1,0:T(8,128)(2,1)S(1)}, bf16[512,128]{1,0:T(8,128)(2,1)S(1)}, u32[]{:S(2)}, u32[]{:S(2)}) collective-permute-start(bf16[512,128]{1,0:T(8,128)(2,1)S(1)} %collective-permute-done.11.f_ref), channel_id=1, source_target_pairs={{0,8},{8,16},{16,24},{24,32},{32,40},{40,48},{48,56},{56,64},{64,7... | collective-permute-start | bytes 393224 | tf_op jit(solution)/shard_map/ppermute | solution.py:328
  55.1 42.4 %copy-start.3 = (bf16[256,1024]{1,0:T(8,128)(2,1)S(1)}, bf16[256,1024]{1,0:T(8,128)(2,1)}, u32[]{:S(2)}) copy-start(bf16[256,1024]{1,0:T(8,128)(2,1)} %q_ref.5) | copy-start | bytes 1572868
  55.2 6.5 %collective-permute-start.1 = (bf16[288,128]{1,0:T(8,128)(2,1)S(1)}, bf16[288,128]{1,0:T(8,128)(2,1)S(1)}, u32[]{:S(2)}, u32[]{:S(2)}) collective-permute-start(bf16[288,128]{1,0:T(8,128)(2,1)S(1)} %get-tuple-element.60), channel_id=1, source_target_pairs={{0,16},{8,24},{16,0},{24,8},{32,48},{40,56},{48,32},{56,40},{64,80... | collective-permute-start | bytes 221192 | tf_op jit(solution)/shard_map/ppermute | solution.py:328
  61.7 35.8 %copy-start.4 = (bf16[256,128]{1,0:T(8,128)(2,1)S(1)}, bf16[256,128]{1,0:T(8,128)(2,1)}, u32[]{:S(2)}) copy-start(bf16[256,128]{1,0:T(8,128)(2,1)} %k_ref.3) | copy-start | bytes 196612
  61.8 8.0 %collective-permute-start.2 = (bf16[160,128]{1,0:T(8,128)(2,1)S(1)}, bf16[160,128]{1,0:T(8,128)(2,1)S(1)}, u32[]{:S(2)}, u32[]{:S(2)}) collective-permute-start(bf16[160,128]{1,0:T(8,128)(2,1)S(1)} %get-tuple-element.63), channel_id=1, source_target_pairs={{0,32},{8,40},{16,48},{24,56},{32,0},{40,8},{48,16},{56,24},{64,96... | collective-permute-start | bytes 122888 | tf_op jit(solution)/shard_map/ppermute | solution.py:328
  69.8 28.7 %copy-start.2 = (bf16[256,1024]{1,0:T(8,128)(2,1)S(1)}, bf16[256,1024]{1,0:T(8,128)(2,1)}, u32[]{:S(2)}) copy-start(bf16[256,1024]{1,0:T(8,128)(2,1)} %q_ref.4) | copy-start | bytes 1572868
  69.8 6.1 %collective-permute-start.3 = (bf16[128,128]{1,0:T(8,128)(2,1)S(1)}, bf16[128,128]{1,0:T(8,128)(2,1)S(1)}, u32[]{:S(2)}, u32[]{:S(2)}) collective-permute-start(bf16[128,128]{1,0:T(8,128)(2,1)S(1)} %get-tuple-element.66), channel_id=1, source_target_pairs={{0,96},{8,104},{16,112},{24,120},{32,64},{40,72},{48,80},{56,88},{... | collective-permute-start | bytes 98312 | tf_op jit(solution)/shard_map/ppermute | solution.py:328
  72.9 20.7 %collective-permute-start.20 = (bf16[512,128]{1,0:T(8,128)(2,1)S(1)}, bf16[512,128]{1,0:T(8,128)(2,1)S(1)}, u32[]{:S(2)}, u32[]{:S(2)}) collective-permute-start(bf16[512,128]{1,0:T(8,128)(2,1)S(1)} %collective-permute-done.19.b_ref), channel_id=1, source_target_pairs={{8,0},{16,8},{24,16},{32,24},{40,32},{48,40},{56,48},{64,56},{72,6... | collective-permute-start | bytes 393224 | tf_op jit(solution)/shard_map/ppermute | solution.py:328
  74.9 22.6 %collective-permute-start.13 = (bf16[512,128]{1,0:T(8,128)(2,1)S(1)}, bf16[512,128]{1,0:T(8,128)(2,1)S(1)}, u32[]{:S(2)}, u32[]{:S(2)}) collective-permute-start(bf16[512,128]{1,0:T(8,128)(2,1)S(1)} %collective-permute-done.12.f_ref), channel_id=1, source_target_pairs={{0,8},{8,16},{16,24},{24,32},{32,40},{40,48},{48,56},{56,64},{64,7... | collective-permute-start | bytes 393224 | tf_op jit(solution)/shard_map/ppermute | solution.py:328
  76.0 8.9 %collective-permute-start.4 = (bf16[128,128]{1,0:T(8,128)(2,1)S(1)}, bf16[128,128]{1,0:T(8,128)(2,1)S(1)}, u32[]{:S(2)}, u32[]{:S(2)}) collective-permute-start(bf16[128,128]{1,0:T(8,128)(2,1)S(1)} %get-tuple-element.70), channel_id=1, source_target_pairs={{0,32},{8,40},{16,48},{24,56},{32,0},{40,8},{48,16},{56,24},{64,96... | collective-permute-start | bytes 98312 | tf_op jit(solution)/shard_map/ppermute | solution.py:328
  84.9 5.3 %collective-permute-start.5 = (bf16[256,128]{1,0:T(8,128)(2,1)S(1)}, bf16[256,128]{1,0:T(8,128)(2,1)S(1)}, u32[]{:S(2)}, u32[]{:S(2)}) collective-permute-start(bf16[256,128]{1,0:T(8,128)(2,1)S(1)} %get-tuple-element.74), channel_id=1, source_target_pairs={{0,16},{8,24},{16,0},{24,8},{32,48},{40,56},{48,32},{56,40},{64,80... | collective-permute-start | bytes 196616 | tf_op jit(solution)/shard_map/ppermute | solution.py:328
  90.2 8.3 %copy-start = (bf16[256,1024]{1,0:T(8,128)(2,1)S(1)}, bf16[256,1024]{1,0:T(8,128)(2,1)}, u32[]{:S(2)}) copy-start(bf16[256,1024]{1,0:T(8,128)(2,1)} %k_ref.2) | copy-start | bytes 1572868
  90.2 8.3 %copy-start.1 = (bf16[256,1024]{1,0:T(8,128)(2,1)S(1)}, bf16[256,1024]{1,0:T(8,128)(2,1)}, u32[]{:S(2)}) copy-start(bf16[256,1024]{1,0:T(8,128)(2,1)} %v_ref.2) | copy-start | bytes 1572868
  90.3 9.2 %collective-permute-start.6 = (bf16[512,128]{1,0:T(8,128)(2,1)S(1)}, bf16[512,128]{1,0:T(8,128)(2,1)S(1)}, u32[]{:S(2)}, u32[]{:S(2)}) collective-permute-start(bf16[512,128]{1,0:T(8,128)(2,1)S(1)} %get-tuple-element.78), channel_id=1, source_target_pairs={{0,8},{8,0},{16,24},{24,16},{32,40},{40,32},{48,56},{56,48},{64,72... | collective-permute-start | bytes 393224 | tf_op jit(solution)/shard_map/ppermute | solution.py:328
  93.6 8.5 %collective-permute-start.21 = (bf16[512,128]{1,0:T(8,128)(2,1)S(1)}, bf16[512,128]{1,0:T(8,128)(2,1)S(1)}, u32[]{:S(2)}, u32[]{:S(2)}) collective-permute-start(bf16[512,128]{1,0:T(8,128)(2,1)S(1)} %collective-permute-done.20.b_ref), channel_id=1, source_target_pairs={{8,0},{16,8},{24,16},{32,24},{40,32},{48,40},{56,48},{64,56},{72,6... | collective-permute-start | bytes 393224 | tf_op jit(solution)/shard_map/ppermute | solution.py:328
  97.5 6.2 %collective-permute-start.14 = (bf16[512,128]{1,0:T(8,128)(2,1)S(1)}, bf16[512,128]{1,0:T(8,128)(2,1)S(1)}, u32[]{:S(2)}, u32[]{:S(2)}) collective-permute-start(bf16[512,128]{1,0:T(8,128)(2,1)S(1)} %collective-permute-done.13.f_ref), channel_id=1, source_target_pairs={{0,8},{8,16},{16,24},{24,32},{32,40},{40,48},{48,56},{56,64},{64,7... | collective-permute-start | bytes 393224 | tf_op jit(solution)/shard_map/ppermute | solution.py:328
  99.5 0.7 copy-start.7

commit v3 on v2

--- a/solution.py
+++ b/solution.py
@@ -176,7 +176,8 @@
         msg_ref[h * width : (h + 1) * width, :] = jnp.where(upper, low, high).astype(BF16)
 
 
-def inside_kernel(bias_ref, q_ref, k_ref, v_ref, c_ref, ct_ref, out_ref):
+def inside_kernel(bias_ref, q_ref, k_ref, v_ref, c_ref, ct_ref, gain_ref, out_ref, scaled_ref, gain_out_ref):
+    gain_out_ref[...] = gain_ref[...]
     i = lax.axis_index("seq")
     rows = q_ref.shape[0]
     heads = c_ref.shape[0]
@@ -187,24 +188,24 @@
     allowed = (col <= row) & (bias_ref[pl.ds(i, 1), :] == 0.0)
     running = c_ref[...]
     running_t = ct_ref[...]
+    grown = jnp.exp(running_t) * scale
     for h in range(heads):
         at = slice(h * width, (h + 1) * width)
         scores = lax.dot_general(
             q_ref[:, at], k_ref[:, at], (((1,), (1,)), ((), ())), preferred_element_type=F32
         )
+        scaled_ref[:, at] = (q_ref[:, at].astype(F32) * grown[:, h : h + 1]).astype(BF16)
         gaps = running_t[:, h : h + 1] - running[h : h + 1, :]
         weights = jnp.exp(jnp.where(allowed, gaps, NEG))
         intra = (scores * scale * weights).astype(BF16)
         out_ref[:, at] = jnp.dot(intra, v_ref[:, at], preferred_element_type=F32)
 
 
-def light_kernel(live_ref, q_ref, inside_ref, held_ref, recv_ref, ct_ref, gain_ref, out_ref):
+def light_kernel(live_ref, q_ref, inside_ref, held_ref, recv_ref, gain_ref, out_ref):
     i = lax.axis_index("seq")
     half, width = held_ref.shape[0], held_ref.shape[1]
-    scale = width ** (-0.5)
     first = keep_bit(i, 0) == 0
     live = live_ref[...] > 0.0
-    grown = jnp.exp(ct_ref[...]) * scale
     for h in range(2 * half):
         at = slice(h * width, (h + 1) * width)
         mod = h % half
@@ -213,7 +214,7 @@
         pick_held = first if h < half else jnp.logical_not(first)
         entering = jnp.where(pick_held, held.astype(F32), got.astype(F32)).astype(BF16)
         across = jnp.dot(q_ref[:, at], entering, preferred_element_type=F32)
-        combined = inside_ref[:, at] + across * grown[:, h : h + 1]
+        combined = inside_ref[:, at] + across
         mean = jnp.mean(combined * combined, axis=-1, keepdims=True)
         normed = combined * lax.rsqrt(mean + 1e-06) * gain_ref[:, at]
         out_ref[:, at] = jnp.where(live, normed, 0.0).astype(BF16)
@@ -263,17 +264,17 @@
     return new, jnp.exp2((old - new) * factor), sum(probs[1:], probs[0]), summed
 
 
-def step_kernel(step, count, bias_ref, q2_ref, f_ref, b_ref, unused_m, unused_l, unused_acc, m_ref, l_ref, acc_ref):
+def step_kernel(step, count, blocks, bias_ref, q2_ref, *refs):
+    kv_refs, (m_ref, l_ref, acc_ref) = refs[:blocks], refs[-3:]
     i = lax.axis_index("seq")
 
     @pl.when(i >= step)
     def run():
         wrapped = i + step - count
-        biases = [
-            bias_ref[pl.ds(i - step, 1), :],
-            bias_ref[pl.ds(jnp.where(wrapped >= 0, wrapped, count), 1), :],
-        ]
-        new, shrink, total, summed = attend(q2_ref, [f_ref, b_ref], biases, m_ref)
+        biases = [bias_ref[pl.ds(i - step, 1), :]]
+        if blocks > 1:
+            biases.append(bias_ref[pl.ds(jnp.where(wrapped >= 0, wrapped, count), 1), :])
+        new, shrink, total, summed = attend(q2_ref, kv_refs, biases, m_ref)
         m_ref[...] = new
         l_ref[...] = shrink * l_ref[...] + total
         acc_ref[...] = shrink * acc_ref[...] + summed
@@ -317,12 +318,15 @@
     width = light_queries.shape[1] // heads
     count = lax.axis_size("seq")
     half = heads // 2
-
-    def forward():
-        return [(i, (i + 1) % count) for i in range(count)]
-
-    def backward():
-        return [((j + 1) % count, j) for j in range(count)]
+    steps = count // 2
+    backs = count - 1 - steps
+
+    def forward(step):
+        if step <= backs:
+            return [(i, (i + 1) % count) for i in range(count)]
+        return [(i, i + 1) for i in range(step - 1, count - 1)]
+
+    backward = [((j + 1) % count, j) for j in range(count)]
 
     def send(x, pairs):
         return lax.ppermute(x, "seq", pairs)
@@ -331,8 +335,8 @@
         return send(x, [(i, i ^ distance) for i in range(count)])
 
     own_kv = jnp.concatenate([soft_keys, soft_values], axis=0)
-    f = send(own_kv, forward())
-    b = send(own_kv, backward())
+    f = send(own_kv, forward(1))
+    b = send(own_kv, backward)
 
     msg, kept, logs, running, running_t, bias, live = call(
         prep_kernel,
@@ -382,9 +386,9 @@
             partial(down_kernel, level, held is None), [((n, width, width), F32), ((n * width, width), BF16)], ins
         )
         recv = exchange(msg, 1 << level)
-    (inside,) = call(
+    inside, scaled, gain = call(
         inside_kernel,
-        [((rows, heads * width), F32)],
+        [((rows, heads * width), F32), ((rows, heads * width), BF16), ((1, heads * width), F32)],
         [
             (False, bias),
             (False, light_queries),
@@ -392,6 +396,7 @@
             (False, light_values),
             (False, running),
             (False, running_t),
+            (False, norm_gain.reshape(1, heads * width)),
         ],
     )
     (light_out,) = call(
@@ -399,12 +404,11 @@
         [((rows, heads * width), BF16)],
         [
             (False, live),
-            (False, light_queries),
+            (False, scaled),
             (False, inside),
             (False, held),
             (False, recv),
-            (False, running_t),
-            (False, norm_gain.reshape(1, heads * width)),
+            (False, gain),
         ],
     )
 
@@ -415,18 +419,20 @@
         [((soft_rows, width + 128), BF16), stat, stat, stat],
         [(False, bias), (False, soft_queries), (False, soft_keys), (False, soft_values)],
     )
-    for step in range(1, count // 2):
-        nf = send(f, forward())
-        nb = send(b, backward()) if step + 1 < count // 2 else None
+    for step in range(1, steps):
+        nf = send(f, forward(step + 1))
+        nb = send(b, backward) if step < backs else None
+        blocks = [(False, f)] + ([(False, b)] if step <= backs else [])
+        at = 2 + len(blocks)
         state = call(
-            partial(step_kernel, step, count),
+            partial(step_kernel, step, count, len(blocks)),
             [stat, stat, stat],
-            [(False, bias), (False, q2), (False, f), (False, b)] + [(False, s) for s in state],
-            aliases={4: 0, 5: 1, 6: 2},
+            [(False, bias), (False, q2)] + blocks + [(False, s) for s in state],
+            aliases={at: 0, at + 1: 1, at + 2: 2},
         )
         f, b = nf, nb
     (soft_out,) = call(
-        partial(last_kernel, count // 2),
+        partial(last_kernel, steps),
         [((rows, soft_queries.shape[1]), BF16)],
         [(False, bias), (False, live), (False, q2), (False, f)] + [(False, s) for s in state],
     )

time: 105 us -> 103 us (0.981)
  waiting for transfers between devices: 36.5 us -> 34.9 us
    ppermute x22, waiting for transfers between devices: 36.5 us -> 34.9 us  [send(): return lax.ppermute(x, 'seq', pairs)]
  transfers between devices with their start and end apart: 22 -> 22, of which waited for: 11 -> 10; matrix products, arithmetic and copies ran while one was open for 0% -> 0% of each run, Pallas kernels for 6% -> 5%
where the time goes in v3:
time: 103 us
  starting transfers between devices  58.3 us (57%)
  waiting for transfers between devices  34.9 us (34%)
  Pallas kernels  6.83 us (7%)
  local copies, waits for them, and re-layouts  2.22 us (2%)
    ppermute x22, starting transfers between devices, send(): return lax.ppermute(x, 'seq', pairs)  58.3 us
    ppermute x22, waiting for transfers between devices, send(): return lax.ppermute(x, 'seq', pairs)  34.9 us
    pallas_call x18, Pallas kernels, call(): pl.pallas_call(kernel, out_shape=outs, in_specs=specs, out_specs=[VMEM] *...  6.83 us
    unnamed x19, local copies, waits for them, and re-layouts  2.21 us
  transfers between devices with their start and end apart: 22, of which 10 were waited for; matrix products, arithmetic and copies ran while one was open for 0% of the time, Pallas kernels for 5%

profile of v3, /device:TPU:36, one launch (start us, length us, event | category | flops | bytes accessed | tf_op | source)
XLA Modules:
  0.0 103.1 jit_solution(6908234665863261087)
XLA Ops:
  0.6 0.9 constant_dynamic-update-slice_fusion.1
  1.5 2.9 %collective-permute-start.7 = (bf16[512,128]{1,0:T(8,128)(2,1)S(1)}, bf16[512,128]{1,0:T(8,128)(2,1)S(1)}, u32[]{:S(2)}, u32[]{:S(2)}) collective-permute-start(bf16[512,128]{1,0:T(8,128)(2,1)S(1)} %constant_dynamic-update-slice_fusion), channel_id=1, source_target_pairs={{0,8},{8,16},{16,24},{24,32},{32,40},{40,48},{48,56},{56,64},{64,7... | collective-permute-start | bytes 393224 | tf_op jit(solution)/shard_map/ppermute | solution.py:332
  4.4 19.7 %collective-permute-start.15 = (bf16[512,128]{1,0:T(8,128)(2,1)S(1)}, bf16[512,128]{1,0:T(8,128)(2,1)S(1)}, u32[]{:S(2)}, u32[]{:S(2)}) collective-permute-start(bf16[512,128]{1,0:T(8,128)(2,1)S(1)} %constant_dynamic-update-slice_fusion), channel_id=1, source_target_pairs={{8,0},{16,8},{24,16},{32,24},{40,32},{48,40},{56,48},{64,56},{72,6... | collective-permute-start | bytes 393224 | tf_op jit(solution)/shard_map/ppermute | solution.py:332
  24.2 3.4 %collective-permute-done.7.refs_0_ = bf16[512,128]{1,0:T(8,128)(2,1)S(1)} collective-permute-done((bf16[512,128]{1,0:T(8,128)(2,1)S(1)}, bf16[512,128]{1,0:T(8,128)(2,1)S(1)}, u32[]{:S(2)}, u32[]{:S(2)}) %collective-permute-start.7) | collective-permute-done | bytes 131104 | tf_op jit(solution)/shard_map/ppermute | solution.py:332
  27.6 3.2 %collective-permute-start.16 = (bf16[512,128]{1,0:T(8,128)(2,1)S(1)}, bf16[512,128]{1,0:T(8,128)(2,1)S(1)}, u32[]{:S(2)}, u32[]{:S(2)}) collective-permute-start(bf16[512,128]{1,0:T(8,128)(2,1)S(1)} %collective-permute-done.15.refs_1_), channel_id=1, source_target_pairs={{8,0},{16,8},{24,16},{32,24},{40,32},{48,40},{56,48},{64,56},{72,6... | collective-permute-start | bytes 393224 | tf_op jit(solution)/shard_map/ppermute | solution.py:332
  30.9 2.9 %collective-permute-done.8.refs_0_ = bf16[512,128]{1,0:T(8,128)(2,1)S(1)} collective-permute-done((bf16[512,128]{1,0:T(8,128)(2,1)S(1)}, bf16[512,128]{1,0:T(8,128)(2,1)S(1)}, u32[]{:S(2)}, u32[]{:S(2)}) %collective-permute-start.8) | collective-permute-done | bytes 131104 | tf_op jit(solution)/shard_map/ppermute | solution.py:332
  33.8 3.2 %collective-permute-start.17 = (bf16[512,128]{1,0:T(8,128)(2,1)S(1)}, bf16[512,128]{1,0:T(8,128)(2,1)S(1)}, u32[]{:S(2)}, u32[]{:S(2)}) collective-permute-start(bf16[512,128]{1,0:T(8,128)(2,1)S(1)} %collective-permute-done.16.refs_1_), channel_id=1, source_target_pairs={{8,0},{16,8},{24,16},{32,24},{40,32},{48,40},{56,48},{64,56},{72,6... | collective-permute-start | bytes 393224 | tf_op jit(solution)/shard_map/ppermute | solution.py:332
  37.0 2.9 %collective-permute-done.9.refs_0_ = bf16[512,128]{1,0:T(8,128)(2,1)S(1)} collective-permute-done((bf16[512,128]{1,0:T(8,128)(2,1)S(1)}, bf16[512,128]{1,0:T(8,128)(2,1)S(1)}, u32[]{:S(2)}, u32[]{:S(2)}) %collective-permute-start.9) | collective-permute-done | bytes 131104 | tf_op jit(solution)/shard_map/ppermute | solution.py:332
  40.0 3.2 %collective-permute-start.18 = (bf16[512,128]{1,0:T(8,128)(2,1)S(1)}, bf16[512,128]{1,0:T(8,128)(2,1)S(1)}, u32[]{:S(2)}, u32[]{:S(2)}) collective-permute-start(bf16[512,128]{1,0:T(8,128)(2,1)S(1)} %collective-permute-done.17.refs_1_), channel_id=1, source_target_pairs={{8,0},{16,8},{24,16},{32,24},{40,32},{48,40},{56,48},{64,56},{72,6... | collective-permute-start | bytes 393224 | tf_op jit(solution)/shard_map/ppermute | solution.py:332
  43.2 3.3 %collective-permute-done.10.refs_0_ = bf16[512,128]{1,0:T(8,128)(2,1)S(1)} collective-permute-done((bf16[512,128]{1,0:T(8,128)(2,1)S(1)}, bf16[512,128]{1,0:T(8,128)(2,1)S(1)}, u32[]{:S(2)}, u32[]{:S(2)}) %collective-permute-start.10) | collective-permute-done | bytes 131104 | tf_op jit(solution)/shard_map/ppermute | solution.py:332
  46.5 0.6 copy-done.8
  47.1 2.0 %shard_map.104 = (bf16[544,128]{1,0:T(8,128)(2,1)S(1)}, f32[4,128,128]{2,1,0:T(8,128)S(1)}, f32[8,128]{1,0:T(8,128)S(1)}, f32[8,256]{1,0:T(8,128)S(1)}, f32[256,...) custom-call(s32[1,16]{1,0:T(1,128)S(1)} %bitcast.5, bf16[256,1024]{1,0:T(8,128)(2,1)} %k_ref.2, ...), custom_call_target="tpu_custom_call" | custom-call | flops 2000000 | bytes 1048576 | tf_op jit(solution)/shard_map/pallas_call | solution.py:24
  49.3 3.4 %collective-permute-start.19 = (bf16[512,128]{1,0:T(8,128)(2,1)S(1)}, bf16[512,128]{1,0:T(8,128)(2,1)S(1)}, u32[]{:S(2)}, u32[]{:S(2)}) collective-permute-start(bf16[512,128]{1,0:T(8,128)(2,1)S(1)} %collective-permute-done.18.refs_1_), channel_id=1, source_target_pairs={{8,0},{16,8},{24,16},{32,24},{40,32},{48,40},{56,48},{64,56},{72,6... | collective-permute-start | bytes 393224 | tf_op jit(solution)/shard_map/ppermute | solution.py:332
  52.7 1.2 %collective-permute-done.11.refs_0_ = bf16[512,128]{1,0:T(8,128)(2,1)S(1)} collective-permute-done((bf16[512,128]{1,0:T(8,128)(2,1)S(1)}, bf16[512,128]{1,0:T(8,128)(2,1)S(1)}, u32[]{:S(2)}, u32[]{:S(2)}) %collective-permute-start.11) | collective-permute-done | bytes 131104 | tf_op jit(solution)/shard_map/ppermute | solution.py:332
  53.8 1.3 %collective-permute-done.recv_ref = bf16[544,128]{1,0:T(8,128)(2,1)S(1)} collective-permute-done((bf16[544,128]{1,0:T(8,128)(2,1)S(1)}, bf16[544,128]{1,0:T(8,128)(2,1)S(1)}, u32[]{:S(2)}, u32[]{:S(2)}) %collective-permute-start) | collective-permute-done | bytes 139296 | tf_op jit(solution)/shard_map/ppermute | solution.py:332
  55.3 6.4 %collective-permute-done.1.recv_ref = bf16[288,128]{1,0:T(8,128)(2,1)S(1)} collective-permute-done((bf16[288,128]{1,0:T(8,128)(2,1)S(1)}, bf16[288,128]{1,0:T(8,128)(2,1)S(1)}, u32[]{:S(2)}, u32[]{:S(2)}) %collective-permute-start.1) | collective-permute-done | bytes 73760 | tf_op jit(solution)/shard_map/ppermute | solution.py:332
  61.9 7.9 %collective-permute-done.2.recv_ref = bf16[160,128]{1,0:T(8,128)(2,1)S(1)} collective-permute-done((bf16[160,128]{1,0:T(8,128)(2,1)S(1)}, bf16[160,128]{1,0:T(8,128)(2,1)S(1)}, u32[]{:S(2)}, u32[]{:S(2)}) %collective-permute-start.2) | collective-permute-done | bytes 40992 | tf_op jit(solution)/shard_map/ppermute | solution.py:332
  69.8 2.9 %collective-permute-start.3 = (bf16[128,128]{1,0:T(8,128)(2,1)S(1)}, bf16[128,128]{1,0:T(8,128)(2,1)S(1)}, u32[]{:S(2)}, u32[]{:S(2)}) collective-permute-start(bf16[128,128]{1,0:T(8,128)(2,1)S(1)} %get-tuple-element.71), channel_id=1, source_target_pairs={{0,96},{8,104},{16,112},{24,120},{32,64},{40,72},{48,80},{56,88},{... | collective-permute-start | bytes 98312 | tf_op jit(solution)/shard_map/ppermute | solution.py:332
  72.7 2.0 %collective-permute-start.20 = (bf16[512,128]{1,0:T(8,128)(2,1)S(1)}, bf16[512,128]{1,0:T(8,128)(2,1)S(1)}, u32[]{:S(2)}, u32[]{:S(2)}) collective-permute-start(bf16[512,128]{1,0:T(8,128)(2,1)S(1)} %collective-permute-done.19.refs_1_), channel_id=1, source_target_pairs={{8,0},{16,8},{24,16},{32,24},{40,32},{48,40},{56,48},{64,56},{72,6... | collective-permute-start | bytes 393224 | tf_op jit(solution)/shard_map/ppermute | solution.py:332
  74.8 1.0 collective-permute-start.13
  75.8 5.7 %collective-permute-start.4 = (bf16[128,128]{1,0:T(8,128)(2,1)S(1)}, bf16[128,128]{1,0:T(8,128)(2,1)S(1)}, u32[]{:S(2)}, u32[]{:S(2)}) collective-permute-start(bf16[128,128]{1,0:T(8,128)(2,1)S(1)} %get-tuple-element.75), channel_id=1, source_target_pairs={{0,32},{8,40},{16,48},{24,56},{32,0},{40,8},{48,16},{56,24},{64,96... | collective-permute-start | bytes 98312 | tf_op jit(solution)/shard_map/ppermute | solution.py:332
  81.5 3.2 %collective-permute-done.4.refs_1_ = bf16[128,128]{1,0:T(8,128)(2,1)S(1)} collective-permute-done((bf16[128,128]{1,0:T(8,128)(2,1)S(1)}, bf16[128,128]{1,0:T(8,128)(2,1)S(1)}, u32[]{:S(2)}, u32[]{:S(2)}) %collective-permute-start.4) | collective-permute-done | bytes 32800 | tf_op jit(solution)/shard_map/ppermute | solution.py:332
  84.8 2.9 %collective-permute-start.5 = (bf16[256,128]{1,0:T(8,128)(2,1)S(1)}, bf16[256,128]{1,0:T(8,128)(2,1)S(1)}, u32[]{:S(2)}, u32[]{:S(2)}) collective-permute-start(bf16[256,128]{1,0:T(8,128)(2,1)S(1)} %get-tuple-element.79), channel_id=1, source_target_pairs={{0,16},{8,24},{16,0},{24,8},{32,48},{40,56},{48,32},{56,40},{64,80... | collective-permute-start | bytes 196616 | tf_op jit(solution)/shard_map/ppermute | solution.py:332
  87.7 2.4 %collective-permute-done.5.refs_1_ = bf16[256,128]{1,0:T(8,128)(2,1)S(1)} collective-permute-done((bf16[256,128]{1,0:T(8,128)(2,1)S(1)}, bf16[256,128]{1,0:T(8,128)(2,1)S(1)}, u32[]{:S(2)}, u32[]{:S(2)}) %collective-permute-start.5) | collective-permute-done | bytes 65568 | tf_op jit(solution)/shard_map/ppermute | solution.py:332
  90.2 3.3 %collective-permute-start.6 = (bf16[512,128]{1,0:T(8,128)(2,1)S(1)}, bf16[512,128]{1,0:T(8,128)(2,1)S(1)}, u32[]{:S(2)}, u32[]{:S(2)}) collective-permute-start(bf16[512,128]{1,0:T(8,128)(2,1)S(1)} %get-tuple-element.83), channel_id=1, source_target_pairs={{0,8},{8,0},{16,24},{24,16},{32,40},{40,32},{48,56},{56,48},{64,72... | collective-permute-start | bytes 393224 | tf_op jit(solution)/shard_map/ppermute | solution.py:332
  93.4 3.7 %collective-permute-start.21 = (bf16[512,128]{1,0:T(8,128)(2,1)S(1)}, bf16[512,128]{1,0:T(8,128)(2,1)S(1)}, u32[]{:S(2)}, u32[]{:S(2)}) collective-permute-start(bf16[512,128]{1,0:T(8,128)(2,1)S(1)} %collective-permute-done.20.refs_1_), channel_id=1, source_target_pairs={{8,0},{16,8},{24,16},{32,24},{40,32},{48,40},{56,48},{64,56},{72,6... | collective-permute-start | bytes 393224 | tf_op jit(solution)/shard_map/ppermute | solution.py:332
  97.1 0.7 collective-permute-start.14
  97.8 0.9 shard_map.113
  98.8 0.7 copy-done.7
  99.4 1.0 shard_map.105
  100.5 1.4 %shard_map.112 = bf16[256,1024]{1,0:T(8,128)(2,1)} custom-call(f32[256,128]{1,0:T(8,128)S(1)} %get-tuple-element.56.live_ref, bf16[256,1024]{1,0:T(8,128)(2,1)S(1)} %get-tuple-element.60.q_ref, f32[256,1024]{1,0:T(8,128)S(1)} %get-tuple-element.61.inside_ref, f32[4,128,128]{2,1,0:T(8,128)S(1)} %get-tuple-element.82.held_ref, ...), custom_call_target="tpu_custom_call" | custom-call | flops 2000000 | bytes 1048576 | tf_op jit(solution)/shard_map/pallas_call | solution.py:24
  101.9 1.2 %shard_map.121 = bf16[256,1024]{1,0:T(8,128)(2,1)} custom-call(f32[24,256]{1,0:T(8,128)S(1)} %get-tuple-element.57.bias_ref, f32[256,128]{1,0:T(8,128)S(1)} %get-tuple-element.56.live_ref, bf16[2048,256]{1,0:T(8,128)(2,1)S(1)} %get-tuple-element.85.q2_ref, bf16[512,128]{1,0:T(8,128)(2,1)S(1)} %collective-permute-done.14.f_ref, ...), custom_call_target="tpu_custom_call" | custom-call | flops 2000000 | bytes 1048576 | tf_op jit(solution)/shard_map/pallas_call | solution.py:24
  (50 shorter events, 0.9 us)
Async XLA Ops:
  0.6 0.9 copy-start.5
  1.5 45.0 %copy-start.6 = (f32[256,8]{0,1:T(8,128)S(1)}, f32[256,8]{0,1:T(8,128)}, u32[]{:S(2)}) copy-start(f32[256,8]{0,1:T(8,128)} %param.12) | copy-start | bytes 24580
  1.5 26.1 %collective-permute-start.7 = (bf16[512,128]{1,0:T(8,128)(2,1)S(1)}, bf16[512,128]{1,0:T(8,128)(2,1)S(1)}, u32[]{:S(2)}, u32[]{:S(2)}) collective-permute-start(bf16[512,128]{1,0:T(8,128)(2,1)S(1)} %constant_dynamic-update-slice_fusion), channel_id=1, source_target_pairs={{0,8},{8,16},{16,24},{24,32},{32,40},{40,48},{48,56},{56,64},{64,7... | collective-permute-start | bytes 393224 | tf_op jit(solution)/shard_map/ppermute | solution.py:332
  4.4 23.2 %collective-permute-start.15 = (bf16[512,128]{1,0:T(8,128)(2,1)S(1)}, bf16[512,128]{1,0:T(8,128)(2,1)S(1)}, u32[]{:S(2)}, u32[]{:S(2)}) collective-permute-start(bf16[512,128]{1,0:T(8,128)(2,1)S(1)} %constant_dynamic-update-slice_fusion), channel_id=1, source_target_pairs={{8,0},{16,8},{24,16},{32,24},{40,32},{48,40},{56,48},{64,56},{72,6... | collective-permute-start | bytes 393224 | tf_op jit(solution)/shard_map/ppermute | solution.py:332
  27.6 6.2 %collective-permute-start.8 = (bf16[512,128]{1,0:T(8,128)(2,1)S(1)}, bf16[512,128]{1,0:T(8,128)(2,1)S(1)}, u32[]{:S(2)}, u32[]{:S(2)}) collective-permute-start(bf16[512,128]{1,0:T(8,128)(2,1)S(1)} %collective-permute-done.7.refs_0_), channel_id=1, source_target_pairs={{0,8},{8,16},{16,24},{24,32},{32,40},{40,48},{48,56},{56,64},{64,7... | collective-permute-start | bytes 393224 | tf_op jit(solution)/shard_map/ppermute | solution.py:332
  27.6 6.2 %collective-permute-start.16 = (bf16[512,128]{1,0:T(8,128)(2,1)S(1)}, bf16[512,128]{1,0:T(8,128)(2,1)S(1)}, u32[]{:S(2)}, u32[]{:S(2)}) collective-permute-start(bf16[512,128]{1,0:T(8,128)(2,1)S(1)} %collective-permute-done.15.refs_1_), channel_id=1, source_target_pairs={{8,0},{16,8},{24,16},{32,24},{40,32},{48,40},{56,48},{64,56},{72,6... | collective-permute-start | bytes 393224 | tf_op jit(solution)/shard_map/ppermute | solution.py:332
  33.8 6.2 %collective-permute-start.9 = (bf16[512,128]{1,0:T(8,128)(2,1)S(1)}, bf16[512,128]{1,0:T(8,128)(2,1)S(1)}, u32[]{:S(2)}, u32[]{:S(2)}) collective-permute-start(bf16[512,128]{1,0:T(8,128)(2,1)S(1)} %collective-permute-done.8.refs_0_), channel_id=1, source_target_pairs={{0,8},{8,16},{16,24},{24,32},{32,40},{40,48},{48,56},{56,64},{64,7... | collective-permute-start | bytes 393224 | tf_op jit(solution)/shard_map/ppermute | solution.py:332
  33.8 6.2 %collective-permute-start.17 = (bf16[512,128]{1,0:T(8,128)(2,1)S(1)}, bf16[512,128]{1,0:T(8,128)(2,1)S(1)}, u32[]{:S(2)}, u32[]{:S(2)}) collective-permute-start(bf16[512,128]{1,0:T(8,128)(2,1)S(1)} %collective-permute-done.16.refs_1_), channel_id=1, source_target_pairs={{8,0},{16,8},{24,16},{32,24},{40,32},{48,40},{56,48},{64,56},{72,6... | collective-permute-start | bytes 393224 | tf_op jit(solution)/shard_map/ppermute | solution.py:332
  40.0 6.5 %collective-permute-start.10 = (bf16[512,128]{1,0:T(8,128)(2,1)S(1)}, bf16[512,128]{1,0:T(8,128)(2,1)S(1)}, u32[]{:S(2)}, u32[]{:S(2)}) collective-permute-start(bf16[512,128]{1,0:T(8,128)(2,1)S(1)} %collective-permute-done.9.refs_0_), channel_id=1, source_target_pairs={{0,8},{8,16},{16,24},{24,32},{32,40},{40,48},{48,56},{56,64},{64,7... | collective-permute-start | bytes 393224 | tf_op jit(solution)/shard_map/ppermute | solution.py:332
  40.0 9.3 %collective-permute-start.18 = (bf16[512,128]{1,0:T(8,128)(2,1)S(1)}, bf16[512,128]{1,0:T(8,128)(2,1)S(1)}, u32[]{:S(2)}, u32[]{:S(2)}) collective-permute-start(bf16[512,128]{1,0:T(8,128)(2,1)S(1)} %collective-permute-done.17.refs_1_), channel_id=1, source_target_pairs={{8,0},{16,8},{24,16},{32,24},{40,32},{48,40},{56,48},{64,56},{72,6... | collective-permute-start | bytes 393224 | tf_op jit(solution)/shard_map/ppermute | solution.py:332
  46.5 7.4 %collective-permute-start.11 = (bf16[512,128]{1,0:T(8,128)(2,1)S(1)}, bf16[512,128]{1,0:T(8,128)(2,1)S(1)}, u32[]{:S(2)}, u32[]{:S(2)}) collective-permute-start(bf16[512,128]{1,0:T(8,128)(2,1)S(1)} %collective-permute-done.10.refs_0_), channel_id=1, source_target_pairs={{0,8},{8,16},{16,24},{24,32},{32,40},{40,48},{48,56},{56,64},{64,7... | collective-permute-start | bytes 393224 | tf_op jit(solution)/shard_map/ppermute | solution.py:332
  46.5 0.7 copy-start.8
  49.2 5.9 %collective-permute-start = (bf16[544,128]{1,0:T(8,128)(2,1)S(1)}, bf16[544,128]{1,0:T(8,128)(2,1)S(1)}, u32[]{:S(2)}, u32[]{:S(2)}) collective-permute-start(bf16[544,128]{1,0:T(8,128)(2,1)S(1)} %get-tuple-element.62), channel_id=1, source_target_pairs={{0,8},{8,0},{16,24},{24,16},{32,40},{40,32},{48,56},{56,48},{64,72... | collective-permute-start | bytes 417800 | tf_op jit(solution)/shard_map/ppermute | solution.py:332
  49.3 23.4 %collective-permute-start.19 = (bf16[512,128]{1,0:T(8,128)(2,1)S(1)}, bf16[512,128]{1,0:T(8,128)(2,1)S(1)}, u32[]{:S(2)}, u32[]{:S(2)}) collective-permute-start(bf16[512,128]{1,0:T(8,128)(2,1)S(1)} %collective-permute-done.18.refs_1_), channel_id=1, source_target_pairs={{8,0},{16,8},{24,16},{32,24},{40,32},{48,40},{56,48},{64,56},{72,6... | collective-permute-start | bytes 393224 | tf_op jit(solution)/shard_map/ppermute | solution.py:332
  53.8 21.0 %collective-permute-start.12 = (bf16[512,128]{1,0:T(8,128)(2,1)S(1)}, bf16[512,128]{1,0:T(8,128)(2,1)S(1)}, u32[]{:S(2)}, u32[]{:S(2)}) collective-permute-start(bf16[512,128]{1,0:T(8,128)(2,1)S(1)} %collective-permute-done.11.refs_0_), channel_id=1, source_target_pairs={{0,8},{8,16},{16,24},{24,32},{32,40},{40,48},{48,56},{56,64},{64,7... | collective-permute-start | bytes 393224 | tf_op jit(solution)/shard_map/ppermute | solution.py:332
  55.1 43.7 %copy-start.3 = (bf16[256,1024]{1,0:T(8,128)(2,1)S(1)}, bf16[256,1024]{1,0:T(8,128)(2,1)}, u32[]{:S(2)}) copy-start(bf16[256,1024]{1,0:T(8,128)(2,1)} %q_ref.2) | copy-start | bytes 1572868
  55.2 6.5 %collective-permute-start.1 = (bf16[288,128]{1,0:T(8,128)(2,1)S(1)}, bf16[288,128]{1,0:T(8,128)(2,1)S(1)}, u32[]{:S(2)}, u32[]{:S(2)}) collective-permute-start(bf16[288,128]{1,0:T(8,128)(2,1)S(1)} %get-tuple-element.65), channel_id=1, source_target_pairs={{0,16},{8,24},{16,0},{24,8},{32,48},{40,56},{48,32},{56,40},{64,80... | collective-permute-start | bytes 221192 | tf_op jit(solution)/shard_map/ppermute | solution.py:332
  61.7 36.1 %copy-start.2 = (bf16[256,1024]{1,0:T(8,128)(2,1)S(1)}, bf16[256,1024]{1,0:T(8,128)(2,1)}, u32[]{:S(2)}) copy-start(bf16[256,1024]{1,0:T(8,128)(2,1)} %q_ref.3) | copy-start | bytes 1572868
  61.8 8.0 %collective-permute-start.2 = (bf16[160,128]{1,0:T(8,128)(2,1)S(1)}, bf16[160,128]{1,0:T(8,128)(2,1)S(1)}, u32[]{:S(2)}, u32[]{:S(2)}) collective-permute-start(bf16[160,128]{1,0:T(8,128)(2,1)S(1)} %get-tuple-element.68), channel_id=1, source_target_pairs={{0,32},{8,40},{16,48},{24,56},{32,0},{40,8},{48,16},{56,24},{64,96... | collective-permute-start | bytes 122888 | tf_op jit(solution)/shard_map/ppermute | solution.py:332
  69.8 5.9 %collective-permute-start.3 = (bf16[128,128]{1,0:T(8,128)(2,1)S(1)}, bf16[128,128]{1,0:T(8,128)(2,1)S(1)}, u32[]{:S(2)}, u32[]{:S(2)}) collective-permute-start(bf16[128,128]{1,0:T(8,128)(2,1)S(1)} %get-tuple-element.71), channel_id=1, source_target_pairs={{0,96},{8,104},{16,112},{24,120},{32,64},{40,72},{48,80},{56,88},{... | collective-permute-start | bytes 98312 | tf_op jit(solution)/shard_map/ppermute | solution.py:332
  72.7 20.7 %collective-permute-start.20 = (bf16[512,128]{1,0:T(8,128)(2,1)S(1)}, bf16[512,128]{1,0:T(8,128)(2,1)S(1)}, u32[]{:S(2)}, u32[]{:S(2)}) collective-permute-start(bf16[512,128]{1,0:T(8,128)(2,1)S(1)} %collective-permute-done.19.refs_1_), channel_id=1, source_target_pairs={{8,0},{16,8},{24,16},{32,24},{40,32},{48,40},{56,48},{64,56},{72,6... | collective-permute-start | bytes 393224 | tf_op jit(solution)/shard_map/ppermute | solution.py:332
  74.8 22.4 %collective-permute-start.13 = (bf16[512,128]{1,0:T(8,128)(2,1)S(1)}, bf16[512,128]{1,0:T(8,128)(2,1)S(1)}, u32[]{:S(2)}, u32[]{:S(2)}) collective-permute-start(bf16[512,128]{1,0:T(8,128)(2,1)S(1)} %collective-permute-done.12.refs_0_), channel_id=1, source_target_pairs={{0,8},{8,16},{16,24},{24,32},{32,40},{40,48},{48,56},{56,64},{64,7... | collective-permute-start | bytes 393224 | tf_op jit(solution)/shard_map/ppermute | solution.py:332
  75.8 8.9 %collective-permute-start.4 = (bf16[128,128]{1,0:T(8,128)(2,1)S(1)}, bf16[128,128]{1,0:T(8,128)(2,1)S(1)}, u32[]{:S(2)}, u32[]{:S(2)}) collective-permute-start(bf16[128,128]{1,0:T(8,128)(2,1)S(1)} %get-tuple-element.75), channel_id=1, source_target_pairs={{0,32},{8,40},{16,48},{24,56},{32,0},{40,8},{48,16},{56,24},{64,96... | collective-permute-start | bytes 98312 | tf_op jit(solution)/shard_map/ppermute | solution.py:332
  84.7 13.1 %copy-start.4 = (bf16[256,128]{1,0:T(8,128)(2,1)S(1)}, bf16[256,128]{1,0:T(8,128)(2,1)}, u32[]{:S(2)}) copy-start(bf16[256,128]{1,0:T(8,128)(2,1)} %k_ref.3) | copy-start | bytes 196612
  84.8 5.3 %collective-permute-start.5 = (bf16[256,128]{1,0:T(8,128)(2,1)S(1)}, bf16[256,128]{1,0:T(8,128)(2,1)S(1)}, u32[]{:S(2)}, u32[]{:S(2)}) collective-permute-start(bf16[256,128]{1,0:T(8,128)(2,1)S(1)} %get-tuple-element.79), channel_id=1, source_target_pairs={{0,16},{8,24},{16,0},{24,8},{32,48},{40,56},{48,32},{56,40},{64,80... | collective-permute-start | bytes 196616 | tf_op jit(solution)/shard_map/ppermute | solution.py:332
  90.1 8.7 %copy-start = (bf16[256,1024]{1,0:T(8,128)(2,1)S(1)}, bf16[256,1024]{1,0:T(8,128)(2,1)}, u32[]{:S(2)}) copy-start(bf16[256,1024]{1,0:T(8,128)(2,1)} %k_ref.2) | copy-start | bytes 1572868
  90.1 8.7 %copy-start.1 = (bf16[256,1024]{1,0:T(8,128)(2,1)S(1)}, bf16[256,1024]{1,0:T(8,128)(2,1)}, u32[]{:S(2)}) copy-start(bf16[256,1024]{1,0:T(8,128)(2,1)} %v_ref.2) | copy-start | bytes 1572868
  90.2 10.4 %collective-permute-start.6 = (bf16[512,128]{1,0:T(8,128)(2,1)S(1)}, bf16[512,128]{1,0:T(8,128)(2,1)S(1)}, u32[]{:S(2)}, u32[]{:S(2)}) collective-permute-start(bf16[512,128]{1,0:T(8,128)(2,1)S(1)} %get-tuple-element.83), channel_id=1, source_target_pairs={{0,8},{8,0},{16,24},{24,16},{32,40},{40,32},{48,56},{56,48},{64,72... | collective-permute-start | bytes 393224 | tf_op jit(solution)/shard_map/ppermute | solution.py:332
  93.4 8.5 %collective-permute-start.21 = (bf16[512,128]{1,0:T(8,128)(2,1)S(1)}, bf16[512,128]{1,0:T(8,128)(2,1)S(1)}, u32[]{:S(2)}, u32[]{:S(2)}) collective-permute-start(bf16[512,128]{1,0:T(8,128)(2,1)S(1)} %collective-permute-done.20.refs_1_), channel_id=1, source_target_pairs={{8,0},{16,8},{24,16},{32,24},{40,32},{48,40},{56,48},{64,56},{72,6... | collective-permute-start | bytes 393224 | tf_op jit(solution)/shard_map/ppermute | solution.py:332
  97.1 4.8 %collective-permute-start.14 = (bf16[512,128]{1,0:T(8,128)(2,1)S(1)}, bf16[512,128]{1,0:T(8,128)(2,1)S(1)}, u32[]{:S(2)}, u32[]{:S(2)}) collective-permute-start(bf16[512,128]{1,0:T(8,128)(2,1)S(1)} %collective-permute-done.13.refs_0_), channel_id=1, source_target_pairs={{56,64},{64,72},{72,80},{80,88},{88,96},{96,104},{104,112},{112,12... | collective-permute-start | bytes 393224 | tf_op jit(solution)/shard_map/ppermute | solution.py:332
  98.7 0.7 copy-start.7

commit v4 on v3

--- a/solution.py
+++ b/solution.py
@@ -37,16 +37,10 @@
     return lax.shift_right_logical(i, level) & 1
 
 
-def keep_bit(i, level):
-    return bit(i, level) ^ (bit(i, 3) if level == 2 else 0)
-
-
 def first_head(i, level):
-    start = keep_bit(i, 0) * 4
+    start = bit(i, 0) * 4
     if level >= 1:
-        start += keep_bit(i, 1) * 2
-    if level >= 2:
-        start += keep_bit(i, 2)
+        start += bit(i, 1) * 2
     return start
 
 
@@ -107,7 +101,7 @@
         kt = k_ref[:, h * width : (h + 1) * width].T.astype(F32)
         scaled = (kt * fading[h : h + 1, :]).astype(BF16)
         states[h] = jnp.dot(scaled, v_ref[:, h * width : (h + 1) * width], preferred_element_type=F32)
-    keep = keep_bit(i, 0) * half
+    keep = bit(i, 0) * half
     send = half - keep
     for h in range(half):
         kept_ref[h] = states[keep + h]
@@ -126,8 +120,6 @@
     grown = jnp.exp(jnp.where(upper, own, other))
     start = first_head(i, level)
     which = lax.broadcasted_iota(jnp.int32, grown.shape, 0)
-    half = count // 2
-    keep = keep_bit(i, level + 1) * half
     totals = []
     for h in range(count):
         factor = jnp.sum(jnp.where(which == start + h, grown, 0.0), axis=0, keepdims=True)
@@ -137,37 +129,56 @@
         high = jnp.where(upper, mine, got)
         low_ref[h] = low
         totals.append(factor * low + high)
-    if count == 1:
-        msg_ref[...] = totals[0].astype(BF16)
+    if level > 0:
+        for h in range(count):
+            msg_ref[h * width : (h + 1) * width, :] = totals[h].astype(BF16)
+        if level == 1:
+            for h in range(count):
+                next_ref[h] = totals[h]
+            sum_ref[...] = own + other
+            put_logs(msg_ref, count * width, own + other)
         return
     sum_ref[...] = own + other
-    first = keep == 0
+    half = count // 2
+    first = bit(i, 1) == 0
     for h in range(half):
         next_ref[h] = jnp.where(first, totals[h], totals[half + h])
         msg_ref[h * width : (h + 1) * width, :] = jnp.where(first, totals[half + h], totals[h]).astype(BF16)
     put_logs(msg_ref, half * width, own + other)
 
 
-def down_kernel(level, top, *refs):
-    if top:
-        recv_ref, low_ref, lowlog_ref, mine_ref, msg_ref = refs
-    else:
-        held_ref, recv_ref, low_ref, lowlog_ref, mine_ref, msg_ref = refs
+def middle_kernel(recv_ref, low2_ref, log2_ref, low1_ref, log1_ref, mine_ref, msg_ref):
+    i = lax.axis_index("seq")
+    count, width = low1_ref.shape[0], low1_ref.shape[1]
+    start = first_head(i, 1)
+    which = lax.broadcasted_iota(jnp.int32, log1_ref.shape, 0)
+    grown2 = jnp.exp(log2_ref[...])
+    grown1 = jnp.exp(log1_ref[...])
+    upper1 = bit(i, 1) == 1
+    upper2 = bit(i, 2) == 1
+    for h in range(count):
+        factor2 = jnp.sum(jnp.where(which == start + h, grown2, 0.0), axis=0, keepdims=True)
+        factor1 = jnp.sum(jnp.where(which == start + h, grown1, 0.0), axis=0, keepdims=True)
+        low = recv_ref[h * width : (h + 1) * width, :].astype(F32)
+        low = jnp.where(upper2, factor2 * low + low2_ref[h], low)
+        high = factor1 * low + low1_ref[h]
+        mine_ref[h] = jnp.where(upper1, high, low)
+        msg_ref[h * width : (h + 1) * width, :] = jnp.where(upper1, low, high).astype(BF16)
+
+
+def down_kernel(held_ref, recv_ref, low_ref, lowlog_ref, mine_ref, msg_ref):
     i = lax.axis_index("seq")
     count, width = low_ref.shape[0], low_ref.shape[1]
     half = count // 2
-    upper = bit(i, level) == 1
+    upper = bit(i, 0) == 1
     grown = jnp.exp(lowlog_ref[...])
-    start = first_head(i, level)
+    start = first_head(i, 0)
     which = lax.broadcasted_iota(jnp.int32, grown.shape, 0)
-    if top:
-        entering = [recv_ref[...].astype(F32)]
-    else:
-        first = keep_bit(i, level + 1) == 0
-        held = [held_ref[h] for h in range(half)]
-        got = [recv_ref[h * width : (h + 1) * width, :].astype(F32) for h in range(half)]
-        entering = [jnp.where(first, a, b) for a, b in zip(held, got)]
-        entering += [jnp.where(first, b, a) for a, b in zip(held, got)]
+    first = bit(i, 1) == 0
+    held = [held_ref[h] for h in range(half)]
+    got = [recv_ref[h * width : (h + 1) * width, :].astype(F32) for h in range(half)]
+    entering = [jnp.where(first, a, b) for a, b in zip(held, got)]
+    entering += [jnp.where(first, b, a) for a, b in zip(held, got)]
     for h in range(count):
         factor = jnp.sum(jnp.where(which == start + h, grown, 0.0), axis=0, keepdims=True)
         low = entering[h]
@@ -204,7 +215,7 @@
 def light_kernel(live_ref, q_ref, inside_ref, held_ref, recv_ref, gain_ref, out_ref):
     i = lax.axis_index("seq")
     half, width = held_ref.shape[0], held_ref.shape[1]
-    first = keep_bit(i, 0) == 0
+    first = bit(i, 0) == 0
     live = live_ref[...] > 0.0
     for h in range(2 * half):
         at = slice(h * width, (h + 1) * width)
@@ -362,30 +373,29 @@
     n = half
     for level in range(3):
         recv = exchange(msg, 1 << level)
-        m = max(n // 2, 1)
-        tail = E_ROWS if n > 1 else 0
-        onward = [((m, width, width), F32), ((heads, 128), F32)] if n > 1 else []
+        m = n // 2 if level == 0 else n
+        tail = E_ROWS if level < 2 else 0
+        onward = [((m, width, width), F32), ((heads, 128), F32)] if level < 2 else []
         msg, low, low_logs, *rest = call(
             partial(up_kernel, level),
             [((m * width + tail, width), BF16), ((n, width, width), F32), ((heads, 128), F32)] + onward,
             [(False, recv), (False, kept), (False, logs)],
         )
-        saved.append((low, low_logs))
-        n //= 2
-        if n:
+        saved.append(((False, low), (False, low_logs)))
+        n = m
+        if level < 2:
             kept, logs = rest
     recv = send(msg, [(i, (i + 4 if i >= 4 else i - 4) % count) for i in range(count // 2)])
-    held = None
-    for level in (2, 1, 0):
-        low, low_logs = saved[level]
-        n = low.shape[0]
-        ins = [(False, recv), (False, low), (False, low_logs)]
-        if held is not None:
-            ins = [(False, held)] + ins
-        held, msg = call(
-            partial(down_kernel, level, held is None), [((n, width, width), F32), ((n * width, width), BF16)], ins
-        )
-        recv = exchange(msg, 1 << level)
+    held, msg = call(
+        middle_kernel, [((n, width, width), F32), ((n * width, width), BF16)], [(False, recv), *saved[2], *saved[1]]
+    )
+    recv = exchange(msg, 2)
+    held, msg = call(
+        down_kernel,
+        [((half, width, width), F32), ((half * width, width), BF16)],
+        [(False, held), (False, recv), *saved[0]],
+    )
+    recv = exchange(msg, 1)
     inside, scaled, gain = call(
         inside_kernel,
         [((rows, heads * width), F32), ((rows, heads * width), BF16), ((1, heads * width), F32)],

time: 103 us -> 91.3 us (0.89)
  starting transfers between devices: 58.3 us -> 51.2 us
  waiting for transfers between devices: 34.9 us -> 29.9 us
    ppermute x22 -> x21, starting transfers between devices: 58.3 us -> 51.2 us  [send(): return lax.ppermute(x, 'seq', pairs)]
    ppermute x22 -> x21, waiting for transfers between devices: 34.9 us -> 29.9 us  [send(): return lax.ppermute(x, 'seq', pairs)]
    pallas_call x18 -> x17, Pallas kernels: 6.83 us -> 6.85 us  [call(): pl.pallas_call(kernel, out_shape=outs, in_specs=specs, out_specs=[VMEM] *...]
  transfers between devices with their start and end apart: 22 -> 21, of which waited for: 10 -> 9; matrix products, arithmetic and copies ran while one was open for 0% -> 0% of each run, Pallas kernels for 5% -> 6%
where the time goes in v4:
time: 91.3 us; the launch traced here: 91 us
  starting transfers between devices  51.2 us (56%)
  waiting for transfers between devices  29.9 us (33%)
  Pallas kernels  6.85 us (8%)
  local copies, waits for them, and re-layouts  2.23 us (2%)
    ppermute x21, starting transfers between devices, send(): return lax.ppermute(x, 'seq', pairs)  51.2 us
    ppermute x21, waiting for transfers between devices, send(): return lax.ppermute(x, 'seq', pairs)  29.9 us
    pallas_call x17, Pallas kernels, call(): pl.pallas_call(kernel, out_shape=outs, in_specs=specs, out_specs=[VMEM] *...  6.85 us
    unnamed x19, local copies, waits for them, and re-layouts  2.21 us
  transfers between devices with their start and end apart: 21, of which 9 were waited for; matrix products, arithmetic and copies ran while one was open for 0% of the time, Pallas kernels for 6%

profile of v4, /device:TPU:36, one launch (start us, length us, event | category | flops | bytes accessed | tf_op | source)
XLA Modules:
  0.0 91.0 jit_solution(3912770155221340749)
XLA Ops:
  0.6 0.9 constant_dynamic-update-slice_fusion.1
  1.5 2.9 %collective-permute-start.6 = (bf16[512,128]{1,0:T(8,128)(2,1)S(1)}, bf16[512,128]{1,0:T(8,128)(2,1)S(1)}, u32[]{:S(2)}, u32[]{:S(2)}) collective-permute-start(bf16[512,128]{1,0:T(8,128)(2,1)S(1)} %constant_dynamic-update-slice_fusion), channel_id=1, source_target_pairs={{0,8},{8,16},{16,24},{24,32},{32,40},{40,48},{48,56},{56,64},{64,7... | collective-permute-start | bytes 393224 | tf_op jit(solution)/shard_map/ppermute | solution.py:343
  4.4 19.7 %collective-permute-start.14 = (bf16[512,128]{1,0:T(8,128)(2,1)S(1)}, bf16[512,128]{1,0:T(8,128)(2,1)S(1)}, u32[]{:S(2)}, u32[]{:S(2)}) collective-permute-start(bf16[512,128]{1,0:T(8,128)(2,1)S(1)} %constant_dynamic-update-slice_fusion), channel_id=1, source_target_pairs={{8,0},{16,8},{24,16},{32,24},{40,32},{48,40},{56,48},{64,56},{72,6... | collective-permute-start | bytes 393224 | tf_op jit(solution)/shard_map/ppermute | solution.py:343
  24.2 3.4 %collective-permute-done.6.refs_0_ = bf16[512,128]{1,0:T(8,128)(2,1)S(1)} collective-permute-done((bf16[512,128]{1,0:T(8,128)(2,1)S(1)}, bf16[512,128]{1,0:T(8,128)(2,1)S(1)}, u32[]{:S(2)}, u32[]{:S(2)}) %collective-permute-start.6) | collective-permute-done | bytes 131104 | tf_op jit(solution)/shard_map/ppermute | solution.py:343
  27.6 3.2 %collective-permute-start.15 = (bf16[512,128]{1,0:T(8,128)(2,1)S(1)}, bf16[512,128]{1,0:T(8,128)(2,1)S(1)}, u32[]{:S(2)}, u32[]{:S(2)}) collective-permute-start(bf16[512,128]{1,0:T(8,128)(2,1)S(1)} %collective-permute-done.14.refs_1_), channel_id=1, source_target_pairs={{8,0},{16,8},{24,16},{32,24},{40,32},{48,40},{56,48},{64,56},{72,6... | collective-permute-start | bytes 393224 | tf_op jit(solution)/shard_map/ppermute | solution.py:343
  30.9 2.9 %collective-permute-done.7.refs_0_ = bf16[512,128]{1,0:T(8,128)(2,1)S(1)} collective-permute-done((bf16[512,128]{1,0:T(8,128)(2,1)S(1)}, bf16[512,128]{1,0:T(8,128)(2,1)S(1)}, u32[]{:S(2)}, u32[]{:S(2)}) %collective-permute-start.7) | collective-permute-done | bytes 131104 | tf_op jit(solution)/shard_map/ppermute | solution.py:343
  33.8 3.2 %collective-permute-start.16 = (bf16[512,128]{1,0:T(8,128)(2,1)S(1)}, bf16[512,128]{1,0:T(8,128)(2,1)S(1)}, u32[]{:S(2)}, u32[]{:S(2)}) collective-permute-start(bf16[512,128]{1,0:T(8,128)(2,1)S(1)} %collective-permute-done.15.refs_1_), channel_id=1, source_target_pairs={{8,0},{16,8},{24,16},{32,24},{40,32},{48,40},{56,48},{64,56},{72,6... | collective-permute-start | bytes 393224 | tf_op jit(solution)/shard_map/ppermute | solution.py:343
  37.0 2.9 %collective-permute-done.8.refs_0_ = bf16[512,128]{1,0:T(8,128)(2,1)S(1)} collective-permute-done((bf16[512,128]{1,0:T(8,128)(2,1)S(1)}, bf16[512,128]{1,0:T(8,128)(2,1)S(1)}, u32[]{:S(2)}, u32[]{:S(2)}) %collective-permute-start.8) | collective-permute-done | bytes 131104 | tf_op jit(solution)/shard_map/ppermute | solution.py:343
  40.0 0.6 copy-done.8
  40.6 2.0 %shard_map.104 = (bf16[544,128]{1,0:T(8,128)(2,1)S(1)}, f32[4,128,128]{2,1,0:T(8,128)S(1)}, f32[8,128]{1,0:T(8,128)S(1)}, f32[8,256]{1,0:T(8,128)S(1)}, f32[256,...) custom-call(s32[1,16]{1,0:T(1,128)S(1)} %bitcast.5, bf16[256,1024]{1,0:T(8,128)(2,1)} %k_ref.2, ...), custom_call_target="tpu_custom_call" | custom-call | flops 2000000 | bytes 1048576 | tf_op jit(solution)/shard_map/pallas_call | solution.py:24
  42.8 3.4 %collective-permute-start.17 = (bf16[512,128]{1,0:T(8,128)(2,1)S(1)}, bf16[512,128]{1,0:T(8,128)(2,1)S(1)}, u32[]{:S(2)}, u32[]{:S(2)}) collective-permute-start(bf16[512,128]{1,0:T(8,128)(2,1)S(1)} %collective-permute-done.16.refs_1_), channel_id=1, source_target_pairs={{8,0},{16,8},{24,16},{32,24},{40,32},{48,40},{56,48},{64,56},{72,6... | collective-permute-start | bytes 393224 | tf_op jit(solution)/shard_map/ppermute | solution.py:343
  46.2 2.6 %collective-permute-done.recv_ref = bf16[544,128]{1,0:T(8,128)(2,1)S(1)} collective-permute-done((bf16[544,128]{1,0:T(8,128)(2,1)S(1)}, bf16[544,128]{1,0:T(8,128)(2,1)S(1)}, u32[]{:S(2)}, u32[]{:S(2)}) %collective-permute-start) | collective-permute-done | bytes 139296 | tf_op jit(solution)/shard_map/ppermute | solution.py:343
  48.8 0.1 collective-permute-start.1
  49.0 2.5 %collective-permute-done.17.refs_1_ = bf16[512,128]{1,0:T(8,128)(2,1)S(1)} collective-permute-done((bf16[512,128]{1,0:T(8,128)(2,1)S(1)}, bf16[512,128]{1,0:T(8,128)(2,1)S(1)}, u32[]{:S(2)}, u32[]{:S(2)}) %collective-permute-start.17) | collective-permute-done | bytes 131104 | tf_op jit(solution)/shard_map/ppermute | solution.py:343
  51.4 1.5 %collective-permute-start.18 = (bf16[512,128]{1,0:T(8,128)(2,1)S(1)}, bf16[512,128]{1,0:T(8,128)(2,1)S(1)}, u32[]{:S(2)}, u32[]{:S(2)}) collective-permute-start(bf16[512,128]{1,0:T(8,128)(2,1)S(1)} %collective-permute-done.17.refs_1_), channel_id=1, source_target_pairs={{8,0},{16,8},{24,16},{32,24},{40,32},{48,40},{56,48},{64,56},{72,6... | collective-permute-start | bytes 393224 | tf_op jit(solution)/shard_map/ppermute | solution.py:343
  52.9 0.3 collective-permute-done.10.refs_0_
  53.2 0.2 collective-permute-start.11
  53.5 1.5 %collective-permute-done.1.recv_ref = bf16[288,128]{1,0:T(8,128)(2,1)S(1)} collective-permute-done((bf16[288,128]{1,0:T(8,128)(2,1)S(1)}, bf16[288,128]{1,0:T(8,128)(2,1)S(1)}, u32[]{:S(2)}, u32[]{:S(2)}) %collective-permute-start.1) | collective-permute-done | bytes 73760 | tf_op jit(solution)/shard_map/ppermute | solution.py:343
  55.2 10.0 %collective-permute-done.2.recv_ref = bf16[288,128]{1,0:T(8,128)(2,1)S(1)} collective-permute-done((bf16[288,128]{1,0:T(8,128)(2,1)S(1)}, bf16[288,128]{1,0:T(8,128)(2,1)S(1)}, u32[]{:S(2)}, u32[]{:S(2)}) %collective-permute-start.2) | collective-permute-done | bytes 73760 | tf_op jit(solution)/shard_map/ppermute | solution.py:343
  65.2 2.3 %collective-permute-start.3 = (bf16[256,128]{1,0:T(8,128)(2,1)S(1)}, bf16[256,128]{1,0:T(8,128)(2,1)S(1)}, u32[]{:S(2)}, u32[]{:S(2)}) collective-permute-start(bf16[256,128]{1,0:T(8,128)(2,1)S(1)} %get-tuple-element.69), channel_id=1, source_target_pairs={{0,96},{8,104},{16,112},{24,120},{32,64},{40,72},{48,80},{56,88},{... | collective-permute-start | bytes 196616 | tf_op jit(solution)/shard_map/ppermute | solution.py:343
  67.5 2.6 %collective-permute-start.19 = (bf16[512,128]{1,0:T(8,128)(2,1)S(1)}, bf16[512,128]{1,0:T(8,128)(2,1)S(1)}, u32[]{:S(2)}, u32[]{:S(2)}) collective-permute-start(bf16[512,128]{1,0:T(8,128)(2,1)S(1)} %collective-permute-done.18.refs_1_), channel_id=1, source_target_pairs={{8,0},{16,8},{24,16},{32,24},{40,32},{48,40},{56,48},{64,56},{72,6... | collective-permute-start | bytes 393224 | tf_op jit(solution)/shard_map/ppermute | solution.py:343
  70.2 1.0 %collective-permute-start.12 = (bf16[512,128]{1,0:T(8,128)(2,1)S(1)}, bf16[512,128]{1,0:T(8,128)(2,1)S(1)}, u32[]{:S(2)}, u32[]{:S(2)}) collective-permute-start(bf16[512,128]{1,0:T(8,128)(2,1)S(1)} %collective-permute-done.11.refs_0_), channel_id=1, source_target_pairs={{0,8},{8,16},{16,24},{24,32},{32,40},{40,48},{48,56},{56,64},{64,7... | collective-permute-start | bytes 393224 | tf_op jit(solution)/shard_map/ppermute | solution.py:343
  71.3 3.7 %collective-permute-start.4 = (bf16[256,128]{1,0:T(8,128)(2,1)S(1)}, bf16[256,128]{1,0:T(8,128)(2,1)S(1)}, u32[]{:S(2)}, u32[]{:S(2)}) collective-permute-start(bf16[256,128]{1,0:T(8,128)(2,1)S(1)} %get-tuple-element.75), channel_id=1, source_target_pairs={{0,16},{8,24},{16,0},{24,8},{32,48},{40,56},{48,32},{56,40},{64,80... | collective-permute-start | bytes 196616 | tf_op jit(solution)/shard_map/ppermute | solution.py:343
  74.9 3.7 %collective-permute-done.4.recv_ref = bf16[256,128]{1,0:T(8,128)(2,1)S(1)} collective-permute-done((bf16[256,128]{1,0:T(8,128)(2,1)S(1)}, bf16[256,128]{1,0:T(8,128)(2,1)S(1)}, u32[]{:S(2)}, u32[]{:S(2)}) %collective-permute-start.4) | collective-permute-done | bytes 65568 | tf_op jit(solution)/shard_map/ppermute | solution.py:343
  78.8 1.9 %collective-permute-start.5 = (bf16[512,128]{1,0:T(8,128)(2,1)S(1)}, bf16[512,128]{1,0:T(8,128)(2,1)S(1)}, u32[]{:S(2)}, u32[]{:S(2)}) collective-permute-start(bf16[512,128]{1,0:T(8,128)(2,1)S(1)} %get-tuple-element.79), channel_id=1, source_target_pairs={{0,8},{8,0},{16,24},{24,16},{32,40},{40,32},{48,56},{56,48},{64,72... | collective-permute-start | bytes 393224 | tf_op jit(solution)/shard_map/ppermute | solution.py:343
  80.7 4.4 %collective-permute-start.20 = (bf16[512,128]{1,0:T(8,128)(2,1)S(1)}, bf16[512,128]{1,0:T(8,128)(2,1)S(1)}, u32[]{:S(2)}, u32[]{:S(2)}) collective-permute-start(bf16[512,128]{1,0:T(8,128)(2,1)S(1)} %collective-permute-done.19.refs_1_), channel_id=1, source_target_pairs={{8,0},{16,8},{24,16},{32,24},{40,32},{48,40},{56,48},{64,56},{72,6... | collective-permute-start | bytes 393224 | tf_op jit(solution)/shard_map/ppermute | solution.py:343
  85.0 0.7 collective-permute-start.13
  85.7 0.9 shard_map.112
  86.7 0.7 copy-done.7
  87.3 1.0 %shard_map.105 = (f32[256,1024]{1,0:T(8,128)S(1)}, bf16[256,1024]{1,0:T(8,128)(2,1)S(1)}, f32[1,1024]{1,0:T(1,128)S(1)}) custom-call(f32[24,256]{1,0:T(8,128)S(1)} %get-tuple-element.55.bias_ref, bf16[256,1024]{1,0:T(8,128)(2,1)S(1)} %copy-done.3, bf16[256,1024]{1,0:T(8,128)(2,1)S(1)} %copy-done, bf16[256,1024]{1,0:T(8,128)(2,1)S(1)} %copy-done.1, ...), custom_call_target="tpu_custom_call" | custom-call | flops 2000000 | bytes 1048576 | tf_op jit(solution)/shard_map/pallas_call | solution.py:24
  88.5 1.4 %shard_map.111 = bf16[256,1024]{1,0:T(8,128)(2,1)} custom-call(f32[256,128]{1,0:T(8,128)S(1)} %get-tuple-element.54.live_ref, bf16[256,1024]{1,0:T(8,128)(2,1)S(1)} %get-tuple-element.58.q_ref, f32[256,1024]{1,0:T(8,128)S(1)} %get-tuple-element.59.inside_ref, f32[4,128,128]{2,1,0:T(8,128)S(1)} %get-tuple-element.78.held_ref, ...), custom_call_target="tpu_custom_call" | custom-call | flops 2000000 | bytes 1048576 | tf_op jit(solution)/shard_map/pallas_call | solution.py:24
  89.8 1.2 %shard_map.120 = bf16[256,1024]{1,0:T(8,128)(2,1)} custom-call(f32[24,256]{1,0:T(8,128)S(1)} %get-tuple-element.55.bias_ref, f32[256,128]{1,0:T(8,128)S(1)} %get-tuple-element.54.live_ref, bf16[2048,256]{1,0:T(8,128)(2,1)S(1)} %get-tuple-element.81.q2_ref, bf16[512,128]{1,0:T(8,128)(2,1)S(1)} %collective-permute-done.13.f_ref, ...), custom_call_target="tpu_custom_call" | custom-call | flops 2000000 | bytes 1048576 | tf_op jit(solution)/shard_map/pallas_call | solution.py:24
  (47 shorter events, 0.8 us)
Async XLA Ops:
  0.6 0.9 copy-start.5
  1.5 38.5 %copy-start.6 = (f32[256,8]{0,1:T(8,128)S(1)}, f32[256,8]{0,1:T(8,128)}, u32[]{:S(2)}) copy-start(f32[256,8]{0,1:T(8,128)} %param.12) | copy-start | bytes 24580
  1.5 26.1 %collective-permute-start.6 = (bf16[512,128]{1,0:T(8,128)(2,1)S(1)}, bf16[512,128]{1,0:T(8,128)(2,1)S(1)}, u32[]{:S(2)}, u32[]{:S(2)}) collective-permute-start(bf16[512,128]{1,0:T(8,128)(2,1)S(1)} %constant_dynamic-update-slice_fusion), channel_id=1, source_target_pairs={{0,8},{8,16},{16,24},{24,32},{32,40},{40,48},{48,56},{56,64},{64,7... | collective-permute-start | bytes 393224 | tf_op jit(solution)/shard_map/ppermute | solution.py:343
  4.4 23.2 %collective-permute-start.14 = (bf16[512,128]{1,0:T(8,128)(2,1)S(1)}, bf16[512,128]{1,0:T(8,128)(2,1)S(1)}, u32[]{:S(2)}, u32[]{:S(2)}) collective-permute-start(bf16[512,128]{1,0:T(8,128)(2,1)S(1)} %constant_dynamic-update-slice_fusion), channel_id=1, source_target_pairs={{8,0},{16,8},{24,16},{32,24},{40,32},{48,40},{56,48},{64,56},{72,6... | collective-permute-start | bytes 393224 | tf_op jit(solution)/shard_map/ppermute | solution.py:343
  27.6 6.2 %collective-permute-start.7 = (bf16[512,128]{1,0:T(8,128)(2,1)S(1)}, bf16[512,128]{1,0:T(8,128)(2,1)S(1)}, u32[]{:S(2)}, u32[]{:S(2)}) collective-permute-start(bf16[512,128]{1,0:T(8,128)(2,1)S(1)} %collective-permute-done.6.refs_0_), channel_id=1, source_target_pairs={{0,8},{8,16},{16,24},{24,32},{32,40},{40,48},{48,56},{56,64},{64,7... | collective-permute-start | bytes 393224 | tf_op jit(solution)/shard_map/ppermute | solution.py:343
  27.6 6.2 %collective-permute-start.15 = (bf16[512,128]{1,0:T(8,128)(2,1)S(1)}, bf16[512,128]{1,0:T(8,128)(2,1)S(1)}, u32[]{:S(2)}, u32[]{:S(2)}) collective-permute-start(bf16[512,128]{1,0:T(8,128)(2,1)S(1)} %collective-permute-done.14.refs_1_), channel_id=1, source_target_pairs={{8,0},{16,8},{24,16},{32,24},{40,32},{48,40},{56,48},{64,56},{72,6... | collective-permute-start | bytes 393224 | tf_op jit(solution)/shard_map/ppermute | solution.py:343
  33.8 6.2 %collective-permute-start.8 = (bf16[512,128]{1,0:T(8,128)(2,1)S(1)}, bf16[512,128]{1,0:T(8,128)(2,1)S(1)}, u32[]{:S(2)}, u32[]{:S(2)}) collective-permute-start(bf16[512,128]{1,0:T(8,128)(2,1)S(1)} %collective-permute-done.7.refs_0_), channel_id=1, source_target_pairs={{0,8},{8,16},{16,24},{24,32},{32,40},{40,48},{48,56},{56,64},{64,7... | collective-permute-start | bytes 393224 | tf_op jit(solution)/shard_map/ppermute | solution.py:343
  33.8 9.0 %collective-permute-start.16 = (bf16[512,128]{1,0:T(8,128)(2,1)S(1)}, bf16[512,128]{1,0:T(8,128)(2,1)S(1)}, u32[]{:S(2)}, u32[]{:S(2)}) collective-permute-start(bf16[512,128]{1,0:T(8,128)(2,1)S(1)} %collective-permute-done.15.refs_1_), channel_id=1, source_target_pairs={{8,0},{16,8},{24,16},{32,24},{40,32},{48,40},{56,48},{64,56},{72,6... | collective-permute-start | bytes 393224 | tf_op jit(solution)/shard_map/ppermute | solution.py:343
  40.0 6.2 %collective-permute-start.9 = (bf16[512,128]{1,0:T(8,128)(2,1)S(1)}, bf16[512,128]{1,0:T(8,128)(2,1)S(1)}, u32[]{:S(2)}, u32[]{:S(2)}) collective-permute-start(bf16[512,128]{1,0:T(8,128)(2,1)S(1)} %collective-permute-done.8.refs_0_), channel_id=1, source_target_pairs={{0,8},{8,16},{16,24},{24,32},{32,40},{40,48},{48,56},{56,64},{64,7... | collective-permute-start | bytes 393224 | tf_op jit(solution)/shard_map/ppermute | solution.py:343
  40.0 0.7 copy-start.8
  42.7 6.1 %collective-permute-start = (bf16[544,128]{1,0:T(8,128)(2,1)S(1)}, bf16[544,128]{1,0:T(8,128)(2,1)S(1)}, u32[]{:S(2)}, u32[]{:S(2)}) collective-permute-start(bf16[544,128]{1,0:T(8,128)(2,1)S(1)} %get-tuple-element.60), channel_id=1, source_target_pairs={{0,8},{8,0},{16,24},{24,16},{32,40},{40,32},{48,56},{56,48},{64,72... | collective-permute-start | bytes 417800 | tf_op jit(solution)/shard_map/ppermute | solution.py:343
  42.8 8.6 %collective-permute-start.17 = (bf16[512,128]{1,0:T(8,128)(2,1)S(1)}, bf16[512,128]{1,0:T(8,128)(2,1)S(1)}, u32[]{:S(2)}, u32[]{:S(2)}) collective-permute-start(bf16[512,128]{1,0:T(8,128)(2,1)S(1)} %collective-permute-done.16.refs_1_), channel_id=1, source_target_pairs={{8,0},{16,8},{24,16},{32,24},{40,32},{48,40},{56,48},{64,56},{72,6... | collective-permute-start | bytes 393224 | tf_op jit(solution)/shard_map/ppermute | solution.py:343
  46.2 7.1 %collective-permute-start.10 = (bf16[512,128]{1,0:T(8,128)(2,1)S(1)}, bf16[512,128]{1,0:T(8,128)(2,1)S(1)}, u32[]{:S(2)}, u32[]{:S(2)}) collective-permute-start(bf16[512,128]{1,0:T(8,128)(2,1)S(1)} %collective-permute-done.9.refs_0_), channel_id=1, source_target_pairs={{0,8},{8,16},{16,24},{24,32},{32,40},{40,48},{48,56},{56,64},{64,7... | collective-permute-start | bytes 393224 | tf_op jit(solution)/shard_map/ppermute | solution.py:343
  48.7 37.9 %copy-start.3 = (bf16[256,1024]{1,0:T(8,128)(2,1)S(1)}, bf16[256,1024]{1,0:T(8,128)(2,1)}, u32[]{:S(2)}) copy-start(bf16[256,1024]{1,0:T(8,128)(2,1)} %q_ref.2) | copy-start | bytes 1572868
  48.8 6.1 %collective-permute-start.1 = (bf16[288,128]{1,0:T(8,128)(2,1)S(1)}, bf16[288,128]{1,0:T(8,128)(2,1)S(1)}, u32[]{:S(2)}, u32[]{:S(2)}) collective-permute-start(bf16[288,128]{1,0:T(8,128)(2,1)S(1)} %get-tuple-element.63), channel_id=1, source_target_pairs={{0,16},{8,24},{16,0},{24,8},{32,48},{40,56},{48,32},{56,40},{64,80... | collective-permute-start | bytes 221192 | tf_op jit(solution)/shard_map/ppermute | solution.py:343
  51.4 16.1 %collective-permute-start.18 = (bf16[512,128]{1,0:T(8,128)(2,1)S(1)}, bf16[512,128]{1,0:T(8,128)(2,1)S(1)}, u32[]{:S(2)}, u32[]{:S(2)}) collective-permute-start(bf16[512,128]{1,0:T(8,128)(2,1)S(1)} %collective-permute-done.17.refs_1_), channel_id=1, source_target_pairs={{8,0},{16,8},{24,16},{32,24},{40,32},{48,40},{56,48},{64,56},{72,6... | collective-permute-start | bytes 393224 | tf_op jit(solution)/shard_map/ppermute | solution.py:343
  53.2 16.9 %collective-permute-start.11 = (bf16[512,128]{1,0:T(8,128)(2,1)S(1)}, bf16[512,128]{1,0:T(8,128)(2,1)S(1)}, u32[]{:S(2)}, u32[]{:S(2)}) collective-permute-start(bf16[512,128]{1,0:T(8,128)(2,1)S(1)} %collective-permute-done.10.refs_0_), channel_id=1, source_target_pairs={{0,8},{8,16},{16,24},{24,32},{32,40},{40,48},{48,56},{56,64},{64,7... | collective-permute-start | bytes 393224 | tf_op jit(solution)/shard_map/ppermute | solution.py:343
  55.0 30.7 %copy-start.2 = (bf16[256,1024]{1,0:T(8,128)(2,1)S(1)}, bf16[256,1024]{1,0:T(8,128)(2,1)}, u32[]{:S(2)}) copy-start(bf16[256,1024]{1,0:T(8,128)(2,1)} %q_ref.3) | copy-start | bytes 1572868
  55.0 10.1 %collective-permute-start.2 = (bf16[288,128]{1,0:T(8,128)(2,1)S(1)}, bf16[288,128]{1,0:T(8,128)(2,1)S(1)}, u32[]{:S(2)}, u32[]{:S(2)}) collective-permute-start(bf16[288,128]{1,0:T(8,128)(2,1)S(1)} %get-tuple-element.66), channel_id=1, source_target_pairs={{0,32},{8,40},{16,48},{24,56},{32,0},{40,8},{48,16},{56,24},{64,96... | collective-permute-start | bytes 221192 | tf_op jit(solution)/shard_map/ppermute | solution.py:343
  65.2 5.9 %collective-permute-start.3 = (bf16[256,128]{1,0:T(8,128)(2,1)S(1)}, bf16[256,128]{1,0:T(8,128)(2,1)S(1)}, u32[]{:S(2)}, u32[]{:S(2)}) collective-permute-start(bf16[256,128]{1,0:T(8,128)(2,1)S(1)} %get-tuple-element.69), channel_id=1, source_target_pairs={{0,96},{8,104},{16,112},{24,120},{32,64},{40,72},{48,80},{56,88},{... | collective-permute-start | bytes 196616 | tf_op jit(solution)/shard_map/ppermute | solution.py:343
  67.5 13.2 %collective-permute-start.19 = (bf16[512,128]{1,0:T(8,128)(2,1)S(1)}, bf16[512,128]{1,0:T(8,128)(2,1)S(1)}, u32[]{:S(2)}, u32[]{:S(2)}) collective-permute-start(bf16[512,128]{1,0:T(8,128)(2,1)S(1)} %collective-permute-done.18.refs_1_), channel_id=1, source_target_pairs={{8,0},{16,8},{24,16},{32,24},{40,32},{48,40},{56,48},{64,56},{72,6... | collective-permute-start | bytes 393224 | tf_op jit(solution)/shard_map/ppermute | solution.py:343
  70.2 14.9 %collective-permute-start.12 = (bf16[512,128]{1,0:T(8,128)(2,1)S(1)}, bf16[512,128]{1,0:T(8,128)(2,1)S(1)}, u32[]{:S(2)}, u32[]{:S(2)}) collective-permute-start(bf16[512,128]{1,0:T(8,128)(2,1)S(1)} %collective-permute-done.11.refs_0_), channel_id=1, source_target_pairs={{0,8},{8,16},{16,24},{24,32},{32,40},{40,48},{48,56},{56,64},{64,7... | collective-permute-start | bytes 393224 | tf_op jit(solution)/shard_map/ppermute | solution.py:343
  71.2 14.5 %copy-start.4 = (bf16[256,128]{1,0:T(8,128)(2,1)S(1)}, bf16[256,128]{1,0:T(8,128)(2,1)}, u32[]{:S(2)}) copy-start(bf16[256,128]{1,0:T(8,128)(2,1)} %k_ref.3) | copy-start | bytes 196612
  71.3 7.4 %collective-permute-start.4 = (bf16[256,128]{1,0:T(8,128)(2,1)S(1)}, bf16[256,128]{1,0:T(8,128)(2,1)S(1)}, u32[]{:S(2)}, u32[]{:S(2)}) collective-permute-start(bf16[256,128]{1,0:T(8,128)(2,1)S(1)} %get-tuple-element.75), channel_id=1, source_target_pairs={{0,16},{8,24},{16,0},{24,8},{32,48},{40,56},{48,32},{56,40},{64,80... | collective-permute-start | bytes 196616 | tf_op jit(solution)/shard_map/ppermute | solution.py:343
  78.7 8.0 %copy-start = (bf16[256,1024]{1,0:T(8,128)(2,1)S(1)}, bf16[256,1024]{1,0:T(8,128)(2,1)}, u32[]{:S(2)}) copy-start(bf16[256,1024]{1,0:T(8,128)(2,1)} %k_ref.2) | copy-start | bytes 1572868
  78.7 8.0 %copy-start.1 = (bf16[256,1024]{1,0:T(8,128)(2,1)S(1)}, bf16[256,1024]{1,0:T(8,128)(2,1)}, u32[]{:S(2)}) copy-start(bf16[256,1024]{1,0:T(8,128)(2,1)} %v_ref.2) | copy-start | bytes 1572868
  78.8 9.7 %collective-permute-start.5 = (bf16[512,128]{1,0:T(8,128)(2,1)S(1)}, bf16[512,128]{1,0:T(8,128)(2,1)S(1)}, u32[]{:S(2)}, u32[]{:S(2)}) collective-permute-start(bf16[512,128]{1,0:T(8,128)(2,1)S(1)} %get-tuple-element.79), channel_id=1, source_target_pairs={{0,8},{8,0},{16,24},{24,16},{32,40},{40,32},{48,56},{56,48},{64,72... | collective-permute-start | bytes 393224 | tf_op jit(solution)/shard_map/ppermute | solution.py:343
  80.7 9.2 %collective-permute-start.20 = (bf16[512,128]{1,0:T(8,128)(2,1)S(1)}, bf16[512,128]{1,0:T(8,128)(2,1)S(1)}, u32[]{:S(2)}, u32[]{:S(2)}) collective-permute-start(bf16[512,128]{1,0:T(8,128)(2,1)S(1)} %collective-permute-done.19.refs_1_), channel_id=1, source_target_pairs={{8,0},{16,8},{24,16},{32,24},{40,32},{48,40},{56,48},{64,56},{72,6... | collective-permute-start | bytes 393224 | tf_op jit(solution)/shard_map/ppermute | solution.py:343
  85.0 4.8 %collective-permute-start.13 = (bf16[512,128]{1,0:T(8,128)(2,1)S(1)}, bf16[512,128]{1,0:T(8,128)(2,1)S(1)}, u32[]{:S(2)}, u32[]{:S(2)}) collective-permute-start(bf16[512,128]{1,0:T(8,128)(2,1)S(1)} %collective-permute-done.12.refs_0_), channel_id=1, source_target_pairs={{56,64},{64,72},{72,80},{80,88},{88,96},{96,104},{104,112},{112,12... | collective-permute-start | bytes 393224 | tf_op jit(solution)/shard_map/ppermute | solution.py:343
  86.6 0.7 copy-start.7

commit v5 on v4

--- a/solution.py
+++ b/solution.py
@@ -59,10 +59,14 @@
 
 
 def prep_kernel(
-    len_ref, k_hbm, v_hbm, dec_ref, msg_ref, kept_ref, logs_ref, c_ref, ct_ref, bias_ref, live_ref, states, k_ref, v_ref, sems
+    len_hbm, k_hbm, v_hbm, dec_hbm, msg_ref, kept_ref, logs_ref, c_ref, ct_ref, bias_ref, live_ref, states, k_ref, v_ref, len_ref, dec_ref, sems
 ):
     k_copy = pltpu.make_async_copy(k_hbm, k_ref, sems.at[0])
     v_copy = pltpu.make_async_copy(v_hbm, v_ref, sems.at[1])
+    len_copy = pltpu.make_async_copy(len_hbm, len_ref, sems.at[2])
+    dec_copy = pltpu.make_async_copy(dec_hbm, dec_ref, sems.at[3])
+    len_copy.start()
+    dec_copy.start()
     k_copy.start()
     v_copy.start()
     i = lax.axis_index("seq")
@@ -71,6 +75,8 @@
     width = k_ref.shape[1] // heads
     half = heads // 2
     blocks = len_ref.shape[1]
+    len_copy.wait()
+    dec_copy.wait()
     lengths = len_ref[...]
     at = lax.broadcasted_iota(jnp.int32, (1, blocks), 1)
     length = jnp.sum(jnp.where(at == i, lengths, 0), axis=1, keepdims=True)
@@ -360,12 +366,17 @@
             ((count + 8, rows), F32),
             ((rows, 128), F32),
         ],
-        [(False, lengths.reshape(1, count)), (None, pltpu.with_memory_space_constraint(light_keys, pltpu.HBM)), (None, pltpu.with_memory_space_constraint(light_values, pltpu.HBM)), (False, decay_log.T)],
+        [
+            (None, pltpu.with_memory_space_constraint(x, pltpu.HBM))
+            for x in (lengths.reshape(1, count), light_keys, light_values, decay_log.T)
+        ],
         scratch=[
             pltpu.VMEM((heads, width, width), F32),
             pltpu.VMEM((rows, heads * width), BF16),
             pltpu.VMEM((rows, heads * width), BF16),
-            pltpu.SemaphoreType.DMA((2,)),
+            pltpu.VMEM((1, count), jnp.int32),
+            pltpu.VMEM((heads, rows), F32),
+            pltpu.SemaphoreType.DMA((4,)),
         ],
         limit=48 * 1024 * 1024,
     )

time: 91.3 us -> 90.7 us (level)
  starting transfers between devices: 51.2 us -> 52.4 us
    ppermute x21, starting transfers between devices: 51.2 us -> 52.4 us  [send(): return lax.ppermute(x, 'seq', pairs)]
    ppermute x21, waiting for transfers between devices: 29.9 us -> 29 us  [send(): return lax.ppermute(x, 'seq', pairs)]
    unnamed x19 -> x15, local copies, waits for them, and re-layouts: 2.21 us -> 1.56 us
where the time goes in v5:
time: 90.7 us; the launch traced here: 90.4 us
  starting transfers between devices  52.4 us (58%)
  waiting for transfers between devices  29 us (32%)
  Pallas kernels  6.61 us (7%)
  local copies, waits for them, and re-layouts  1.57 us (2%)
    ppermute x21, starting transfers between devices, send(): return lax.ppermute(x, 'seq', pairs)  52.4 us
    ppermute x21, waiting for transfers between devices, send(): return lax.ppermute(x, 'seq', pairs)  29 us
    pallas_call x17, Pallas kernels, call(): pl.pallas_call(kernel, out_shape=outs, in_specs=specs, out_specs=[VMEM] *...  6.61 us
  transfers between devices with their start and end apart: 21, of which 9 were waited for; matrix products, arithmetic and copies ran while one was open for 0% of the time, Pallas kernels for 6%

profile of v5, /device:TPU:36, one launch (start us, length us, event | category | flops | bytes accessed | tf_op | source)
XLA Modules:
  0.0 90.4 jit_solution(11339744326960782173)
XLA Ops:
  0.6 0.9 constant_dynamic-update-slice_fusion.1
  1.5 2.9 %collective-permute-start.6 = (bf16[512,128]{1,0:T(8,128)(2,1)S(1)}, bf16[512,128]{1,0:T(8,128)(2,1)S(1)}, u32[]{:S(2)}, u32[]{:S(2)}) collective-permute-start(bf16[512,128]{1,0:T(8,128)(2,1)S(1)} %constant_dynamic-update-slice_fusion), channel_id=1, source_target_pairs={{0,8},{8,16},{16,24},{24,32},{32,40},{40,48},{48,56},{56,64},{64,7... | collective-permute-start | bytes 393224 | tf_op jit(solution)/shard_map/ppermute | solution.py:349
  4.4 19.7 %collective-permute-start.14 = (bf16[512,128]{1,0:T(8,128)(2,1)S(1)}, bf16[512,128]{1,0:T(8,128)(2,1)S(1)}, u32[]{:S(2)}, u32[]{:S(2)}) collective-permute-start(bf16[512,128]{1,0:T(8,128)(2,1)S(1)} %constant_dynamic-update-slice_fusion), channel_id=1, source_target_pairs={{8,0},{16,8},{24,16},{32,24},{40,32},{48,40},{56,48},{64,56},{72,6... | collective-permute-start | bytes 393224 | tf_op jit(solution)/shard_map/ppermute | solution.py:349
  24.2 3.4 %collective-permute-done.6.refs_0_ = bf16[512,128]{1,0:T(8,128)(2,1)S(1)} collective-permute-done((bf16[512,128]{1,0:T(8,128)(2,1)S(1)}, bf16[512,128]{1,0:T(8,128)(2,1)S(1)}, u32[]{:S(2)}, u32[]{:S(2)}) %collective-permute-start.6) | collective-permute-done | bytes 131104 | tf_op jit(solution)/shard_map/ppermute | solution.py:349
  27.6 3.2 %collective-permute-start.15 = (bf16[512,128]{1,0:T(8,128)(2,1)S(1)}, bf16[512,128]{1,0:T(8,128)(2,1)S(1)}, u32[]{:S(2)}, u32[]{:S(2)}) collective-permute-start(bf16[512,128]{1,0:T(8,128)(2,1)S(1)} %collective-permute-done.14.refs_1_), channel_id=1, source_target_pairs={{8,0},{16,8},{24,16},{32,24},{40,32},{48,40},{56,48},{64,56},{72,6... | collective-permute-start | bytes 393224 | tf_op jit(solution)/shard_map/ppermute | solution.py:349
  30.8 2.9 %collective-permute-done.7.refs_0_ = bf16[512,128]{1,0:T(8,128)(2,1)S(1)} collective-permute-done((bf16[512,128]{1,0:T(8,128)(2,1)S(1)}, bf16[512,128]{1,0:T(8,128)(2,1)S(1)}, u32[]{:S(2)}, u32[]{:S(2)}) %collective-permute-start.7) | collective-permute-done | bytes 131104 | tf_op jit(solution)/shard_map/ppermute | solution.py:349
  33.8 3.2 %collective-permute-start.16 = (bf16[512,128]{1,0:T(8,128)(2,1)S(1)}, bf16[512,128]{1,0:T(8,128)(2,1)S(1)}, u32[]{:S(2)}, u32[]{:S(2)}) collective-permute-start(bf16[512,128]{1,0:T(8,128)(2,1)S(1)} %collective-permute-done.15.refs_1_), channel_id=1, source_target_pairs={{8,0},{16,8},{24,16},{32,24},{40,32},{48,40},{56,48},{64,56},{72,6... | collective-permute-start | bytes 393224 | tf_op jit(solution)/shard_map/ppermute | solution.py:349
  37.0 2.9 %collective-permute-done.8.refs_0_ = bf16[512,128]{1,0:T(8,128)(2,1)S(1)} collective-permute-done((bf16[512,128]{1,0:T(8,128)(2,1)S(1)}, bf16[512,128]{1,0:T(8,128)(2,1)S(1)}, u32[]{:S(2)}, u32[]{:S(2)}) %collective-permute-start.8) | collective-permute-done | bytes 131104 | tf_op jit(solution)/shard_map/ppermute | solution.py:349
  40.0 1.8 %shard_map.104 = (bf16[544,128]{1,0:T(8,128)(2,1)S(1)}, f32[4,128,128]{2,1,0:T(8,128)S(1)}, f32[8,128]{1,0:T(8,128)S(1)}, f32[8,256]{1,0:T(8,128)S(1)}, f32[256,...) custom-call(s32[1,16]{1,0:T(1,128)} %bitcast.5, bf16[256,1024]{1,0:T(8,128)(2,1)} %k_ref.2, ...), custom_call_target="tpu_custom_call" | custom-call | flops 2000000 | bytes 1048576 | tf_op jit(solution)/shard_map/pallas_call | solution.py:24
  41.7 0.1 collective-permute-start
  41.9 3.4 %collective-permute-start.17 = (bf16[512,128]{1,0:T(8,128)(2,1)S(1)}, bf16[512,128]{1,0:T(8,128)(2,1)S(1)}, u32[]{:S(2)}, u32[]{:S(2)}) collective-permute-start(bf16[512,128]{1,0:T(8,128)(2,1)S(1)} %collective-permute-done.16.refs_1_), channel_id=1, source_target_pairs={{8,0},{16,8},{24,16},{32,24},{40,32},{48,40},{56,48},{64,56},{72,6... | collective-permute-start | bytes 393224 | tf_op jit(solution)/shard_map/ppermute | solution.py:349
  45.3 1.2 %collective-permute-done.9.refs_0_ = bf16[512,128]{1,0:T(8,128)(2,1)S(1)} collective-permute-done((bf16[512,128]{1,0:T(8,128)(2,1)S(1)}, bf16[512,128]{1,0:T(8,128)(2,1)S(1)}, u32[]{:S(2)}, u32[]{:S(2)}) %collective-permute-start.9) | collective-permute-done | bytes 131104 | tf_op jit(solution)/shard_map/ppermute | solution.py:349
  46.5 0.7 collective-permute-done.recv_ref
  47.2 0.1 collective-permute-start.1
  47.4 3.1 %collective-permute-done.17.refs_1_ = bf16[512,128]{1,0:T(8,128)(2,1)S(1)} collective-permute-done((bf16[512,128]{1,0:T(8,128)(2,1)S(1)}, bf16[512,128]{1,0:T(8,128)(2,1)S(1)}, u32[]{:S(2)}, u32[]{:S(2)}) %collective-permute-start.17) | collective-permute-done | bytes 131104 | tf_op jit(solution)/shard_map/ppermute | solution.py:349
  50.5 1.5 %collective-permute-start.18 = (bf16[512,128]{1,0:T(8,128)(2,1)S(1)}, bf16[512,128]{1,0:T(8,128)(2,1)S(1)}, u32[]{:S(2)}, u32[]{:S(2)}) collective-permute-start(bf16[512,128]{1,0:T(8,128)(2,1)S(1)} %collective-permute-done.17.refs_1_), channel_id=1, source_target_pairs={{8,0},{16,8},{24,16},{32,24},{40,32},{48,40},{56,48},{64,56},{72,6... | collective-permute-start | bytes 393224 | tf_op jit(solution)/shard_map/ppermute | solution.py:349
  52.0 1.9 %collective-permute-done.10.refs_0_ = bf16[512,128]{1,0:T(8,128)(2,1)S(1)} collective-permute-done((bf16[512,128]{1,0:T(8,128)(2,1)S(1)}, bf16[512,128]{1,0:T(8,128)(2,1)S(1)}, u32[]{:S(2)}, u32[]{:S(2)}) %collective-permute-start.10) | collective-permute-done | bytes 131104 | tf_op jit(solution)/shard_map/ppermute | solution.py:349
  54.1 0.1 collective-permute-start.2
  54.2 10.2 %collective-permute-done.2.recv_ref = bf16[288,128]{1,0:T(8,128)(2,1)S(1)} collective-permute-done((bf16[288,128]{1,0:T(8,128)(2,1)S(1)}, bf16[288,128]{1,0:T(8,128)(2,1)S(1)}, u32[]{:S(2)}, u32[]{:S(2)}) %collective-permute-start.2) | collective-permute-done | bytes 73760 | tf_op jit(solution)/shard_map/ppermute | solution.py:349
  64.5 4.3 %collective-permute-start.3 = (bf16[256,128]{1,0:T(8,128)(2,1)S(1)}, bf16[256,128]{1,0:T(8,128)(2,1)S(1)}, u32[]{:S(2)}, u32[]{:S(2)}) collective-permute-start(bf16[256,128]{1,0:T(8,128)(2,1)S(1)} %get-tuple-element.69), channel_id=1, source_target_pairs={{0,96},{8,104},{16,112},{24,120},{32,64},{40,72},{48,80},{56,88},{... | collective-permute-start | bytes 196616 | tf_op jit(solution)/shard_map/ppermute | solution.py:349
  68.8 0.7 collective-permute-start.19
  69.4 1.7 %collective-permute-start.12 = (bf16[512,128]{1,0:T(8,128)(2,1)S(1)}, bf16[512,128]{1,0:T(8,128)(2,1)S(1)}, u32[]{:S(2)}, u32[]{:S(2)}) collective-permute-start(bf16[512,128]{1,0:T(8,128)(2,1)S(1)} %collective-permute-done.11.refs_0_), channel_id=1, source_target_pairs={{0,8},{8,16},{16,24},{24,32},{32,40},{40,48},{48,56},{56,64},{64,7... | collective-permute-start | bytes 393224 | tf_op jit(solution)/shard_map/ppermute | solution.py:349
  71.2 3.1 %collective-permute-start.4 = (bf16[256,128]{1,0:T(8,128)(2,1)S(1)}, bf16[256,128]{1,0:T(8,128)(2,1)S(1)}, u32[]{:S(2)}, u32[]{:S(2)}) collective-permute-start(bf16[256,128]{1,0:T(8,128)(2,1)S(1)} %get-tuple-element.75), channel_id=1, source_target_pairs={{0,16},{8,24},{16,0},{24,8},{32,48},{40,56},{48,32},{56,40},{64,80... | collective-permute-start | bytes 196616 | tf_op jit(solution)/shard_map/ppermute | solution.py:349
  74.2 2.4 %collective-permute-done.4.recv_ref = bf16[256,128]{1,0:T(8,128)(2,1)S(1)} collective-permute-done((bf16[256,128]{1,0:T(8,128)(2,1)S(1)}, bf16[256,128]{1,0:T(8,128)(2,1)S(1)}, u32[]{:S(2)}, u32[]{:S(2)}) %collective-permute-start.4) | collective-permute-done | bytes 65568 | tf_op jit(solution)/shard_map/ppermute | solution.py:349
  76.8 3.0 %collective-permute-start.5 = (bf16[512,128]{1,0:T(8,128)(2,1)S(1)}, bf16[512,128]{1,0:T(8,128)(2,1)S(1)}, u32[]{:S(2)}, u32[]{:S(2)}) collective-permute-start(bf16[512,128]{1,0:T(8,128)(2,1)S(1)} %get-tuple-element.79), channel_id=1, source_target_pairs={{0,8},{8,0},{16,24},{24,16},{32,40},{40,32},{48,56},{56,48},{64,72... | collective-permute-start | bytes 393224 | tf_op jit(solution)/shard_map/ppermute | solution.py:349
  79.8 4.7 %collective-permute-start.20 = (bf16[512,128]{1,0:T(8,128)(2,1)S(1)}, bf16[512,128]{1,0:T(8,128)(2,1)S(1)}, u32[]{:S(2)}, u32[]{:S(2)}) collective-permute-start(bf16[512,128]{1,0:T(8,128)(2,1)S(1)} %collective-permute-done.19.refs_1_), channel_id=1, source_target_pairs={{8,0},{16,8},{24,16},{32,24},{40,32},{48,40},{56,48},{64,56},{72,6... | collective-permute-start | bytes 393224 | tf_op jit(solution)/shard_map/ppermute | solution.py:349
  84.5 0.7 collective-permute-start.13
  85.1 0.9 %shard_map.112 = (bf16[2048,256]{1,0:T(8,128)(2,1)S(1)}, f32[2048,128]{1,0:T(8,128)S(1)}, f32[2048,128]{1,0:T(8,128)S(1)}, f32[2048,128]{1,0:T(8,128)S(1)}) custom-call(f32[24,256]{1,0:T(8,128)S(1)} %get-tuple-element.55.bias_ref, bf16[256,1024]{1,0:T(8,128)(2,1)S(1)} %copy-done.2, bf16[256,128]{1,0:T(8,128)(2,1)S(1)} %copy-done.4, ...), custom_call_target="tpu_custom_call" | custom-call | flops 2000000 | bytes 1048576 | tf_op jit(solution)/shard_map/pallas_call | solution.py:24
  86.1 0.7 copy-done.6
  86.7 1.0 %shard_map.105 = (f32[256,1024]{1,0:T(8,128)S(1)}, bf16[256,1024]{1,0:T(8,128)(2,1)S(1)}, f32[1,1024]{1,0:T(1,128)S(1)}) custom-call(f32[24,256]{1,0:T(8,128)S(1)} %get-tuple-element.55.bias_ref, bf16[256,1024]{1,0:T(8,128)(2,1)S(1)} %copy-done.3, bf16[256,1024]{1,0:T(8,128)(2,1)S(1)} %copy-done, bf16[256,1024]{1,0:T(8,128)(2,1)S(1)} %copy-done.1, ...), custom_call_target="tpu_custom_call" | custom-call | flops 2000000 | bytes 1048576 | tf_op jit(solution)/shard_map/pallas_call | solution.py:24
  87.9 1.4 %shard_map.111 = bf16[256,1024]{1,0:T(8,128)(2,1)} custom-call(f32[256,128]{1,0:T(8,128)S(1)} %get-tuple-element.54.live_ref, bf16[256,1024]{1,0:T(8,128)(2,1)S(1)} %get-tuple-element.58.q_ref, f32[256,1024]{1,0:T(8,128)S(1)} %get-tuple-element.59.inside_ref, f32[4,128,128]{2,1,0:T(8,128)S(1)} %get-tuple-element.78.held_ref, ...), custom_call_target="tpu_custom_call" | custom-call | flops 2000000 | bytes 1048576 | tf_op jit(solution)/shard_map/pallas_call | solution.py:24
  89.3 1.2 %shard_map.120 = bf16[256,1024]{1,0:T(8,128)(2,1)} custom-call(f32[24,256]{1,0:T(8,128)S(1)} %get-tuple-element.55.bias_ref, f32[256,128]{1,0:T(8,128)S(1)} %get-tuple-element.54.live_ref, bf16[2048,256]{1,0:T(8,128)(2,1)S(1)} %get-tuple-element.81.q2_ref, bf16[512,128]{1,0:T(8,128)(2,1)S(1)} %collective-permute-done.13.f_ref, ...), custom_call_target="tpu_custom_call" | custom-call | flops 2000000 | bytes 1048576 | tf_op jit(solution)/shard_map/pallas_call | solution.py:24
  (43 shorter events, 0.5 us)
Async XLA Ops:
  0.6 0.9 copy-start.5
  1.5 26.1 %collective-permute-start.6 = (bf16[512,128]{1,0:T(8,128)(2,1)S(1)}, bf16[512,128]{1,0:T(8,128)(2,1)S(1)}, u32[]{:S(2)}, u32[]{:S(2)}) collective-permute-start(bf16[512,128]{1,0:T(8,128)(2,1)S(1)} %constant_dynamic-update-slice_fusion), channel_id=1, source_target_pairs={{0,8},{8,16},{16,24},{24,32},{32,40},{40,48},{48,56},{56,64},{64,7... | collective-permute-start | bytes 393224 | tf_op jit(solution)/shard_map/ppermute | solution.py:349
  4.4 23.2 %collective-permute-start.14 = (bf16[512,128]{1,0:T(8,128)(2,1)S(1)}, bf16[512,128]{1,0:T(8,128)(2,1)S(1)}, u32[]{:S(2)}, u32[]{:S(2)}) collective-permute-start(bf16[512,128]{1,0:T(8,128)(2,1)S(1)} %constant_dynamic-update-slice_fusion), channel_id=1, source_target_pairs={{8,0},{16,8},{24,16},{32,24},{40,32},{48,40},{56,48},{64,56},{72,6... | collective-permute-start | bytes 393224 | tf_op jit(solution)/shard_map/ppermute | solution.py:349
  27.6 6.2 %collective-permute-start.7 = (bf16[512,128]{1,0:T(8,128)(2,1)S(1)}, bf16[512,128]{1,0:T(8,128)(2,1)S(1)}, u32[]{:S(2)}, u32[]{:S(2)}) collective-permute-start(bf16[512,128]{1,0:T(8,128)(2,1)S(1)} %collective-permute-done.6.refs_0_), channel_id=1, source_target_pairs={{0,8},{8,16},{16,24},{24,32},{32,40},{40,48},{48,56},{56,64},{64,7... | collective-permute-start | bytes 393224 | tf_op jit(solution)/shard_map/ppermute | solution.py:349
  27.6 6.2 %collective-permute-start.15 = (bf16[512,128]{1,0:T(8,128)(2,1)S(1)}, bf16[512,128]{1,0:T(8,128)(2,1)S(1)}, u32[]{:S(2)}, u32[]{:S(2)}) collective-permute-start(bf16[512,128]{1,0:T(8,128)(2,1)S(1)} %collective-permute-done.14.refs_1_), channel_id=1, source_target_pairs={{8,0},{16,8},{24,16},{32,24},{40,32},{48,40},{56,48},{64,56},{72,6... | collective-permute-start | bytes 393224 | tf_op jit(solution)/shard_map/ppermute | solution.py:349
  33.8 6.2 %collective-permute-start.8 = (bf16[512,128]{1,0:T(8,128)(2,1)S(1)}, bf16[512,128]{1,0:T(8,128)(2,1)S(1)}, u32[]{:S(2)}, u32[]{:S(2)}) collective-permute-start(bf16[512,128]{1,0:T(8,128)(2,1)S(1)} %collective-permute-done.7.refs_0_), channel_id=1, source_target_pairs={{0,8},{8,16},{16,24},{24,32},{32,40},{40,48},{48,56},{56,64},{64,7... | collective-permute-start | bytes 393224 | tf_op jit(solution)/shard_map/ppermute | solution.py:349
  33.8 8.1 %collective-permute-start.16 = (bf16[512,128]{1,0:T(8,128)(2,1)S(1)}, bf16[512,128]{1,0:T(8,128)(2,1)S(1)}, u32[]{:S(2)}, u32[]{:S(2)}) collective-permute-start(bf16[512,128]{1,0:T(8,128)(2,1)S(1)} %collective-permute-done.15.refs_1_), channel_id=1, source_target_pairs={{8,0},{16,8},{24,16},{32,24},{40,32},{48,40},{56,48},{64,56},{72,6... | collective-permute-start | bytes 393224 | tf_op jit(solution)/shard_map/ppermute | solution.py:349
  40.0 6.5 %collective-permute-start.9 = (bf16[512,128]{1,0:T(8,128)(2,1)S(1)}, bf16[512,128]{1,0:T(8,128)(2,1)S(1)}, u32[]{:S(2)}, u32[]{:S(2)}) collective-permute-start(bf16[512,128]{1,0:T(8,128)(2,1)S(1)} %collective-permute-done.8.refs_0_), channel_id=1, source_target_pairs={{0,8},{8,16},{16,24},{24,32},{32,40},{40,48},{48,56},{56,64},{64,7... | collective-permute-start | bytes 393224 | tf_op jit(solution)/shard_map/ppermute | solution.py:349
  41.7 5.4 %collective-permute-start = (bf16[544,128]{1,0:T(8,128)(2,1)S(1)}, bf16[544,128]{1,0:T(8,128)(2,1)S(1)}, u32[]{:S(2)}, u32[]{:S(2)}) collective-permute-start(bf16[544,128]{1,0:T(8,128)(2,1)S(1)} %get-tuple-element.60), channel_id=1, source_target_pairs={{0,8},{8,0},{16,24},{24,16},{32,40},{40,32},{48,56},{56,48},{64,72... | collective-permute-start | bytes 417800 | tf_op jit(solution)/shard_map/ppermute | solution.py:349
  41.9 8.6 %collective-permute-start.17 = (bf16[512,128]{1,0:T(8,128)(2,1)S(1)}, bf16[512,128]{1,0:T(8,128)(2,1)S(1)}, u32[]{:S(2)}, u32[]{:S(2)}) collective-permute-start(bf16[512,128]{1,0:T(8,128)(2,1)S(1)} %collective-permute-done.16.refs_1_), channel_id=1, source_target_pairs={{8,0},{16,8},{24,16},{32,24},{40,32},{48,40},{56,48},{64,56},{72,6... | collective-permute-start | bytes 393224 | tf_op jit(solution)/shard_map/ppermute | solution.py:349
  46.5 7.5 %collective-permute-start.10 = (bf16[512,128]{1,0:T(8,128)(2,1)S(1)}, bf16[512,128]{1,0:T(8,128)(2,1)S(1)}, u32[]{:S(2)}, u32[]{:S(2)}) collective-permute-start(bf16[512,128]{1,0:T(8,128)(2,1)S(1)} %collective-permute-done.9.refs_0_), channel_id=1, source_target_pairs={{0,8},{8,16},{16,24},{24,32},{32,40},{40,48},{48,56},{56,64},{64,7... | collective-permute-start | bytes 393224 | tf_op jit(solution)/shard_map/ppermute | solution.py:349
  47.1 38.9 %copy-start.3 = (bf16[256,1024]{1,0:T(8,128)(2,1)S(1)}, bf16[256,1024]{1,0:T(8,128)(2,1)}, u32[]{:S(2)}) copy-start(bf16[256,1024]{1,0:T(8,128)(2,1)} %q_ref.2) | copy-start | bytes 1572868
  47.2 6.8 %collective-permute-start.1 = (bf16[288,128]{1,0:T(8,128)(2,1)S(1)}, bf16[288,128]{1,0:T(8,128)(2,1)S(1)}, u32[]{:S(2)}, u32[]{:S(2)}) collective-permute-start(bf16[288,128]{1,0:T(8,128)(2,1)S(1)} %get-tuple-element.63), channel_id=1, source_target_pairs={{0,16},{8,24},{16,0},{24,8},{32,48},{40,56},{48,32},{56,40},{64,80... | collective-permute-start | bytes 221192 | tf_op jit(solution)/shard_map/ppermute | solution.py:349
  50.5 18.3 %collective-permute-start.18 = (bf16[512,128]{1,0:T(8,128)(2,1)S(1)}, bf16[512,128]{1,0:T(8,128)(2,1)S(1)}, u32[]{:S(2)}, u32[]{:S(2)}) collective-permute-start(bf16[512,128]{1,0:T(8,128)(2,1)S(1)} %collective-permute-done.17.refs_1_), channel_id=1, source_target_pairs={{8,0},{16,8},{24,16},{32,24},{40,32},{48,40},{56,48},{64,56},{72,6... | collective-permute-start | bytes 393224 | tf_op jit(solution)/shard_map/ppermute | solution.py:349
  54.0 15.5 %collective-permute-start.11 = (bf16[512,128]{1,0:T(8,128)(2,1)S(1)}, bf16[512,128]{1,0:T(8,128)(2,1)S(1)}, u32[]{:S(2)}, u32[]{:S(2)}) collective-permute-start(bf16[512,128]{1,0:T(8,128)(2,1)S(1)} %collective-permute-done.10.refs_0_), channel_id=1, source_target_pairs={{0,8},{8,16},{16,24},{24,32},{32,40},{40,48},{48,56},{56,64},{64,7... | collective-permute-start | bytes 393224 | tf_op jit(solution)/shard_map/ppermute | solution.py:349
  54.0 31.1 %copy-start.2 = (bf16[256,1024]{1,0:T(8,128)(2,1)S(1)}, bf16[256,1024]{1,0:T(8,128)(2,1)}, u32[]{:S(2)}) copy-start(bf16[256,1024]{1,0:T(8,128)(2,1)} %q_ref.3) | copy-start | bytes 1572868
  54.1 10.4 %collective-permute-start.2 = (bf16[288,128]{1,0:T(8,128)(2,1)S(1)}, bf16[288,128]{1,0:T(8,128)(2,1)S(1)}, u32[]{:S(2)}, u32[]{:S(2)}) collective-permute-start(bf16[288,128]{1,0:T(8,128)(2,1)S(1)} %get-tuple-element.66), channel_id=1, source_target_pairs={{0,32},{8,40},{16,48},{24,56},{32,0},{40,8},{48,16},{56,24},{64,96... | collective-permute-start | bytes 221192 | tf_op jit(solution)/shard_map/ppermute | solution.py:349
  64.5 6.6 %collective-permute-start.3 = (bf16[256,128]{1,0:T(8,128)(2,1)S(1)}, bf16[256,128]{1,0:T(8,128)(2,1)S(1)}, u32[]{:S(2)}, u32[]{:S(2)}) collective-permute-start(bf16[256,128]{1,0:T(8,128)(2,1)S(1)} %get-tuple-element.69), channel_id=1, source_target_pairs={{0,96},{8,104},{16,112},{24,120},{32,64},{40,72},{48,80},{56,88},{... | collective-permute-start | bytes 196616 | tf_op jit(solution)/shard_map/ppermute | solution.py:349
  68.8 11.0 %collective-permute-start.19 = (bf16[512,128]{1,0:T(8,128)(2,1)S(1)}, bf16[512,128]{1,0:T(8,128)(2,1)S(1)}, u32[]{:S(2)}, u32[]{:S(2)}) collective-permute-start(bf16[512,128]{1,0:T(8,128)(2,1)S(1)} %collective-permute-done.18.refs_1_), channel_id=1, source_target_pairs={{8,0},{16,8},{24,16},{32,24},{40,32},{48,40},{56,48},{64,56},{72,6... | collective-permute-start | bytes 393224 | tf_op jit(solution)/shard_map/ppermute | solution.py:349
  69.4 15.0 %collective-permute-start.12 = (bf16[512,128]{1,0:T(8,128)(2,1)S(1)}, bf16[512,128]{1,0:T(8,128)(2,1)S(1)}, u32[]{:S(2)}, u32[]{:S(2)}) collective-permute-start(bf16[512,128]{1,0:T(8,128)(2,1)S(1)} %collective-permute-done.11.refs_0_), channel_id=1, source_target_pairs={{0,8},{8,16},{16,24},{24,32},{32,40},{40,48},{48,56},{56,64},{64,7... | collective-permute-start | bytes 393224 | tf_op jit(solution)/shard_map/ppermute | solution.py:349
  71.1 14.0 %copy-start.4 = (bf16[256,128]{1,0:T(8,128)(2,1)S(1)}, bf16[256,128]{1,0:T(8,128)(2,1)}, u32[]{:S(2)}) copy-start(bf16[256,128]{1,0:T(8,128)(2,1)} %k_ref.3) | copy-start | bytes 196612
  71.2 5.5 %collective-permute-start.4 = (bf16[256,128]{1,0:T(8,128)(2,1)S(1)}, bf16[256,128]{1,0:T(8,128)(2,1)S(1)}, u32[]{:S(2)}, u32[]{:S(2)}) collective-permute-start(bf16[256,128]{1,0:T(8,128)(2,1)S(1)} %get-tuple-element.75), channel_id=1, source_target_pairs={{0,16},{8,24},{16,0},{24,8},{32,48},{40,56},{48,32},{56,40},{64,80... | collective-permute-start | bytes 196616 | tf_op jit(solution)/shard_map/ppermute | solution.py:349
  76.7 9.4 %copy-start = (bf16[256,1024]{1,0:T(8,128)(2,1)S(1)}, bf16[256,1024]{1,0:T(8,128)(2,1)}, u32[]{:S(2)}) copy-start(bf16[256,1024]{1,0:T(8,128)(2,1)} %k_ref.2) | copy-start | bytes 1572868
  76.7 9.4 %copy-start.1 = (bf16[256,1024]{1,0:T(8,128)(2,1)S(1)}, bf16[256,1024]{1,0:T(8,128)(2,1)}, u32[]{:S(2)}) copy-start(bf16[256,1024]{1,0:T(8,128)(2,1)} %v_ref.2) | copy-start | bytes 1572868
  76.8 11.1 %collective-permute-start.5 = (bf16[512,128]{1,0:T(8,128)(2,1)S(1)}, bf16[512,128]{1,0:T(8,128)(2,1)S(1)}, u32[]{:S(2)}, u32[]{:S(2)}) collective-permute-start(bf16[512,128]{1,0:T(8,128)(2,1)S(1)} %get-tuple-element.79), channel_id=1, source_target_pairs={{0,8},{8,0},{16,24},{24,16},{32,40},{40,32},{48,56},{56,48},{64,72... | collective-permute-start | bytes 393224 | tf_op jit(solution)/shard_map/ppermute | solution.py:349
  79.8 9.5 %collective-permute-start.20 = (bf16[512,128]{1,0:T(8,128)(2,1)S(1)}, bf16[512,128]{1,0:T(8,128)(2,1)S(1)}, u32[]{:S(2)}, u32[]{:S(2)}) collective-permute-start(bf16[512,128]{1,0:T(8,128)(2,1)S(1)} %collective-permute-done.19.refs_1_), channel_id=1, source_target_pairs={{8,0},{16,8},{24,16},{32,24},{40,32},{48,40},{56,48},{64,56},{72,6... | collective-permute-start | bytes 393224 | tf_op jit(solution)/shard_map/ppermute | solution.py:349
  84.5 4.8 %collective-permute-start.13 = (bf16[512,128]{1,0:T(8,128)(2,1)S(1)}, bf16[512,128]{1,0:T(8,128)(2,1)S(1)}, u32[]{:S(2)}, u32[]{:S(2)}) collective-permute-start(bf16[512,128]{1,0:T(8,128)(2,1)S(1)} %collective-permute-done.12.refs_0_), channel_id=1, source_target_pairs={{56,64},{64,72},{72,80},{80,88},{88,96},{96,104},{104,112},{112,12... | collective-permute-start | bytes 393224 | tf_op jit(solution)/shard_map/ppermute | solution.py:349
  86.1 0.7 copy-start.6
